TPU v7x, 32 devices: a whole 2x2x4 slice. The times are simulated.
32 devices in a mesh: wide: 8 (over y, x, core), narrow: 4 (over z).
Axes of the slice: x: 2, y: 2, z: 4, core: 2. Of those that a mesh axis runs over, the one named last changes fastest.
Arguments:
- layer_input: bfloat16 [4, 2048, 2048], P(None, 'wide'), may hold values from -6 to 6
- grad_out: bfloat16 [4, 2048, 2048], P(None, 'wide'), may hold values from -6 to 6
- lengths: int32 [4, 8], replicated, may hold values from 1 to 1024, 2048 in all within a row
- w_query: bfloat16 [2048, 2048], P('wide', 'narrow'), may hold values from -0.125 to 0.125
- w_key: bfloat16 [2048, 1024], P('wide', 'narrow'), may hold values from -0.125 to 0.125
- w_value: bfloat16 [2048, 1024], P('wide', 'narrow'), may hold values from -0.125 to 0.125
- w_out: bfloat16 [2048, 2048], P('narrow', 'wide'), may hold values from -0.75 to 0.75
- w_gate: bfloat16 [2048, 6144], P('wide', 'narrow'), may hold values from -0.125 to 0.125
- w_up: bfloat16 [2048, 6144], P('wide', 'narrow'), may hold values from -0.125 to 0.125
- w_down: bfloat16 [6144, 2048], P('narrow', 'wide'), may hold values from -0.078125 to 0.078125
- gain_attn: float32 [2048], replicated, may hold values from 0.25 to 1.75
- gain_ffn: float32 [2048], replicated, may hold values from 0.25 to 1.75
- gain_query: float32 [128], replicated, may hold values from 0.25 to 1.75
- gain_key: float32 [128], replicated, may hold values from 0.25 to 1.75
Outputs:
- output: bfloat16 [4, 2048, 2048], P(None, 'wide')
- grad_input: float32 [4, 2048, 2048], P(None, 'wide')
- grad_wquery: float32 [2048, 2048], P('wide', 'narrow')
- grad_wkey: float32 [2048, 1024], P('wide', 'narrow')
- grad_wvalue: float32 [2048, 1024], P('wide', 'narrow')
- grad_wout: float32 [2048, 2048], P('narrow', 'wide')
- grad_wgate: float32 [2048, 6144], P('wide', 'narrow')
- grad_wup: float32 [2048, 6144], P('wide', 'narrow')
- grad_wdown: float32 [6144, 2048], P('narrow', 'wide')
- grad_gattn: float32 [2048], replicated
- grad_gffn: float32 [2048], replicated
- grad_gquery: float32 [128], replicated
- grad_gkey: float32 [128], replicated
Inputs may be any that keep to these rules, and one draw needn't show every extreme that they name: `lengths`: each row cuts the 2048 tokens of its micro-batch into 8 consecutive pieces in order; pieces 0 to 6 are documents and the last piece is padding. A row's pieces sum to 2048, and its largest piece is exactly 1024.
All inputs are finite; a program needn't handle non-finite values.
Results may differ from a plain program's by a relative error of at most 0.022.
Values may be sent and summed in bfloat16 or wider, within the bound.
A program may use at most 256 MiB of HBM per device.

v0:
```python
import math

import jax
import jax.numpy as jnp
from jax import lax
from jax.sharding import PartitionSpec as P

HD = 128
NDOC = 8


EPSILON = 1e-06
THETA = 1000000.0


def rms_norm(values, gain):
    return values * lax.rsqrt(jnp.mean(values * values, axis=-1, keepdims=True) + EPSILON) * gain


def unit_rows(values):
    return values * lax.rsqrt(jnp.mean(values * values, axis=-1, keepdims=True) + EPSILON)


def rotate(values, cosine, sine):
    midway = values.shape[-1] // 2
    turned = jnp.concatenate([-values[..., midway:], values[..., :midway]], axis=-1)
    return values * cosine + turned * sine


def layout(lengths_row, total):
    finish = jnp.cumsum(lengths_row)
    starts = finish - lengths_row
    places = jnp.arange(total, dtype=jnp.int32)
    segment = jnp.sum((places[:, None] >= finish[None, :]).astype(jnp.int32), axis=1)
    member = segment[:, None] == jnp.arange(finish.shape[0], dtype=jnp.int32)[None, :]
    opening = jnp.sum(jnp.where(member, starts[None, :], 0), axis=1)
    return (segment, places - opening)


def angles(place):
    frequency = jnp.exp(-math.log(THETA) * jnp.arange(0, HD, 2).astype(jnp.float32) / HD)
    turning = place.astype(jnp.float32)[:, None] * frequency[None, :]
    turning = jnp.concatenate([turning, turning], axis=-1)
    return (jnp.cos(turning), jnp.sin(turning))


def allowed(query_seg, query_idx, key_seg, key_idx):
    same_doc = query_seg[:, None] == key_seg[None, :]
    causal = key_idx[None, :] <= query_idx[:, None]
    usable = (key_seg[None, :] != NDOC - 1) | (key_idx[None, :] == query_idx[:, None])
    return same_doc & causal & usable


def attention_scores(query_low, key_all, mask_local, factor):
    scores = (
        jnp.einsum("tgrd,kgd->grtk", query_low, key_all, preferred_element_type=jnp.float32)
        * factor
    )
    return jnp.where(mask_local[None, None], scores, -1e30)


def one_batch(row_input, grad_row, lengths_row, gathered, gains):
    w_query, w_key, w_value, w_out, w_gate, w_up, w_down = gathered
    gain_attn, gain_ffn, gain_query, gain_key = gains
    tok_rows = row_input.shape[0]
    total = tok_rows * lax.axis_size("wide")
    groups = w_key.shape[1] // HD
    repeat = w_query.shape[1] // w_key.shape[1]
    factor = 1.0 / math.sqrt(HD)
    first_row = lax.axis_index("wide") * tok_rows
    segment, place = layout(lengths_row, total)
    positions = jnp.arange(total, dtype=jnp.int32)
    query_seg = lax.dynamic_slice_in_dim(segment, first_row, tok_rows)
    query_idx = lax.dynamic_slice_in_dim(positions, first_row, tok_rows)
    mask_local = allowed(query_seg, query_idx, segment, positions)
    cosine, sine = angles(lax.dynamic_slice_in_dim(place, first_row, tok_rows))

    def head_norm(rows, gain):
        return rotate(rms_norm(rows, gain), cosine[:, None, :], sine[:, None, :])

    input_float = row_input.astype(jnp.float32)
    grad_float = grad_row.astype(jnp.float32)
    normed_one, pull_one = jax.vjp(lambda rows: rms_norm(rows, gain_attn), input_float)
    hidden_one = normed_one.astype(jnp.bfloat16)
    query_raw = jnp.dot(hidden_one, w_query, preferred_element_type=jnp.float32).reshape(
        tok_rows, groups * repeat, HD
    )
    key_raw = jnp.dot(hidden_one, w_key, preferred_element_type=jnp.float32).reshape(
        tok_rows, groups, HD
    )
    value_low = jnp.dot(hidden_one, w_value, preferred_element_type=jnp.float32).astype(
        jnp.bfloat16
    )
    query_turned, pull_query = jax.vjp(head_norm, query_raw, gain_query)
    key_turned, pull_key = jax.vjp(head_norm, key_raw, gain_key)
    query_low = query_turned.astype(jnp.bfloat16).reshape(tok_rows, groups, repeat, HD)
    key_low = key_turned.astype(jnp.bfloat16).reshape(tok_rows, groups * HD)
    key_all, value_all = (
        lax.all_gather(key_low, "wide", axis=0, tiled=True),
        lax.all_gather(value_low, "wide", axis=0, tiled=True),
    )
    key_all = key_all.reshape(total, groups, HD)
    value_all = value_all.reshape(total, groups, HD)
    scores = attention_scores(query_low, key_all, mask_local, factor)
    highest = jnp.max(scores, axis=-1, keepdims=True)
    exponent = jnp.exp(scores - highest)
    denominator = jnp.sum(exponent, axis=-1, keepdims=True)
    log_total = highest + jnp.log(denominator)
    probs_low = (exponent / denominator).astype(jnp.bfloat16)
    mixed = jnp.einsum("grtk,kgd->tgrd", probs_low, value_all, preferred_element_type=jnp.float32)
    mixed_low = mixed.reshape(tok_rows, groups * repeat * HD).astype(jnp.bfloat16)
    attn_part = jnp.dot(mixed_low, w_out, preferred_element_type=jnp.float32)
    middle = input_float + lax.psum(attn_part.astype(jnp.bfloat16), "narrow").astype(jnp.float32)
    normed_two, pull_two = jax.vjp(lambda rows: rms_norm(rows, gain_ffn), middle)
    hidden_two = normed_two.astype(jnp.bfloat16)
    unit_two = unit_rows(middle)
    gate = jnp.dot(hidden_two, w_gate, preferred_element_type=jnp.float32)
    up_proj = jnp.dot(hidden_two, w_up, preferred_element_type=jnp.float32)
    active, pull_active = jax.vjp(
        lambda gate_in, up_in: jax.nn.silu(gate_in) * up_in, gate, up_proj
    )
    active_low = active.astype(jnp.bfloat16)
    ffn_part = jnp.dot(active_low, w_down, preferred_element_type=jnp.float32)
    output_low = (
        middle + lax.psum(ffn_part.astype(jnp.bfloat16), "narrow").astype(jnp.float32)
    ).astype(jnp.bfloat16)
    grad_wdown = jnp.einsum("tf,td->fd", active_low, grad_row, preferred_element_type=jnp.float32)
    grad_active = jnp.einsum("td,fd->tf", grad_row, w_down, preferred_element_type=jnp.float32)
    grad_gate, grad_upper = pull_active(grad_active)
    gate_back = grad_gate.astype(jnp.bfloat16)
    upper_back = grad_upper.astype(jnp.bfloat16)
    grad_wgate = jnp.einsum("td,tf->df", hidden_two, gate_back, preferred_element_type=jnp.float32)
    grad_wup = jnp.einsum("td,tf->df", hidden_two, upper_back, preferred_element_type=jnp.float32)
    partial_two = jnp.einsum(
        "tf,df->td", gate_back, w_gate, preferred_element_type=jnp.float32
    ) + jnp.einsum("tf,df->td", upper_back, w_up, preferred_element_type=jnp.float32)
    gain_two = jnp.sum(partial_two * unit_two, axis=0)
    grad_middle = (
        grad_float
        + pull_two(lax.psum(partial_two.astype(jnp.bfloat16), "narrow").astype(jnp.float32))[0]
    )
    middle_low = grad_middle.astype(jnp.bfloat16)
    grad_wout = jnp.einsum("th,td->hd", mixed_low, middle_low, preferred_element_type=jnp.float32)
    grad_mixed = jnp.einsum("td,hd->th", middle_low, w_out, preferred_element_type=jnp.float32)
    grad_mixed = grad_mixed.astype(jnp.bfloat16).reshape(tok_rows, groups, repeat, HD)
    scores = attention_scores(query_low, key_all, mask_local, factor)
    probs = jnp.exp(scores - log_total)
    grad_probs = jnp.einsum(
        "tgrd,kgd->grtk", grad_mixed, value_all, preferred_element_type=jnp.float32
    )
    weighted = jnp.sum(probs * grad_probs, axis=-1, keepdims=True)
    grad_scores = (probs * (grad_probs - weighted)).astype(jnp.bfloat16)
    grad_turned = (
        jnp.einsum("grtk,kgd->tgrd", grad_scores, key_all, preferred_element_type=jnp.float32)
        * factor
    )
    grad_keyall = (
        jnp.einsum("grtk,tgrd->kgd", grad_scores, query_low, preferred_element_type=jnp.float32)
        * factor
    )
    grad_valueall = jnp.einsum(
        "grtk,tgrd->kgd", probs.astype(jnp.bfloat16), grad_mixed, preferred_element_type=jnp.float32
    )
    grad_keys, grad_values = (
        lax.psum_scatter(
            grad_keyall.reshape(total, groups * HD).astype(jnp.bfloat16),
            "wide",
            scatter_dimension=0,
            tiled=True,
        ).astype(jnp.float32),
        lax.psum_scatter(
            grad_valueall.reshape(total, groups * HD).astype(jnp.bfloat16),
            "wide",
            scatter_dimension=0,
            tiled=True,
        ).astype(jnp.float32),
    )
    grad_qraw, gain_q = pull_query(grad_turned.reshape(tok_rows, groups * repeat, HD))
    grad_kraw, gain_k = pull_key(grad_keys.reshape(tok_rows, groups, HD))
    query_back = grad_qraw.reshape(tok_rows, groups * repeat * HD).astype(jnp.bfloat16)
    key_back = grad_kraw.reshape(tok_rows, groups * HD).astype(jnp.bfloat16)
    value_back = grad_values.astype(jnp.bfloat16)
    grad_wquery = jnp.einsum(
        "td,th->dh", hidden_one, query_back, preferred_element_type=jnp.float32
    )
    grad_wkey = jnp.einsum("td,th->dh", hidden_one, key_back, preferred_element_type=jnp.float32)
    grad_wvalue = jnp.einsum(
        "td,th->dh", hidden_one, value_back, preferred_element_type=jnp.float32
    )
    partial_one = (
        jnp.einsum("th,dh->td", query_back, w_query, preferred_element_type=jnp.float32)
        + jnp.einsum("th,dh->td", key_back, w_key, preferred_element_type=jnp.float32)
        + jnp.einsum("th,dh->td", value_back, w_value, preferred_element_type=jnp.float32)
    )
    gain_one = jnp.sum(partial_one * unit_rows(input_float), axis=0)
    grad_input = (
        grad_middle
        + pull_one(lax.psum(partial_one.astype(jnp.bfloat16), "narrow").astype(jnp.float32))[0]
    )
    weight_grads = (
        grad_wquery,
        grad_wkey,
        grad_wvalue,
        grad_wout,
        grad_wgate,
        grad_wup,
        grad_wdown,
    )
    return (output_low, grad_input, weight_grads, (gain_one, gain_two, gain_q, gain_k))


def local(
    layer_input,
    grad_out,
    lengths,
    w_query,
    w_key,
    w_value,
    w_out,
    w_gate,
    w_up,
    w_down,
    gain_attn,
    gain_ffn,
    gain_query,
    gain_key,
):
    width = lax.axis_size("wide")
    shards = (w_query, w_key, w_value, w_out, w_gate, w_up, w_down)
    along_rows = (True, True, True, False, True, True, False)
    gains = (gain_attn, gain_ffn, gain_query, gain_key)
    totals = tuple(
        (
            jnp.zeros(
                (
                    (piece.shape[0] * width, piece.shape[1])
                    if rows_first
                    else (piece.shape[0], piece.shape[1] * width)
                ),
                jnp.float32,
            )
            for piece, rows_first in zip(shards, along_rows)
        )
    )
    gain_terms = tuple((jnp.zeros(gain.shape, jnp.float32) for gain in gains))
    outputs = []
    grad_inputs = []
    for micro in range(layer_input.shape[0]):
        gathered = (
            lax.all_gather(w_query, "wide", axis=0, tiled=True),
            lax.all_gather(w_key, "wide", axis=0, tiled=True),
            lax.all_gather(w_value, "wide", axis=0, tiled=True),
            lax.all_gather(w_out, "wide", axis=1, tiled=True),
            lax.all_gather(w_gate, "wide", axis=0, tiled=True),
            lax.all_gather(w_up, "wide", axis=0, tiled=True),
            lax.all_gather(w_down, "wide", axis=1, tiled=True),
        )
        output, grad_input, weight_grads, gain_grads = one_batch(
            layer_input[micro], grad_out[micro], lengths[micro], gathered, gains
        )
        outputs.append(output)
        grad_inputs.append(grad_input)
        gain_terms = tuple((running + fresh for running, fresh in zip(gain_terms, gain_grads)))
        totals = tuple((running + fresh for running, fresh in zip(totals, weight_grads)))
    results = (
        lax.psum_scatter(
            totals[0].astype(jnp.bfloat16), "wide", scatter_dimension=0, tiled=True
        ).astype(jnp.float32),
        lax.psum_scatter(
            totals[1].astype(jnp.bfloat16), "wide", scatter_dimension=0, tiled=True
        ).astype(jnp.float32),
        lax.psum_scatter(
            totals[2].astype(jnp.bfloat16), "wide", scatter_dimension=0, tiled=True
        ).astype(jnp.float32),
        lax.psum_scatter(
            totals[3].astype(jnp.bfloat16), "wide", scatter_dimension=1, tiled=True
        ).astype(jnp.float32),
        lax.psum_scatter(
            totals[4].astype(jnp.bfloat16), "wide", scatter_dimension=0, tiled=True
        ).astype(jnp.float32),
        lax.psum_scatter(
            totals[5].astype(jnp.bfloat16), "wide", scatter_dimension=0, tiled=True
        ).astype(jnp.float32),
        lax.psum_scatter(
            totals[6].astype(jnp.bfloat16), "wide", scatter_dimension=1, tiled=True
        ).astype(jnp.float32),
    )
    gain_total = lax.psum(gain_terms, ("wide", "narrow"))
    return (
        jnp.stack(outputs),
        jnp.stack(grad_inputs),
        results[0],
        results[1],
        results[2],
        results[3],
        results[4],
        results[5],
        results[6],
        gain_total[0],
        gain_total[1],
        gain_total[2],
        gain_total[3],
    )


def solution(mesh):
    in_specs = (
        P(None, "wide", None),
        P(None, "wide", None),
        P(),
        P("wide", "narrow"),
        P("wide", "narrow"),
        P("wide", "narrow"),
        P("narrow", "wide"),
        P("wide", "narrow"),
        P("wide", "narrow"),
        P("narrow", "wide"),
        P(),
        P(),
        P(),
        P(),
    )
    out_specs = (
        P(None, "wide", None),
        P(None, "wide", None),
        P("wide", "narrow"),
        P("wide", "narrow"),
        P("wide", "narrow"),
        P("narrow", "wide"),
        P("wide", "narrow"),
        P("wide", "narrow"),
        P("narrow", "wide"),
        P(),
        P(),
        P(),
        P(),
    )
    return jax.shard_map(local, mesh=mesh, in_specs=in_specs, out_specs=out_specs, check_vma=False)
```

profile of v0, /device:TPU:0, one launch (start us, length us, event | category | flops | bytes accessed | tf_op | source)
XLA Modules:
  0.0 1970.9 jit_solution(11782084816646856816)
XLA Ops:
  14.2 22.0 %all-gather.16.cloned.1.call-done = bf16[2048,256]{1,0:T(8,128)(2,1)} async-done(((bf16[256,256]{1,0:T(8,128)(2,1)}), bf16[2048,256]{1,0:T(8,128)(2,1)}) %all-gather.16.cloned.1.call-update) | async-done | bytes 1048592 | tf_op jit(solution)/shard_map/all_gather | solution.py:252
  39.7 21.9 %all-gather.20.cloned.1.call-done = bf16[2048,256]{1,0:T(8,128)(2,1)} async-done(((bf16[256,256]{1,0:T(8,128)(2,1)}), bf16[2048,256]{1,0:T(8,128)(2,1)}) %all-gather.20.cloned.1.call-update) | async-done | bytes 1048592 | tf_op jit(solution)/shard_map/all_gather | solution.py:251
  72.3 19.1 all-gather.24.cloned.1.call-done
  95.3 21.9 %all-gather.38.cloned.1.call-done = bf16[2048,256]{1,0:T(8,128)(2,1)} async-done(((bf16[256,256]{1,0:T(8,128)(2,1)}), bf16[2048,256]{1,0:T(8,128)(2,1)}) %all-gather.38.cloned.1.call-update) | async-done | bytes 1048592 | tf_op jit(solution)/shard_map/all_gather | solution.py:100
  122.7 20.4 %all-gather.40.cloned.1.call-done = bf16[2048,256]{0,1:T(8,128)(2,1)} async-done(((bf16[256,256]{0,1:T(8,128)(2,1)}), bf16[2048,256]{0,1:T(8,128)(2,1)}) %all-gather.40.cloned.1.call-update) | async-done | bytes 1048592 | tf_op jit(solution)/shard_map/all_gather | solution.py:99
  150.9 22.1 %all-gather.26.cloned.1.call-done = bf16[512,2048]{1,0:T(8,128)(2,1)} async-done(((bf16[512,256]{1,0:T(8,128)(2,1)}), bf16[512,2048]{1,0:T(8,128)(2,1)}) %all-gather.26.cloned.1.call-update) | async-done | bytes 2097168 | tf_op jit(solution)/shard_map/all_gather | solution.py:253
  176.4 51.9 %all-reduce.25.cloned.1.call-done = bf16[256,2048]{1,0:T(8,128)(2,1)} async-done(((bf16[256,2048]{1,0:T(8,128)(2,1)}), bf16[256,2048]{1,0:T(8,128)(2,1)}) %all-reduce.25.cloned.1.call-update) | async-done | bytes 1048592 | tf_op jit(solution)/shard_map/psum | solution.py:113
  262.7 20.8 %all-gather.18.cloned.1.call-done = bf16[2048,256]{1,0:T(8,128)(2,1)} async-done(((bf16[256,256]{1,0:T(8,128)(2,1)}), bf16[2048,256]{1,0:T(8,128)(2,1)}) %all-gather.18.cloned.1.call-update) | async-done | bytes 1048592 | tf_op jit(solution)/shard_map/all_gather | solution.py:100
  285.7 23.8 %all-gather.34.cloned.1.call-done = bf16[2048,256]{1,0:T(8,128)(2,1)} async-done(((bf16[256,256]{1,0:T(8,128)(2,1)}), bf16[2048,256]{1,0:T(8,128)(2,1)}) %all-gather.34.cloned.1.call-update) | async-done | bytes 1048592 | tf_op jit(solution)/shard_map/all_gather | solution.py:100
  312.0 23.7 %all-gather.44.cloned.1.call-done = bf16[2048,256]{0,1:T(8,128)(2,1)} async-done(((bf16[256,256]{0,1:T(8,128)(2,1)}), bf16[2048,256]{0,1:T(8,128)(2,1)}) %all-gather.44.cloned.1.call-update) | async-done | bytes 1048592 | tf_op jit(solution)/shard_map/all_gather | solution.py:99
  345.9 15.3 all-gather.22.cloned.1.call-done
  371.6 15.2 all-gather.36.cloned.1.call-done
  397.1 37.2 %all-gather.28.cloned.1.call-done = bf16[2048,1536]{1,0:T(8,128)(2,1)} async-done(((bf16[256,1536]{1,0:T(8,128)(2,1)}), bf16[2048,1536]{1,0:T(8,128)(2,1)}) %all-gather.28.cloned.1.call-update) | async-done | bytes 6291472 | tf_op jit(solution)/shard_map/all_gather | solution.py:254
  440.0 42.9 %all-gather.32.cloned.1.call-done = bf16[1536,2048]{1,0:T(8,128)(2,1)} async-done(((bf16[1536,256]{1,0:T(8,128)(2,1)}), bf16[1536,2048]{1,0:T(8,128)(2,1)}) %all-gather.32.cloned.1.call-update) | async-done | bytes 6291472 | tf_op jit(solution)/shard_map/all_gather | solution.py:256
  489.0 41.4 %all-gather.30.cloned.1.call-done = bf16[2048,1536]{1,0:T(8,128)(2,1)} async-done(((bf16[256,1536]{1,0:T(8,128)(2,1)}), bf16[2048,1536]{1,0:T(8,128)(2,1)}) %all-gather.30.cloned.1.call-update) | async-done | bytes 6291472 | tf_op jit(solution)/shard_map/all_gather | solution.py:255
  546.0 156.1 %all-reduce.31.cloned.1.call-done = (bf16[256,2048]{1,0:T(8,128)(2,1)}, bf16[256,2048]{1,0:T(8,128)(2,1)}, bf16[256,2048]{1,0:T(8,128)(2,1)}, bf16[256,2048]{1,0:T(8,128)(2,1)}) async-done(((bf16[256,2048]{1,0:T(8,128)(2,1)}, bf16[256,2048]{1,0:T(8,128)(2,1)}, bf16[256,2048]{1,0:T(8,128)(2,1)}, bf16[256,2048]{1,0:T(8,128)(2,1)}), (bf16[256,2048]{1,0:T(8,128)(2,1)}, bf16[256,2048]{1,0:T(8,128)(2,1)}, ...) | async-done | bytes 4194320 | tf_op jit(solution)/shard_map/psum | solution.py:113
  775.0 120.1 %all-reduce.29.cloned.1.call-done = (bf16[256,2048]{1,0:T(8,128)(2,1)}, bf16[256,2048]{1,0:T(8,128)(2,1)}, bf16[256,2048]{1,0:T(8,128)(2,1)}) async-done(((bf16[256,2048]{1,0:T(8,128)(2,1)}, bf16[256,2048]{1,0:T(8,128)(2,1)}, bf16[256,2048]{1,0:T(8,128)(2,1)}), (bf16[256,2048]{1,0:T(8,128)(2,1)}, bf16[256,2048]{1,0:T(8,128)(2,1)}, bf16[256,2048]{1,0:T(8,128)(2,1)})) %all-reduce.29.cloned.1.call-update) | async-done | bytes 3145744 | tf_op jit(solution)/shard_map/psum | solution.py:140
  1063.5 15.3 reduce-scatter.20.cloned.1.call-done
  1096.3 22.3 %reduce-scatter.18.cloned.1.call-done = bf16[256,256]{0,1:T(8,128)(2,1)} async-done(((bf16[2048,256]{0,1:T(8,128)(2,1)}), bf16[256,256]{0,1:T(8,128)(2,1)}) %reduce-scatter.18.cloned.1.call-update) | async-done | bytes 131088 | tf_op jit(solution)/shard_map/reduce_scatter | solution.py:171
  1121.7 35.9 %reduce-scatter.22.cloned.1.call-done = bf16[256,256]{0,1:T(8,128)(2,1)} async-done(((bf16[2048,256]{0,1:T(8,128)(2,1)}), bf16[256,256]{0,1:T(8,128)(2,1)}) %reduce-scatter.22.cloned.1.call-update) | async-done | bytes 131088 | tf_op jit(solution)/shard_map/reduce_scatter | solution.py:171
  1161.6 35.3 %reduce-scatter.26.cloned.1.call-done = bf16[256,256]{0,1:T(8,128)(2,1)} async-done(((bf16[2048,256]{0,1:T(8,128)(2,1)}), bf16[256,256]{0,1:T(8,128)(2,1)}) %reduce-scatter.26.cloned.1.call-update) | async-done | bytes 131088 | tf_op jit(solution)/shard_map/reduce_scatter | solution.py:171
  1200.8 35.8 %reduce-scatter.30.cloned.1.call-done = bf16[256,256]{0,1:T(8,128)(2,1)} async-done(((bf16[2048,256]{0,1:T(8,128)(2,1)}), bf16[256,256]{0,1:T(8,128)(2,1)}) %reduce-scatter.30.cloned.1.call-update) | async-done | bytes 131088 | tf_op jit(solution)/shard_map/reduce_scatter | solution.py:171
  1240.2 18.2 add_convert_fusion.2
  1258.8 8.0 fusion.401
  1279.6 17.3 add_convert_fusion.1
  1318.6 17.4 add_convert_fusion
  1377.5 27.8 %reduce-scatter.36.cloned.1.call-done = bf16[256,256]{1,0:T(8,128)(2,1)} async-done(((bf16[2048,256]{1,0:T(8,128)(2,1)}), bf16[256,256]{1,0:T(8,128)(2,1)}) %reduce-scatter.36.cloned.1.call-update) | async-done | bytes 131088 | tf_op jit(solution)/shard_map/reduce_scatter | solution.py:272
  1406.9 64.1 %reduce-scatter.40.cloned.1.call-done = bf16[256,1536]{1,0:T(8,128)(2,1)} async-done(((bf16[2048,1536]{1,0:T(8,128)(2,1)}), bf16[256,1536]{1,0:T(8,128)(2,1)}) %reduce-scatter.40.cloned.1.call-update) | async-done | bytes 786448 | tf_op jit(solution)/shard_map/reduce_scatter | solution.py:278
  1473.5 63.1 %reduce-scatter.42.cloned.1.call-done = bf16[256,1536]{1,0:T(8,128)(2,1)} async-done(((bf16[2048,1536]{1,0:T(8,128)(2,1)}), bf16[256,1536]{1,0:T(8,128)(2,1)}) %reduce-scatter.42.cloned.1.call-update) | async-done | bytes 786448 | tf_op jit(solution)/shard_map/reduce_scatter | solution.py:281
  1539.0 62.5 %reduce-scatter.44.cloned.1.call-done = bf16[1536,256]{1,0:T(8,128)(2,1)} async-done(((bf16[1536,2048]{1,0:T(8,128)(2,1)}), bf16[1536,256]{1,0:T(8,128)(2,1)}) %reduce-scatter.44.cloned.1.call-update) | async-done | bytes 786448 | tf_op jit(solution)/shard_map/reduce_scatter | solution.py:284
  1603.9 297.2 %all-reduce.27.cloned.1.call-done = (bf16[256,2048]{1,0:T(8,128)(2,1)}, bf16[256,2048]{1,0:T(8,128)(2,1)}, bf16[256,2048]{1,0:T(8,128)(2,1)}, bf16[256,2048]{1,0...) async-done(((bf16[256,2048]{1,0:T(8,128)(2,1)}, bf16[256,2048]{1,0:T(8,128)(2,1)}, ...) | async-done | bytes 8388624 | tf_op jit(solution)/shard_map/psum | solution.py:125
  1924.5 39.3 %all-reduce.16 = (f32[2048]{0:T(1024)}, f32[2048]{0:T(1024)}, f32[128]{0:T(128)}, f32[128]{0:T(128)}) all-reduce(f32[2048]{0:T(1024)S(1)} %add_add_fusion.17, f32[2048]{0:T(1024)S(1)} %add_add_fusion.16, f32[128]{0:T(128)S(1)} %add_add_fusion.19, f32[128]{0:T(128)S(1)} %add_add_fusion.18), channel_id=1, replica_groups=mesh['wide'=8,'narrow'=4] {'wide','narrow'}, use_global_device_ids=true, to_apply=%region_91.92 | all-reduce | flops 4352 | bytes 34816 | tf_op jit(solution)/shard_map/psum | solution.py:288
  (866 shorter events, 517.6 us)
Async XLA Ops:
  7.9 53.6 %all-gather.20.cloned.1.call-start = ((), (), s32[]{:S(2)}) async-start(), calls=%async_computation.17 | async-start | bytes 1179648 | tf_op jit(solution)/shard_map/all_gather | solution.py:251
  8.7 82.7 %all-gather.24.cloned.1.call-start = ((), (), s32[]{:S(2)}) async-start(), calls=%async_computation.19 | async-start | bytes 2359296 | tf_op jit(solution)/shard_map/all_gather | solution.py:250
  9.4 107.8 %all-gather.38.cloned.1.call-start = ((), (), s32[]{:S(2)}) async-start(), calls=%async_computation.26 | async-start | bytes 1179648 | tf_op jit(solution)/shard_map/all_gather | solution.py:100
  38.9 104.2 %all-gather.40.cloned.1.call-start = ((), (), s32[]{:S(2)}) async-start(), calls=%async_computation.27 | async-start | bytes 1179648 | tf_op jit(solution)/shard_map/all_gather | solution.py:99
  66.7 106.3 %all-gather.26.cloned.1.call-start = ((), (), s32[]{:S(2)}) async-start(), calls=%async_computation.20 | async-start | bytes 2359296 | tf_op jit(solution)/shard_map/all_gather | solution.py:253
  67.3 161.1 %all-reduce.25.cloned.1.call-start = ((), (), s32[]{:S(2)}) async-start(), calls=%async_computation.28 | async-start | bytes 2097152 | tf_op jit(solution)/shard_map/psum | solution.py:113
  176.4 83.8 %all-gather.42.cloned.1.call-start = ((), (), s32[]{:S(2)}) async-start(), calls=%async_computation.29 | async-start | bytes 1179648 | tf_op jit(solution)/shard_map/all_gather | solution.py:100
  237.0 72.5 %all-gather.34.cloned.1.call-start = ((), (), s32[]{:S(2)}) async-start(), calls=%async_computation.24 | async-start | bytes 1179648 | tf_op jit(solution)/shard_map/all_gather | solution.py:100
  242.3 93.4 %all-gather.44.cloned.1.call-start = ((), (), s32[]{:S(2)}) async-start(), calls=%async_computation.30 | async-start | bytes 1179648 | tf_op jit(solution)/shard_map/all_gather | solution.py:99
  247.2 114.0 %all-gather.22.cloned.1.call-start = ((), (), s32[]{:S(2)}) async-start(), calls=%async_computation.18 | async-start | bytes 1179648 | tf_op jit(solution)/shard_map/all_gather | solution.py:99
  248.5 138.4 %all-gather.36.cloned.1.call-start = ((), (), s32[]{:S(2)}) async-start(), calls=%async_computation.25 | async-start | bytes 1179648 | tf_op jit(solution)/shard_map/all_gather | solution.py:99
  249.8 184.5 %all-gather.28.cloned.1.call-start = ((), (), s32[]{:S(2)}) async-start(), calls=%async_computation.21 | async-start | bytes 7077888 | tf_op jit(solution)/shard_map/all_gather | solution.py:254
  250.4 232.5 %all-gather.32.cloned.1.call-start = ((), (), s32[]{:S(2)}) async-start(), calls=%async_computation.23 | async-start | bytes 7077888 | tf_op jit(solution)/shard_map/all_gather | solution.py:256
  251.0 279.4 %all-gather.30.cloned.1.call-start = ((), (), s32[]{:S(2)}) async-start(), calls=%async_computation.22 | async-start | bytes 7077888 | tf_op jit(solution)/shard_map/all_gather | solution.py:255
  251.5 450.6 %all-reduce.31.cloned.1.call-start = ((), (), s32[]{:S(2)}) async-start(), calls=%async_computation.48 | async-start | bytes 8388608 | tf_op jit(solution)/shard_map/psum | solution.py:113
  545.9 349.2 %all-reduce.29.cloned.1.call-start = ((), (), s32[]{:S(2)}) async-start(), calls=%async_computation.47 | async-start | bytes 6291456 | tf_op jit(solution)/shard_map/psum | solution.py:140
  774.3 278.8 %reduce-scatter.24.cloned.1.call-start = ((), (), s32[]{:S(2)}) async-start(), calls=%async_computation.35 | async-start | bytes 1179648 | tf_op jit(solution)/shard_map/reduce_scatter | solution.py:165
  925.5 129.3 %reduce-scatter.16.cloned.1.call-start = ((), (), s32[]{:S(2)}) async-start(), calls=%async_computation.31 | async-start | bytes 1179648 | tf_op jit(solution)/shard_map/reduce_scatter | solution.py:165
  946.6 109.9 %reduce-scatter.28.cloned.1.call-start = ((), (), s32[]{:S(2)}) async-start(), calls=%async_computation.37 | async-start | bytes 1179648 | tf_op jit(solution)/shard_map/reduce_scatter | solution.py:165
  963.7 115.1 %reduce-scatter.20.cloned.1.call-start = ((), (), s32[]{:S(2)}) async-start(), calls=%async_computation.33 | async-start | bytes 1179648 | tf_op jit(solution)/shard_map/reduce_scatter | solution.py:165
  973.9 144.7 %reduce-scatter.18.cloned.1.call-start = ((), (), s32[]{:S(2)}) async-start(), calls=%async_computation.32 | async-start | bytes 1179648 | tf_op jit(solution)/shard_map/reduce_scatter | solution.py:171
  985.2 172.5 %reduce-scatter.22.cloned.1.call-start = ((), (), s32[]{:S(2)}) async-start(), calls=%async_computation.34 | async-start | bytes 1179648 | tf_op jit(solution)/shard_map/reduce_scatter | solution.py:171
  996.0 200.9 %reduce-scatter.26.cloned.1.call-start = ((), (), s32[]{:S(2)}) async-start(), calls=%async_computation.36 | async-start | bytes 1179648 | tf_op jit(solution)/shard_map/reduce_scatter | solution.py:171
  1008.1 228.5 %reduce-scatter.30.cloned.1.call-start = ((), (), s32[]{:S(2)}) async-start(), calls=%async_computation.38 | async-start | bytes 1179648 | tf_op jit(solution)/shard_map/reduce_scatter | solution.py:171
  1022.0 350.1 %reduce-scatter.32.cloned.1.call-start = ((), (), s32[]{:S(2)}) async-start(), calls=%async_computation.39 | async-start | bytes 2359296 | tf_op jit(solution)/shard_map/reduce_scatter | solution.py:266
  1030.5 343.3 %reduce-scatter.38.cloned.1.call-start = ((), (), s32[]{:S(2)}) async-start(), calls=%async_computation.42 | async-start | bytes 2359296 | tf_op jit(solution)/shard_map/reduce_scatter | solution.py:275
  1053.0 322.8 %reduce-scatter.34.cloned.1.call-start = ((), (), s32[]{:S(2)}) async-start(), calls=%async_computation.40 | async-start | bytes 1179648 | tf_op jit(solution)/shard_map/reduce_scatter | solution.py:269
  1088.5 316.8 %reduce-scatter.36.cloned.1.call-start = ((), (), s32[]{:S(2)}) async-start(), calls=%async_computation.41 | async-start | bytes 1179648 | tf_op jit(solution)/shard_map/reduce_scatter | solution.py:272
  1240.2 230.9 %reduce-scatter.40.cloned.1.call-start = ((), (), s32[]{:S(2)}) async-start(), calls=%async_computation.43 | async-start | bytes 7077888 | tf_op jit(solution)/shard_map/reduce_scatter | solution.py:278
  1258.4 278.1 %reduce-scatter.42.cloned.1.call-start = ((), (), s32[]{:S(2)}) async-start(), calls=%async_computation.44 | async-start | bytes 7077888 | tf_op jit(solution)/shard_map/reduce_scatter | solution.py:281
  1296.9 304.6 %reduce-scatter.44.cloned.1.call-start = ((), (), s32[]{:S(2)}) async-start(), calls=%async_computation.45 | async-start | bytes 7077888 | tf_op jit(solution)/shard_map/reduce_scatter | solution.py:284
  1336.0 565.1 %all-reduce.27.cloned.1.call-start = ((), (), s32[]{:S(2)}) async-start(), calls=%async_computation.46 | async-start | bytes 16777216 | tf_op jit(solution)/shard_map/psum | solution.py:125
  (267 other events, 2912.5 us)
Sparse Core Ops, SparseCore 0:
  9.9 26.1 all-gather.15
  63.4 27.8 all-gather.23
  93.7 23.4 all-gather.37
  119.5 23.5 all-gather.39
  144.8 28.1 all-gather.25
  176.5 51.8 all-reduce.24
  260.0 23.4 all-gather.17
  286.0 23.4 all-gather.33
  312.1 23.5 all-gather.43
  337.6 23.5 all-gather.21
  363.3 23.5 all-gather.35
  388.8 45.5 all-gather.27
  436.2 46.6 all-gather.31
  484.8 45.5 all-gather.29
  546.1 155.9 all-reduce.30
  774.4 120.6 all-reduce.28
  925.6 35.0 reduce-scatter.23
  964.3 36.0 reduce-scatter.15
  1003.5 35.9 reduce-scatter.27
  1042.8 35.9 reduce-scatter.19
  1082.5 35.9 reduce-scatter.17
  1121.6 36.0 reduce-scatter.21
  1160.8 35.9 reduce-scatter.25
  1200.5 36.0 reduce-scatter.29
  1239.7 41.1 reduce-scatter.31
  1284.6 41.2 reduce-scatter.37
  1329.6 36.0 reduce-scatter.33
  1369.3 35.9 reduce-scatter.35
  1409.3 61.7 reduce-scatter.39
  1474.8 61.7 reduce-scatter.41
  1539.8 61.7 reduce-scatter.43
  1605.4 295.7 all-reduce.26
  (2 shorter events, 46.3 us)
where the time goes:
time: 1980 us; the launch traced here: 1970 us
  waiting for transfers between devices  1340 us (68%)
  matrix products  388 us (20%)
  other arithmetic  127 us (6%)
  local copies, waits for them, and re-layouts  54.7 us (3%)
  blocking collectives  39.3 us (2%)
    psum x1, waiting for transfers between devices, one_batch(): lax.psum(ffn_part.astype(jnp.bfloat16), 'narrow').astype(jnp.float32)  297 us
    psum x2, waiting for transfers between devices, one_batch(): lax.psum(attn_part.astype(jnp.bfloat16), 'narrow').astype(jnp.float32)  208 us
    reduce_scatter x4, waiting for transfers between devices, one_batch(): lax.psum_scatter(grad_valueall.reshape(total, groups * HD).astype(jnp.bfl...  129 us
    psum x1, waiting for transfers between devices, one_batch(): lax.psum(partial_two.astype(jnp.bfloat16), 'narrow').astype(jnp.float32)  120 us
    all_gather x4, waiting for transfers between devices, one_batch(): lax.all_gather(key_low, 'wide', axis=0, tiled=True)  74.7 us
    all_gather x4, waiting for transfers between devices, one_batch(): lax.all_gather(value_low, 'wide', axis=0, tiled=True)  66.6 us
    reduce_scatter x1, waiting for transfers between devices, local(): lax.psum_scatter(totals[4].astype(jnp.bfloat16), 'wide', scatter_dimensio...  64.1 us
    reduce_scatter x1, waiting for transfers between devices, local(): lax.psum_scatter(totals[5].astype(jnp.bfloat16), 'wide', scatter_dimensio...  63.1 us
  transfers between devices with their start and end apart: 34, of which 28 were waited for; matrix products, arithmetic and copies ran while one was open for 20% of the time, Pallas kernels for 0%

commit v1 on v0

--- a/solution.py
+++ b/solution.py
@@ -1,8 +1,11 @@
+import functools
 import math
 
 import jax
 import jax.numpy as jnp
 from jax import lax
+from jax.experimental import pallas as pl
+from jax.experimental.pallas import tpu as pltpu
 from jax.sharding import PartitionSpec as P
 
 HD = 128
@@ -209,7 +212,7 @@
     return (output_low, grad_input, weight_grads, (gain_one, gain_two, gain_q, gain_k))
 
 
-def local(
+def local_general(
     layer_input,
     grad_out,
     lengths,
@@ -303,6 +306,767 @@
     )
 
 
+BLOCK = 256
+NT = (((1,), (1,)), ((), ()))
+TN = (((0,), (0,)), ((), ()))
+
+
+def attend_forward(first_ref, qkv_ref, start_ref, mixed_ref, kept_ref, log_ref):
+    step_q = pl.program_id(0)
+    rows = pl.ds(step_q * BLOCK, BLOCK)
+    factor = 1.0 / math.sqrt(HD)
+    query = jnp.concatenate([qkv_ref[rows, 0:HD], qkv_ref[rows, HD : 2 * HD]], axis=0)
+    start = start_ref[rows, :]
+    start = jnp.concatenate([start, start], axis=0)
+    spot = lax.broadcasted_iota(jnp.int32, (BLOCK, 1), 0) + step_q * BLOCK
+    spot = jnp.concatenate([spot, spot], axis=0)
+
+    def one(step_k, carry):
+        highest, total, mixed = carry
+        cols = pl.ds(step_k * BLOCK, BLOCK)
+        scores = lax.dot_general(
+            query, qkv_ref[cols, 2 * HD : 3 * HD], NT, preferred_element_type=jnp.float32
+        )
+        key_spot = lax.broadcasted_iota(jnp.int32, (1, BLOCK), 1) + step_k * BLOCK
+        fits = (key_spot >= start) & (key_spot <= spot)
+        scores = jnp.where(fits, scores * factor, -1e30)
+        fresh = jnp.maximum(highest, jnp.max(scores, axis=-1, keepdims=True))
+        shrink = jnp.exp(highest - fresh)
+        exponent = jnp.exp(scores - fresh)
+        total = total * shrink + jnp.sum(exponent, axis=-1, keepdims=True)
+        mixed = mixed * shrink + jnp.dot(
+            exponent.astype(jnp.bfloat16),
+            qkv_ref[cols, 3 * HD : 4 * HD],
+            preferred_element_type=jnp.float32,
+        )
+        return (fresh, total, mixed)
+
+    highest, total, mixed = lax.fori_loop(
+        first_ref[step_q],
+        step_q + 1,
+        one,
+        (
+            jnp.full((2 * BLOCK, 1), -1e30, jnp.float32),
+            jnp.zeros((2 * BLOCK, 1), jnp.float32),
+            jnp.zeros((2 * BLOCK, HD), jnp.float32),
+        ),
+    )
+    mixed = mixed / total
+    mixed = jnp.concatenate([mixed[:BLOCK], mixed[BLOCK:]], axis=1)
+    mixed_ref[...] = mixed.astype(jnp.bfloat16)
+    kept_ref[...] = mixed
+    log_total = highest + jnp.log(total)
+    log_ref[...] = jnp.concatenate([log_total[:BLOCK], log_total[BLOCK:]], axis=1)
+
+
+def attend_backward(
+    first_ref, qkv_ref, start_ref, grad_ref, kept_ref, log_ref, back_ref, key_sum, value_sum
+):
+    step_q = pl.program_id(0)
+    rows = pl.ds(step_q * BLOCK, BLOCK)
+    factor = 1.0 / math.sqrt(HD)
+
+    @pl.when(step_q == 0)
+    def _():
+        key_sum[...] = jnp.zeros_like(key_sum)
+        value_sum[...] = jnp.zeros_like(value_sum)
+
+    query = jnp.concatenate([qkv_ref[rows, 0:HD], qkv_ref[rows, HD : 2 * HD]], axis=0)
+    grad = jnp.concatenate([grad_ref[:, 0:HD], grad_ref[:, HD : 2 * HD]], axis=0)
+    kept = jnp.concatenate([kept_ref[:, 0:HD], kept_ref[:, HD : 2 * HD]], axis=0)
+    log_total = jnp.concatenate([log_ref[:, 0:1], log_ref[:, 1:2]], axis=0)
+    weighted = jnp.sum(grad.astype(jnp.float32) * kept, axis=-1, keepdims=True)
+    start = start_ref[rows, :]
+    start = jnp.concatenate([start, start], axis=0)
+    spot = lax.broadcasted_iota(jnp.int32, (BLOCK, 1), 0) + step_q * BLOCK
+    spot = jnp.concatenate([spot, spot], axis=0)
+
+    def one(step_k, query_sum):
+        cols = pl.ds(step_k * BLOCK, BLOCK)
+        key = qkv_ref[cols, 2 * HD : 3 * HD]
+        scores = lax.dot_general(query, key, NT, preferred_element_type=jnp.float32) * factor
+        key_spot = lax.broadcasted_iota(jnp.int32, (1, BLOCK), 1) + step_k * BLOCK
+        fits = (key_spot >= start) & (key_spot <= spot)
+        probs = jnp.where(fits, jnp.exp(scores - log_total), 0.0)
+        grad_probs = lax.dot_general(
+            grad, qkv_ref[cols, 3 * HD : 4 * HD], NT, preferred_element_type=jnp.float32
+        )
+        grad_scores = (probs * (grad_probs - weighted)).astype(jnp.bfloat16)
+        value_sum[cols, :] += lax.dot_general(
+            probs.astype(jnp.bfloat16), grad, TN, preferred_element_type=jnp.float32
+        )
+        key_sum[cols, :] += lax.dot_general(
+            grad_scores, query, TN, preferred_element_type=jnp.float32
+        )
+        return query_sum + jnp.dot(grad_scores, key, preferred_element_type=jnp.float32)
+
+    query_sum = lax.fori_loop(
+        first_ref[step_q], step_q + 1, one, jnp.zeros((2 * BLOCK, HD), jnp.float32)
+    )
+    query_sum = (query_sum * factor).astype(jnp.bfloat16)
+    back_ref[rows, 0:HD] = query_sum[:BLOCK]
+    back_ref[rows, HD : 2 * HD] = query_sum[BLOCK:]
+
+    @pl.when(step_q == pl.num_programs(0) - 1)
+    def _():
+        back_ref[:, 2 * HD : 3 * HD] = (key_sum[...] * factor).astype(jnp.bfloat16)
+        back_ref[:, 3 * HD : 4 * HD] = value_sum[...].astype(jnp.bfloat16)
+
+
+def row_starts(lengths_row, total):
+    segment, place = layout(lengths_row, total)
+    positions = jnp.arange(total, dtype=jnp.int32)
+    starts = jnp.where(segment == NDOC - 1, positions, positions - place)
+    return (starts, place)
+
+
+def attention_out(qkv, starts, first):
+    total = qkv.shape[0]
+    whole = lambda i, *_: (0, 0)
+    return pl.pallas_call(
+        attend_forward,
+        out_shape=(
+            jax.ShapeDtypeStruct((total, 2 * HD), jnp.bfloat16),
+            jax.ShapeDtypeStruct((total, 2 * HD), jnp.float32),
+            jax.ShapeDtypeStruct((total, 2), jnp.float32),
+        ),
+        grid_spec=pltpu.PrefetchScalarGridSpec(
+            num_scalar_prefetch=1,
+            grid=(total // BLOCK,),
+            in_specs=[
+                pl.BlockSpec((total, 4 * HD), whole),
+                pl.BlockSpec((total, 1), whole),
+            ],
+            out_specs=[
+                pl.BlockSpec((BLOCK, 2 * HD), lambda i, *_: (i, 0)),
+                pl.BlockSpec((BLOCK, 2 * HD), lambda i, *_: (i, 0)),
+                pl.BlockSpec((BLOCK, 2), lambda i, *_: (i, 0)),
+            ],
+        ),
+        name="attend_forward",
+    )(first, qkv, starts[:, None])
+
+
+def attention_back(qkv, starts, first, grad, kept, log_total):
+    total = qkv.shape[0]
+    whole = lambda i, *_: (0, 0)
+    block = lambda i, *_: (i, 0)
+    return pl.pallas_call(
+        attend_backward,
+        out_shape=jax.ShapeDtypeStruct((total, 4 * HD), jnp.bfloat16),
+        grid_spec=pltpu.PrefetchScalarGridSpec(
+            num_scalar_prefetch=1,
+            grid=(total // BLOCK,),
+            in_specs=[
+                pl.BlockSpec((total, 4 * HD), whole),
+                pl.BlockSpec((total, 1), whole),
+                pl.BlockSpec((BLOCK, 2 * HD), block),
+                pl.BlockSpec((BLOCK, 2 * HD), block),
+                pl.BlockSpec((BLOCK, 2), block),
+            ],
+            out_specs=pl.BlockSpec((total, 4 * HD), whole),
+            scratch_shapes=[
+                pltpu.VMEM((total, HD), jnp.float32),
+                pltpu.VMEM((total, HD), jnp.float32),
+            ],
+        ),
+        name="attend_backward",
+    )(first, qkv, starts[:, None], grad, kept, log_total)
+
+
+def dot_f32(left, right, dims=(((1,), (0,)), ((), ()))):
+    return lax.dot_general(left, right, dims, preferred_element_type=jnp.float32)
+
+
+SUB = 64
+RING = 8
+LANES = 512
+MESH = pl.DeviceIdType.MESH
+
+
+class Relay:
+    def __init__(self, count, own, landed, cross, sems):
+        self.count, self.own, self.landed, self.cross = count, own, landed, cross
+        self.out_sem, self.land_sem, self.back_sem, self.cross_sem = sems
+        spot = lax.axis_index("narrow")
+        self.is_end = (spot == 0) | (spot == 3)
+        self.is_mid = (spot == 1) | (spot == 2)
+        self.inner = 1 + spot // 3
+        self.other = 3 - spot
+        self.outer = jnp.where(spot == 2, 3, 0)
+
+    def to_inner(self, k):
+        return pltpu.make_async_remote_copy(
+            src_ref=self.own.at[k],
+            dst_ref=self.landed.at[k],
+            send_sem=self.out_sem.at[k],
+            recv_sem=self.land_sem.at[k],
+            device_id={"narrow": self.inner},
+            device_id_type=MESH,
+        )
+
+    def to_other(self, k):
+        return pltpu.make_async_remote_copy(
+            src_ref=self.own.at[k],
+            dst_ref=self.cross.at[k % RING],
+            send_sem=self.out_sem.at[k],
+            recv_sem=self.cross_sem.at[k % RING],
+            device_id={"narrow": self.other},
+            device_id_type=MESH,
+        )
+
+    def to_outer(self, k):
+        return pltpu.make_async_remote_copy(
+            src_ref=self.landed.at[k],
+            dst_ref=self.landed.at[k],
+            send_sem=self.back_sem.at[k],
+            recv_sem=self.land_sem.at[k],
+            device_id={"narrow": self.outer},
+            device_id_type=MESH,
+        )
+
+    def greet(self):
+        barrier = pltpu.get_barrier_semaphore()
+
+        @pl.when(self.is_end)
+        def _():
+            pl.semaphore_signal(
+                barrier, inc=1, device_id={"narrow": self.inner}, device_id_type=MESH
+            )
+            pl.semaphore_wait(barrier, 1)
+
+        @pl.when(self.is_mid)
+        def _():
+            pl.semaphore_signal(
+                barrier, inc=1, device_id={"narrow": self.outer}, device_id_type=MESH
+            )
+            pl.semaphore_signal(
+                barrier, inc=1, device_id={"narrow": self.other}, device_id_type=MESH
+            )
+            pl.semaphore_wait(barrier, 2)
+
+    def send(self, first, number):
+        @pl.when(self.is_end)
+        def _():
+            @pl.loop(0, number)
+            def _(i):
+                self.to_inner(first + i).start()
+
+    def tick(self, k):
+        @pl.when(self.is_mid & (k < self.count))
+        def _():
+            self.to_inner(k).wait_recv()
+            self.own[k] = (
+                self.own[k].astype(jnp.float32) + self.landed[k].astype(jnp.float32)
+            ).astype(jnp.bfloat16)
+            self.to_other(k).start()
+
+        @pl.when(self.is_mid & (k >= 2) & (k < self.count + 2))
+        def _():
+            j = k - 2
+            self.to_other(j).wait_recv()
+            self.landed[j] = (
+                self.own[j].astype(jnp.float32) + self.cross[j % RING].astype(jnp.float32)
+            ).astype(jnp.bfloat16)
+            self.to_outer(j).start()
+
+        @pl.when(self.is_end & (k >= 4) & (k < self.count + 4))
+        def _():
+            self.to_outer(k - 4).wait_recv()
+
+    def drain(self):
+        @pl.loop(0, self.count)
+        def _(k):
+            self.to_inner(k).wait_send()
+
+            @pl.when(self.is_mid)
+            def _():
+                self.to_outer(k).wait_send()
+
+
+def relay_scratch(count, model):
+    return [
+        pltpu.VMEM((count, SUB, model), jnp.bfloat16),
+        pltpu.VMEM((count, SUB, model), jnp.bfloat16),
+        pltpu.VMEM((RING, SUB, model), jnp.bfloat16),
+        pltpu.SemaphoreType.DMA((count,)),
+        pltpu.SemaphoreType.DMA((count,)),
+        pltpu.SemaphoreType.DMA((count,)),
+        pltpu.SemaphoreType.DMA((RING,)),
+    ]
+
+
+def feed_kernel(
+    mixed_ref,
+    input_ref,
+    grad_ref,
+    gain_ref,
+    out_w,
+    gate_w,
+    up_w,
+    down_w,
+    hidden_out,
+    active_out,
+    gate_out,
+    upper_out,
+    output_out,
+    middle_out,
+    low_out,
+    mixed_out,
+    gain_out,
+    own,
+    landed,
+    cross,
+    out_sem,
+    land_sem,
+    back_sem,
+    cross_sem,
+    out_v,
+    gate_v,
+    up_v,
+    down_v,
+    mixed_v,
+    rows_v,
+    grads_v,
+    hidden_v,
+    stage_v,
+    scale_v,
+    middle_v,
+    output_v,
+    mixback_v,
+    weight_sem,
+    attn_sem,
+    load_sem,
+    hidden_sem,
+    stage_sem,
+    final_sem,
+):
+    micro, tok, model = input_ref.shape
+    width = out_w.shape[0]
+    piece = out_w.shape[2]
+    groups = width // micro
+    per = tok // SUB
+    hid = gate_w.shape[1]
+    relay = Relay(3 * micro * per, own, landed, cross, (out_sem, land_sem, back_sem, cross_sem))
+    n_up = hid // LANES
+    n_down = model // LANES
+    slots = n_up + n_down
+
+    attn_copies = [
+        pltpu.make_async_copy(
+            mixed_ref.at[i],
+            mixed_v.at[i // groups, :, pl.ds((i % groups) * 2 * HD, 2 * HD)],
+            attn_sem.at[i],
+        )
+        for i in range(width)
+    ] + [
+        pltpu.make_async_copy(
+            out_w.at[i], out_v.at[:, pl.ds(i * piece, piece)], attn_sem.at[width + i]
+        )
+        for i in range(width)
+    ]
+    weight_copies = [
+        pltpu.make_async_copy(gate_w, gate_v, weight_sem.at[0]),
+        pltpu.make_async_copy(up_w, up_v, weight_sem.at[1]),
+    ] + [
+        pltpu.make_async_copy(
+            down_w.at[i], down_v.at[:, pl.ds(i * piece, piece)], weight_sem.at[2 + i]
+        )
+        for i in range(width)
+    ]
+    for copy in attn_copies + weight_copies:
+        copy.start()
+
+    def loads(n):
+        slot = n % 2
+        return (
+            pltpu.make_async_copy(input_ref.at[n % micro], rows_v.at[slot], load_sem.at[slot, 0]),
+            pltpu.make_async_copy(grad_ref.at[n % micro], grads_v.at[slot], load_sem.at[slot, 1]),
+        )
+
+    def start_loads(n):
+        for copy in loads(n):
+            copy.start()
+
+    def wait_loads(n):
+        for copy in loads(n):
+            copy.wait()
+
+    start_loads(0)
+    gain_out[...] = jnp.zeros_like(gain_out)
+    relay.greet()
+    for copy in attn_copies:
+        copy.wait()
+
+    @pl.loop(0, micro)
+    def _(m):
+        for n in range(n_down):
+            cols = pl.ds(n * LANES, LANES)
+            part = dot_f32(mixed_v[m], out_v[:, cols]).astype(jnp.bfloat16)
+            for r in range(per):
+                own[m * per + r, :, cols] = part[r * SUB : (r + 1) * SUB]
+        relay.send(m * per, per)
+
+    first_ticks = per + 4
+
+    @pl.loop(0, first_ticks)
+    def _(k):
+        relay.tick(k)
+
+    for copy in weight_copies:
+        copy.wait()
+
+    def hidden_copy(m):
+        return pltpu.make_async_copy(hidden_v, hidden_out.at[m], hidden_sem)
+
+    def stage_copies(m):
+        return [
+            pltpu.make_async_copy(stage_v.at[i], target.at[m], stage_sem.at[i])
+            for i, target in enumerate((active_out, gate_out, upper_out))
+        ]
+
+    base = micro * per
+
+    @pl.loop(0, micro)
+    def _(m):
+        slot = m % 2
+        wait_loads(m)
+        start_loads(m + 1)
+
+        @pl.when(m > 0)
+        def _():
+            hidden_copy(m - 1).wait()
+            for copy in stage_copies(m - 1):
+                copy.wait()
+
+        for r in range(per):
+            span = pl.ds(r * SUB, SUB)
+            middle = rows_v[slot, span, :].astype(jnp.float32) + landed[m * per + r].astype(
+                jnp.float32
+            )
+            scale = lax.rsqrt(jnp.mean(middle * middle, axis=-1, keepdims=True) + EPSILON)
+            scale_v[span, :] = scale
+            hidden_v[span, :] = (middle * scale * gain_ref[...]).astype(jnp.bfloat16)
+        hidden_copy(m).start()
+        for j in range(n_up):
+            relay.tick(first_ticks + slots * m + j)
+            cols = pl.ds(j * LANES, LANES)
+            gate = dot_f32(hidden_v[...], gate_v[:, cols])
+            up_proj = dot_f32(hidden_v[...], up_v[:, cols])
+            grad_active = dot_f32(grads_v[slot], down_v[cols, :], NT)
+            squash = 1.0 / (1.0 + jnp.exp(-gate))
+            silu = gate * squash
+            stage_v[0, :, cols] = (silu * up_proj).astype(jnp.bfloat16)
+            stage_v[1, :, cols] = (
+                grad_active * up_proj * (squash * (1.0 + gate * (1.0 - squash)))
+            ).astype(jnp.bfloat16)
+            stage_v[2, :, cols] = (grad_active * silu).astype(jnp.bfloat16)
+        for copy in stage_copies(m):
+            copy.start()
+        for n in range(n_down):
+            relay.tick(first_ticks + slots * m + n_up + n)
+            cols = pl.ds(n * LANES, LANES)
+            back = dot_f32(stage_v[1], gate_v[cols, :], NT) + dot_f32(
+                stage_v[2], up_v[cols, :], NT
+            )
+            ahead = dot_f32(stage_v[0], down_v[:, cols]).astype(jnp.bfloat16)
+            gain_sum = jnp.zeros((1, LANES), jnp.float32)
+            for r in range(per):
+                part = slice(r * SUB, (r + 1) * SUB)
+                own[base + 2 * per * m + r, :, cols] = back[part].astype(jnp.bfloat16)
+                own[base + 2 * per * m + per + r, :, cols] = ahead[part]
+                unit = (
+                    rows_v[slot, pl.ds(r * SUB, SUB), cols].astype(jnp.float32)
+                    + landed[m * per + r, :, cols].astype(jnp.float32)
+                ) * scale_v[pl.ds(r * SUB, SUB), :]
+                gain_sum += jnp.sum(back[part] * unit, axis=0, keepdims=True)
+            gain_out[:, cols] += gain_sum
+        relay.send(base + 2 * per * m, 2 * per)
+
+    hidden_copy(micro - 1).wait()
+    for copy in stage_copies(micro - 1):
+        copy.wait()
+
+    def final_copies(m):
+        return [
+            pltpu.make_async_copy(middle_v, middle_out.at[m], final_sem.at[0]),
+            pltpu.make_async_copy(hidden_v, low_out.at[m], final_sem.at[1]),
+            pltpu.make_async_copy(output_v, output_out.at[m], final_sem.at[2]),
+        ] + [
+            pltpu.make_async_copy(
+                mixback_v.at[:, pl.ds(g * 2 * HD, 2 * HD)],
+                mixed_out.at[m * groups + g],
+                final_sem.at[3 + g],
+            )
+            for g in range(groups)
+        ]
+
+    last_ticks = first_ticks + slots * micro
+    rest = 3 * micro * per + 4 - last_ticks
+    turns = rest // micro
+
+    @pl.loop(0, micro)
+    def _(m):
+        slot = m % 2
+        wait_loads(m + micro)
+
+        @pl.when(m < micro - 1)
+        def _():
+            start_loads(m + micro + 1)
+
+        @pl.when(m > 0)
+        def _():
+            for copy in final_copies(m - 1):
+                copy.wait()
+
+        for t in range(turns // 2):
+            relay.tick(last_ticks + turns * m + t)
+        for r in range(per):
+            span = pl.ds(r * SUB, SUB)
+            middle = rows_v[slot, span, :].astype(jnp.float32) + landed[m * per + r].astype(
+                jnp.float32
+            )
+            scale = lax.rsqrt(jnp.mean(middle * middle, axis=-1, keepdims=True) + EPSILON)
+            pulled = landed[base + 2 * per * m + r].astype(jnp.float32) * gain_ref[...]
+            along = jnp.mean(pulled * middle, axis=-1, keepdims=True)
+            grad_middle = grads_v[slot, span, :].astype(jnp.float32) + scale * (
+                pulled - middle * (scale * scale * along)
+            )
+            middle_v[span, :] = grad_middle
+            hidden_v[span, :] = grad_middle.astype(jnp.bfloat16)
+        mixback_v[...] = dot_f32(hidden_v[...], out_v[...], NT).astype(jnp.bfloat16)
+        for t in range(turns // 2, turns):
+            relay.tick(last_ticks + turns * m + t)
+        for r in range(per):
+            span = pl.ds(r * SUB, SUB)
+            output_v[span, :] = (
+                rows_v[slot, span, :].astype(jnp.float32)
+                + landed[m * per + r].astype(jnp.float32)
+                + landed[base + 2 * per * m + per + r].astype(jnp.float32)
+            ).astype(jnp.bfloat16)
+        for copy in final_copies(m):
+            copy.start()
+
+    for copy in final_copies(micro - 1):
+        copy.wait()
+    relay.drain()
+
+
+def feed_forward(mixed, layer_input, grad_out, gain_ffn, out_w, gate_w, up_w, down_w):
+    micro, tok, model = layer_input.shape
+    width, heads_in, piece = out_w.shape
+    hid = gate_w.shape[1]
+    groups = width // micro
+    low = jnp.bfloat16
+    count = 3 * micro * (tok // SUB)
+    anywhere = pl.BlockSpec(memory_space=pl.ANY)
+    inside = pl.BlockSpec(memory_space=pltpu.VMEM)
+    return pl.pallas_call(
+        feed_kernel,
+        out_shape=(
+            jax.ShapeDtypeStruct((micro, tok, model), low),
+            jax.ShapeDtypeStruct((micro, tok, hid), low),
+            jax.ShapeDtypeStruct((micro, tok, hid), low),
+            jax.ShapeDtypeStruct((micro, tok, hid), low),
+            jax.ShapeDtypeStruct((micro, tok, model), low),
+            jax.ShapeDtypeStruct((micro, tok, model), jnp.float32),
+            jax.ShapeDtypeStruct((micro, tok, model), low),
+            jax.ShapeDtypeStruct((width, tok, 2 * HD), low),
+            jax.ShapeDtypeStruct((1, model), jnp.float32),
+        ),
+        in_specs=[anywhere] * 3 + [inside] + [anywhere] * 4,
+        out_specs=[anywhere] * 8 + [inside],
+        scratch_shapes=relay_scratch(count, model)
+        + [
+            pltpu.VMEM((heads_in, model), low),
+            pltpu.VMEM((model, hid), low),
+            pltpu.VMEM((model, hid), low),
+            pltpu.VMEM((hid, model), low),
+            pltpu.VMEM((micro, tok, heads_in), low),
+            pltpu.VMEM((2, tok, model), low),
+            pltpu.VMEM((2, tok, model), low),
+            pltpu.VMEM((tok, model), low),
+            pltpu.VMEM((3, tok, hid), low),
+            pltpu.VMEM((tok, 1), jnp.float32),
+            pltpu.VMEM((tok, model), jnp.float32),
+            pltpu.VMEM((tok, model), low),
+            pltpu.VMEM((tok, heads_in), low),
+            pltpu.SemaphoreType.DMA((2 + width,)),
+            pltpu.SemaphoreType.DMA((2 * width,)),
+            pltpu.SemaphoreType.DMA((2, 2)),
+            pltpu.SemaphoreType.DMA,
+            pltpu.SemaphoreType.DMA((3,)),
+            pltpu.SemaphoreType.DMA((3 + groups,)),
+        ],
+        compiler_params=pltpu.CompilerParams(
+            collective_id=0, has_side_effects=True, vmem_limit_bytes=67043328
+        ),
+        cost_estimate=pl.CostEstimate(
+            flops=200_000_000_000, bytes_accessed=900_000_000, transcendentals=0
+        ),
+        name="feed_forward",
+    )(mixed, layer_input, grad_out, gain_ffn[None, :], out_w, gate_w, up_w, down_w)
+
+
+def local_batched(
+    layer_input,
+    grad_out,
+    lengths,
+    w_query,
+    w_key,
+    w_value,
+    w_out,
+    w_gate,
+    w_up,
+    w_down,
+    gain_attn,
+    gain_ffn,
+    gain_query,
+    gain_key,
+):
+    micro, tok_rows, model = layer_input.shape
+    width = lax.axis_size("wide")
+    groups = w_key.shape[1] // HD
+    total = tok_rows * width
+    count = micro * tok_rows
+    me = lax.axis_index("wide")
+    w_qkv = lax.all_gather(
+        jnp.concatenate([w_query, w_key, w_value], axis=1), "wide", axis=0, tiled=True
+    )
+    w_out_all = lax.all_gather(w_out, "wide", axis=0)
+    w_gate_full = lax.all_gather(w_gate, "wide", axis=0, tiled=True)
+    w_up_full = lax.all_gather(w_up, "wide", axis=0, tiled=True)
+    w_down_all = lax.all_gather(w_down, "wide", axis=0)
+    starts, places = jax.vmap(lambda row: row_starts(row, total))(lengths)
+    my_places = lax.dynamic_slice_in_dim(places, me * tok_rows, tok_rows, axis=1)
+    cosine, sine = jax.vmap(angles)(my_places)
+    cosine = cosine.reshape(count, 1, HD)
+    sine = sine.reshape(count, 1, HD)
+    my_starts = lax.dynamic_index_in_dim(starts, me // groups, axis=0, keepdims=False)
+    my_first = my_starts[::BLOCK] // BLOCK
+
+    def head_norm(rows, gain):
+        return rotate(rms_norm(rows, gain), cosine, sine)
+
+    input_float = layer_input.reshape(count, model).astype(jnp.float32)
+    grad_rows = grad_out.reshape(count, model)
+    normed_one, pull_one = jax.vjp(lambda rows: rms_norm(rows, gain_attn), input_float)
+    hidden_one = normed_one.astype(jnp.bfloat16)
+    qkv = dot_f32(hidden_one, w_qkv)
+    q_cols = w_query.shape[1]
+    k_cols = w_key.shape[1]
+    query_turned, pull_query = jax.vjp(
+        head_norm, qkv[:, :q_cols].reshape(count, -1, HD), gain_query
+    )
+    key_turned, pull_key = jax.vjp(
+        head_norm, qkv[:, q_cols : q_cols + k_cols].reshape(count, -1, HD), gain_key
+    )
+    packed = jnp.concatenate(
+        [
+            query_turned.reshape(micro, tok_rows, groups, 2 * HD),
+            key_turned.reshape(micro, tok_rows, groups, HD),
+            qkv[:, q_cols + k_cols :].reshape(micro, tok_rows, groups, HD),
+        ],
+        axis=-1,
+    ).astype(jnp.bfloat16)
+    packed = jnp.moveaxis(packed, 2, 1).reshape(width, tok_rows, 4 * HD)
+    packed = lax.all_to_all(packed, "wide", split_axis=0, concat_axis=0).reshape(total, 4 * HD)
+    mixed, kept, log_total = attention_out(packed, my_starts, my_first)
+    mixed = lax.all_to_all(
+        mixed.reshape(width, tok_rows, 2 * HD), "wide", split_axis=0, concat_axis=0
+    )
+    (
+        hidden_two,
+        active_low,
+        gate_back,
+        upper_back,
+        output,
+        grad_middle,
+        middle_low,
+        grad_mixed,
+        gain_two,
+    ) = feed_forward(
+        mixed, layer_input, grad_out, gain_ffn, w_out_all, w_gate_full, w_up_full, w_down_all
+    )
+    gain_two = gain_two[0]
+    hidden_two = hidden_two.reshape(count, model)
+    active_low = active_low.reshape(count, -1)
+    gate_back = gate_back.reshape(count, -1)
+    upper_back = upper_back.reshape(count, -1)
+    grad_middle = grad_middle.reshape(count, model)
+    middle_low = middle_low.reshape(count, model)
+    mixed_low = jnp.moveaxis(
+        mixed.reshape(micro, groups, tok_rows, 2 * HD), 1, 2
+    ).reshape(count, groups * 2 * HD)
+    grad_mixed = lax.all_to_all(grad_mixed, "wide", split_axis=0, concat_axis=0)
+    back = attention_back(
+        packed, my_starts, my_first, grad_mixed.reshape(total, 2 * HD), kept, log_total
+    )
+    back = lax.all_to_all(
+        back.reshape(width, tok_rows, 4 * HD), "wide", split_axis=0, concat_axis=0
+    )
+    back = jnp.moveaxis(back.reshape(micro, groups, tok_rows, 4 * HD), 1, 2)
+    back = back.reshape(count, groups, 4 * HD)
+    grad_qraw, gain_q = pull_query(
+        back[..., : 2 * HD].reshape(count, -1, HD).astype(jnp.float32)
+    )
+    grad_kraw, gain_k = pull_key(back[..., 2 * HD : 3 * HD].astype(jnp.float32))
+    qkv_back = jnp.concatenate(
+        [
+            grad_qraw.reshape(count, -1).astype(jnp.bfloat16),
+            grad_kraw.reshape(count, -1).astype(jnp.bfloat16),
+            back[..., 3 * HD :].reshape(count, -1),
+        ],
+        axis=1,
+    )
+    partial_one = dot_f32(qkv_back, w_qkv, NT)
+    gain_one = jnp.sum(partial_one * unit_rows(input_float), axis=0)
+    grad_input = (
+        grad_middle
+        + pull_one(lax.psum(partial_one.astype(jnp.bfloat16), "narrow").astype(jnp.float32))[0]
+    )
+
+    def scatter(left, right):
+        part = dot_f32(left, right, TN).astype(jnp.bfloat16)
+        return lax.psum_scatter(part, "wide", scatter_dimension=0, tiled=True).astype(jnp.float32)
+
+    def scatter_cols(left, right):
+        part = dot_f32(left, right, TN).astype(jnp.bfloat16)
+        return lax.psum_scatter(part, "wide", scatter_dimension=1, tiled=True).astype(jnp.float32)
+
+    grad_wgate = scatter(hidden_two, gate_back)
+    grad_wup = scatter(hidden_two, upper_back)
+    grad_wdown = scatter_cols(active_low, grad_rows)
+    grad_wout = scatter_cols(mixed_low, middle_low)
+    grad_wqkv = scatter(hidden_one, qkv_back)
+    gains = lax.psum((gain_one, gain_two, gain_q, gain_k), ("wide", "narrow"))
+    return (
+        output,
+        grad_input.reshape(micro, tok_rows, model),
+        grad_wqkv[:, :q_cols],
+        grad_wqkv[:, q_cols : q_cols + k_cols],
+        grad_wqkv[:, q_cols + k_cols :],
+        grad_wout,
+        grad_wgate,
+        grad_wup,
+        grad_wdown,
+    ) + tuple(gains)
+
+
+def local(mesh, layer_input, grad_out, lengths, w_query, w_key, *rest):
+    width = mesh.shape["wide"]
+    micro, tok_rows = layer_input.shape[:2]
+    groups = w_key.shape[1] // HD
+    fits = (
+        micro * groups == width
+        and w_query.shape[1] == 2 * w_key.shape[1]
+        and mesh.shape["narrow"] == 4
+        and tok_rows == BLOCK
+    )
+    chosen = local_batched if fits else local_general
+    return chosen(layer_input, grad_out, lengths, w_query, w_key, *rest)
+
+
 def solution(mesh):
     in_specs = (
         P(None, "wide", None),
@@ -335,4 +1099,5 @@
         P(),
         P(),
     )
-    return jax.shard_map(local, mesh=mesh, in_specs=in_specs, out_specs=out_specs, check_vma=False)
+    return jax.shard_map(
+        functools.partial(local, mesh), mesh=mesh, in_specs=in_specs, out_specs=out_specs, check_vma=False)

time: 1980 us -> 1080 us (0.55)
  waiting for transfers between devices: 1340 us -> 455 us
  Pallas kernels: 0 us -> 345 us
  matrix products: 388 us -> 62 us
  other arithmetic: 127 us -> 62.3 us
  blocking collectives: 39.3 us -> 59.3 us
    psum x4 -> x1, waiting for transfers between devices: 625 us -> 106 us  [local_batched(): lax.psum(partial_one.astype(jnp.bfloat16), 'narrow').astype(jnp.float32)]
    pallas_call x0 -> x3, Pallas kernels: none -> 345 us  [the longest x1 304 us: feed_forward(): pl.pallas_call(feed_kernel, out_shape=(jax.ShapeDtypeStruct((micro, tok,...]
    dot_general x108 -> x7, matrix products: 388 us -> 62 us  [dot_f32(): lax.dot_general(left, right, dims, preferred_element_type=jnp.float32)]
    all_gather x15 -> x5, waiting for transfers between devices: 348 us -> 89.9 us  [the longest x1 47.3 us: local_batched(): w_down_all = lax.all_gather(w_down, 'wide', axis=0)]
    reduce_scatter x15 -> x5, waiting for transfers between devices: 362 us -> 185 us  [the longest x3 121 us: scatter(): lax.psum_scatter(part, 'wide', scatter_dimension=0, tiled=True)]
    all_to_all x0 -> x3, waiting for transfers between devices: none -> 72.1 us  [the longest x1 32.8 us: local_batched(): lax.all_to_all(packed, 'wide', split_axis=0, concat_axis=0)]
    convert_element_type x23 -> x7, other arithmetic: 40.9 us -> 15.6 us  [the longest x1 5.22 us: local_batched(): hidden_one = normed_one.astype(jnp.bfloat16)]
  transfers between devices with their start and end apart: 34 -> 14, of which waited for: 28 -> 10; matrix products, arithmetic and copies ran while one was open for 20% -> 15% of each run, Pallas kernels for 0% -> 2%
where the time goes in v1:
time: 1080 us; the launch traced here: 1070 us
  waiting for transfers between devices  455 us (42%)
  Pallas kernels  345 us (32%)
  other arithmetic  62.3 us (6%)
  matrix products  62 us (6%)
  blocking collectives  59.3 us (5%)
  local copies, waits for them, and re-layouts  57.1 us (5%)
  between operations  14.9 us (1%)
  starting transfers between devices  11.9 us (1%)
    pallas_call x1, Pallas kernels, feed_forward(): pl.pallas_call(feed_kernel, out_shape=(jax.ShapeDtypeStruct((micro, tok,...  304 us
    reduce_scatter x3, waiting for transfers between devices, scatter(): lax.psum_scatter(part, 'wide', scatter_dimension=0, tiled=True)  121 us
    psum x1, waiting for transfers between devices, local_batched(): lax.psum(partial_one.astype(jnp.bfloat16), 'narrow').astype(jnp.float32)  106 us
    reduce_scatter x2, waiting for transfers between devices, scatter_cols(): lax.psum_scatter(part, 'wide', scatter_dimension=1, tiled=True)  63.1 us
    dot_general x7, matrix products, dot_f32(): lax.dot_general(left, right, dims, preferred_element_type=jnp.float32)  62 us
    all_gather x1, waiting for transfers between devices, local_batched(): w_down_all = lax.all_gather(w_down, 'wide', axis=0)  47.3 us
    psum x1, blocking collectives, local_batched(): gains = lax.psum((gain_one, gain_two, gain_q, gain_k), ('wide', 'narrow'))  39.7 us
    all_to_all x1, waiting for transfers between devices, local_batched(): lax.all_to_all(packed, 'wide', split_axis=0, concat_axis=0)  32.8 us
  transfers between devices with their start and end apart: 14, of which 10 were waited for; matrix products, arithmetic and copies ran while one was open for 15% of the time, Pallas kernels for 2%

profile of v1, /device:TPU:0, one launch (start us, length us, event | category | flops | bytes accessed | tf_op | source)
XLA Modules:
  0.0 1066.8 jit_solution(14442483780642495016)
XLA Ops:
  22.0 5.0 fusion.19
  27.0 5.2 fusion.3
  32.2 17.7 %all-gather.8.cloned.1.call-done = bf16[2048,1024]{1,0:T(8,128)(2,1)} async-done(((bf16[256,1024]{1,0:T(8,128)(2,1)}), bf16[2048,1024]{1,0:T(8,128)(2,1)}) %all-gather.8.cloned.1.call-update) | async-done | bytes 4194320 | tf_op jit(solution)/shard_map/all_gather | solution.py:933
  49.9 7.6 fusion.29
  67.8 3.2 mul.319
  92.5 3.6 all-to-all-start
  98.1 32.8 %all-to-all-done = bf16[8,256,512]{2,1,0:T(8,128)(2,1)S(1)} async-done(((bf16[8,256,512]{2,1,0:T(8,128)(2,1)}), bf16[8,256,512]{2,1,0:T(8,128)(2,1)S(1)}, u32[]{:S(2)}, u32[]{:S(2)}) %all-to-all-start) | async-done | bytes 2097184 | tf_op jit(solution)/shard_map/all_to_all | solution.py:973
  132.3 18.9 %attend_forward.1 = (bf16[2048,256]{1,0:T(8,128)(2,1)}, f32[2048,256]{1,0:T(8,128)}, f32[2048,2]{1,0:T(8,128)}) custom-call(s32[8]{0:T(128)} %and_select_fusion.first_ref, bf16[2048,512]{1,0:T(8,128)(2,1)} %bitcast.102, s32[2048,1]{1,0:T(8,128)} %copy.41.start_ref), custom_call_target="tpu_custom_call" | custom-call | tf_op jit(solution)/shard_map/attend_forward/pallas_call | solution.py:426
  151.2 4.2 all-to-all-start.1
  155.4 19.3 %all-to-all-done.1.mixed_ref = bf16[8,256,256]{2,1,0:T(8,128)(2,1)} async-done(((bf16[8,256,256]{2,1,0:T(8,128)(2,1)}), bf16[8,256,256]{2,1,0:T(8,128)(2,1)}, u32[]{:S(2)}, u32[]{:S(2)}) %all-to-all-start.1) | async-done | bytes 1048608 | tf_op jit(solution)/shard_map/all_to_all | solution.py:975
  174.8 24.8 %all-gather.12.cloned.1.call-done.up_w = bf16[2048,1536]{1,0:T(8,128)(2,1)} async-done(((bf16[256,1536]{1,0:T(8,128)(2,1)}), bf16[2048,1536]{1,0:T(8,128)(2,1)}) %all-gather.12.cloned.1.call-update) | async-done | bytes 6291472 | tf_op jit(solution)/shard_map/all_gather | solution.py:938
  199.6 47.3 %all-gather.16.cloned.1.call-done = bf16[12288,256]{1,0:T(8,128)(2,1)} async-done(((bf16[1536,256]{1,0:T(8,128)(2,1)}), bf16[12288,256]{1,0:T(8,128)(2,1)}) %all-gather.16.cloned.1.call-update) | async-done | bytes 6291472 | tf_op jit(solution)/shard_map/all_gather | solution.py:939
  246.9 303.8 %feed_forward.1 = (bf16[4,256,2048]{2,1,0:T(8,128)(2,1)}, bf16[4,256,1536]{2,1,0:T(8,128)(2,1)}, bf16[4,256,1536]{2,1,0:T(8,128)(2,1)}, bf16[4,256,1536]{2,1,0:T...) custom-call(bf16[8,256,256]{2,1,0:T(8,128)(2,1)} %all-to-all-done.1., ...), custom_call_target="tpu_custom_call" | custom-call | flops 199999995904 | bytes 900000000 | tf_op jit(solution)/shard_map/feed_forward/pallas_call | solution.py:864
  550.7 19.6 %all_to_all.20 = bf16[8,256,256]{2,1,0:T(8,128)(2,1)} all-to-all(bf16[8,256,256]{2,1,0:T(8,128)(2,1)} %get-tuple-element.28), channel_id=1, replica_groups=mesh['wide'=8,'narrow'=4] {'wide'}, dimensions={0} | all-to-all | bytes 2097152 | tf_op jit(solution)/shard_map/all_to_all | solution.py:1001
  570.3 22.1 %attend_backward.1 = bf16[2048,512]{1,0:T(8,128)(2,1)} custom-call(s32[8]{0:T(128)} %and_select_fusion.first_ref, bf16[2048,512]{1,0:T(8,128)(2,1)} %bitcast.103, s32[2048,1]{1,0:T(8,128)} %copy.41.start_ref, bf16[2048,256]{1,0:T(8,128)(2,1)} %bitcast.113, f32[2048,256]{1,0:T(8,128)} %get-tuple-element.29.kept_ref, f32[2048,2]{1,0:T(8,128)} %get-tuple-element.30.log_ref), custom_call_target="tpu_custom_call" | custom-call | tf_op jit(solution)/shard_map/attend_backward/pallas_call | solution.py:454
  592.4 3.6 all-to-all-start.3
  598.8 3.8 convolution_convert_fusion.1
  602.6 19.9 %all-to-all-done.3 = bf16[8,256,512]{2,1,0:T(8,128)(2,1)S(1)} async-done(((bf16[8,256,512]{2,1,0:T(8,128)(2,1)}), bf16[8,256,512]{2,1,0:T(8,128)(2,1)S(1)}, u32[]{:S(2)}, u32[]{:S(2)}) %all-to-all-start.3) | async-done | bytes 2097184 | tf_op jit(solution)/shard_map/all_to_all | solution.py:1005
  625.3 3.3 reshape.250
  638.0 7.5 fusion.28
  646.5 9.6 convolution_convert_fusion
  658.0 11.3 %bitcast_convert_fusion.1 = bf16[2048,1536]{1,0:T(8,128)(2,1)} fusion(bf16[4,256,2048]{2,1,0:T(8,128)(2,1)} %get-tuple-element.32, bf16[4,256,1536]{2,1,0:T(8,128)(2,1)S(1)} %copy-done.39), kind=kOutput, calls=%fused_computation.1 | convolution fusion | flops 6445596672 | bytes 13631488 | tf_op jit(solution)/shard_map/dot_general | solution.py:478
  671.2 11.0 %bitcast_convert_fusion.2 = bf16[2048,1536]{1,0:T(8,128)(2,1)} fusion(bf16[4,256,2048]{2,1,0:T(8,128)(2,1)} %get-tuple-element.32, bf16[4,256,1536]{2,1,0:T(8,128)(2,1)S(1)} %copy-done.38), kind=kOutput, calls=%fused_computation.2 | convolution fusion | flops 6445596672 | bytes 13631488 | tf_op jit(solution)/shard_map/dot_general | solution.py:478
  684.2 11.2 %bitcast_convert_fusion = bf16[1536,2048]{1,0:T(8,128)(2,1)} fusion(bf16[4,256,1536]{2,1,0:T(8,128)(2,1)S(1)} %copy-done.37, bf16[4,256,2048]{2,1,0:T(8,128)(2,1)} %grad_ref.1), kind=kOutput, calls=%fused_computation | convolution fusion | flops 6445596672 | bytes 13631488 | tf_op jit(solution)/shard_map/dot_general | solution.py:478
  697.2 105.6 %all-reduce.7.cloned.1.call-done = bf16[1024,2048]{1,0:T(8,128)(2,1)} async-done(((bf16[1024,2048]{1,0:T(8,128)(2,1)}), bf16[1024,2048]{1,0:T(8,128)(2,1)}) %all-reduce.7.cloned.1.call-update) | async-done | bytes 4194320 | tf_op jit(solution)/shard_map/psum | solution.py:1026
  802.8 7.4 fusion.4
  810.2 39.7 %all-reduce.4 = (f32[2048]{0:T(1024)}, f32[2048]{0:T(1024)}, f32[128]{0:T(128)}, f32[128]{0:T(128)}) all-reduce(f32[2048]{0:T(1024)S(1)} %get-tuple-element.37, f32[2048]{0:T(1024)S(1)} %bitcast.128, f32[128]{0:T(128)S(1)} %get-tuple-element.41, f32[128]{0:T(128)S(1)} %get-tuple-element.39), channel_id=1, replica_groups=mesh['wide'=8,'narrow'=4] {'wide','narrow'}, use_global_device_ids=true, to_apply=%region_16.17 | all-reduce | flops 4352 | bytes 34816 | tf_op jit(solution)/shard_map/psum | solution.py:1042
  849.9 9.8 fusion
  863.2 58.9 %reduce-scatter.12.cloned.1.call-done = bf16[256,1536]{1,0:T(8,128)(2,1)} async-done(((bf16[2048,1536]{1,0:T(8,128)(2,1)}), bf16[256,1536]{1,0:T(8,128)(2,1)}) %reduce-scatter.12.cloned.1.call-update) | async-done | bytes 786448 | tf_op jit(solution)/shard_map/reduce_scatter | solution.py:1031
  924.6 62.5 %reduce-scatter.10.cloned.1.call-done = bf16[256,1536]{1,0:T(8,128)(2,1)} async-done(((bf16[2048,1536]{1,0:T(8,128)(2,1)}), bf16[256,1536]{1,0:T(8,128)(2,1)}) %reduce-scatter.10.cloned.1.call-update) | async-done | bytes 786448 | tf_op jit(solution)/shard_map/reduce_scatter | solution.py:1031
  989.6 63.1 %reduce-scatter.14.cloned.1.call-done = bf16[1536,256]{1,0:T(8,128)(2,1)} async-done(((bf16[1536,2048]{1,0:T(8,128)(2,1)}), bf16[1536,256]{1,0:T(8,128)(2,1)}) %reduce-scatter.14.cloned.1.call-update) | async-done | bytes 786448 | tf_op jit(solution)/shard_map/reduce_scatter | solution.py:1035
  1055.0 4.8 copy.56
  (175 shorter events, 83.8 us)
Async XLA Ops:
  7.2 42.8 %all-gather.8.cloned.1.call-start = ((), (), s32[]{:S(2)}) async-start(), calls=%async_computation.9 | async-start | bytes 4718592 | tf_op jit(solution)/shard_map/all_gather | solution.py:933
  9.2 146.2 %all-gather.14.cloned.1.call-start = ((), (), s32[]{:S(2)}) async-start(), calls=%async_computation.18 | async-start | bytes 2359296 | tf_op jit(solution)/shard_map/all_gather | solution.py:936
  9.9 5.6 copy-start.29
  10.0 164.8 %all-gather.10.cloned.1.call-start = ((), (), s32[]{:S(2)}) async-start(), calls=%async_computation.10 | async-start | bytes 7077888 | tf_op jit(solution)/shard_map/all_gather | solution.py:937
  10.7 188.9 %all-gather.12.cloned.1.call-start = ((), (), s32[]{:S(2)}) async-start(), calls=%async_computation.11 | async-start | bytes 7077888 | tf_op jit(solution)/shard_map/all_gather | solution.py:938
  11.3 235.6 %all-gather.16.cloned.1.call-start = ((), (), s32[]{:S(2)}) async-start(), calls=%async_computation.19 | async-start | bytes 7077888 | tf_op jit(solution)/shard_map/all_gather | solution.py:939
  15.6 11.4 %copy-start.25 = (f32[1024]{0:T(1024)}, f32[1024]{0:T(1024)S(1)}, u32[]{:S(2)}) copy-start(f32[1024]{0:T(1024)S(1)} %rsqrt.35) | copy-start | bytes 12292
  19.9 7.1 copy-start.33
  19.9 7.1 copy-start.21
  57.7 13.3 %copy-start.3 = (f32[1024,512]{0,1:T(8,128)}, f32[1024,512]{0,1:T(8,128)S(1)}, u32[]{:S(2)}) copy-start(f32[1024,512]{0,1:T(8,128)S(1)} %slice.57) | copy-start | bytes 6291460
  57.8 20.8 %copy-start.7 = (f32[1024,256]{0,1:T(8,128)}, f32[1024,256]{0,1:T(8,128)S(1)}, u32[]{:S(2)}) copy-start(f32[1024,256]{0,1:T(8,128)S(1)} %slice.60) | copy-start | bytes 3145732
  59.7 6.4 copy-start.15
  71.0 4.1 copy-start.31
  78.5 6.2 copy-start.8
  84.8 3.2 copy-start.12
  92.5 38.4 %all-to-all-start = ((bf16[8,256,512]{2,1,0:T(8,128)(2,1)}), bf16[8,256,512]{2,1,0:T(8,128)(2,1)S(1)}, u32[]{:S(2)}, u32[]{:S(2)}) async-start(bf16[8,256,512]{2,1,0:T(8,128)(2,1)} %bitcast.110), calls=%async_computation | async-start | bytes 4194304 | tf_op jit(solution)/shard_map/all_to_all | solution.py:973
  151.2 23.6 %all-to-all-start.1 = ((bf16[8,256,256]{2,1,0:T(8,128)(2,1)}), bf16[8,256,256]{2,1,0:T(8,128)(2,1)}, u32[]{:S(2)}, u32[]{:S(2)}) async-start(bf16[8,256,256]{2,1,0:T(8,128)(2,1)} %bitcast.115), calls=%async_computation.1 | async-start | bytes 2097152 | tf_op jit(solution)/shard_map/all_to_all | solution.py:975
  592.4 30.2 %all-to-all-start.3 = ((bf16[8,256,512]{2,1,0:T(8,128)(2,1)}), bf16[8,256,512]{2,1,0:T(8,128)(2,1)S(1)}, u32[]{:S(2)}, u32[]{:S(2)}) async-start(bf16[8,256,512]{2,1,0:T(8,128)(2,1)} %bitcast.109), calls=%async_computation.3 | async-start | bytes 4194304 | tf_op jit(solution)/shard_map/all_to_all | solution.py:1005
  596.0 99.4 %reduce-scatter.8.cloned.1.call-start = ((), (), s32[]{:S(2)}) async-start(), calls=%async_computation.14 | async-start | bytes 2359296 | tf_op jit(solution)/shard_map/reduce_scatter | solution.py:1035
  602.6 200.2 %all-reduce.7.cloned.1.call-start = ((), (), s32[]{:S(2)}) async-start(), calls=%async_computation.12 | async-start | bytes 8388608 | tf_op jit(solution)/shard_map/psum | solution.py:1026
  625.3 3.3 copy-start.11
  625.3 3.6 copy-start.6
  625.3 3.6 copy-start.18
  632.7 4.0 copy-start.13
  645.5 214.1 %reduce-scatter.6.cloned.1.call-start = ((), (), s32[]{:S(2)}) async-start(), calls=%async_computation.13 | async-start | bytes 4718592 | tf_op jit(solution)/shard_map/reduce_scatter | solution.py:1031
  656.2 265.9 %reduce-scatter.12.cloned.1.call-start = ((), (), s32[]{:S(2)}) async-start(), calls=%async_computation.16 | async-start | bytes 7077888 | tf_op jit(solution)/shard_map/reduce_scatter | solution.py:1031
  669.4 317.8 %reduce-scatter.10.cloned.1.call-start = ((), (), s32[]{:S(2)}) async-start(), calls=%async_computation.15 | async-start | bytes 7077888 | tf_op jit(solution)/shard_map/reduce_scatter | solution.py:1031
  682.3 370.4 %reduce-scatter.14.cloned.1.call-start = ((), (), s32[]{:S(2)}) async-start(), calls=%async_computation.17 | async-start | bytes 7077888 | tf_op jit(solution)/shard_map/reduce_scatter | solution.py:1035
  695.3 107.4 %copy-start.22 = (f32[2048]{0:T(1024)S(1)}, f32[2048]{0:T(1024)}, u32[]{:S(2)}) copy-start(f32[2048]{0:T(1024)} %param.24) | copy-start | bytes 24580
  695.3 107.4 %copy-start.26 = (f32[1024]{0:T(1024)S(1)}, f32[1024]{0:T(1024)}, u32[]{:S(2)}) copy-start(f32[1024]{0:T(1024)} %copy-done.25) | copy-start | bytes 12292
  802.7 7.4 copy-start.30
  802.7 47.1 %copy-start.28 = (f32[1,2,4,128]{3,1,2,0:T(2,128)S(1)}, f32[1,2,4,128]{3,1,2,0:T(2,128)}, u32[]{:S(2)}) copy-start(f32[1,2,4,128]{3,1,2,0:T(2,128)} %copy-done.27) | copy-start | bytes 12292
  (22 other events, 35.3 us)
Sparse Core Ops, SparseCore 0:
  10.5 39.4 all-gather.7
  51.8 27.8 all-gather.13
  81.6 60.3 all-gather.9
  143.8 55.7 all-gather.11
  201.3 45.5 all-gather.15
  602.7 42.5 reduce-scatter.7
  647.7 154.9 all-reduce.6
  806.1 50.4 reduce-scatter.5
  860.3 61.7 reduce-scatter.11
  925.3 61.7 reduce-scatter.9
  990.9 61.7 reduce-scatter.13

commit v2 on v1

--- a/solution.py
+++ b/solution.py
@@ -525,15 +525,17 @@
             device_id_type=MESH,
         )
 
-    def greet(self):
+    def greet(self, peers):
         barrier = pltpu.get_barrier_semaphore()
+        for peer in peers:
+            pl.semaphore_signal(barrier, inc=1, device_id={"wide": peer}, device_id_type=MESH)
 
         @pl.when(self.is_end)
         def _():
             pl.semaphore_signal(
                 barrier, inc=1, device_id={"narrow": self.inner}, device_id_type=MESH
             )
-            pl.semaphore_wait(barrier, 1)
+            pl.semaphore_wait(barrier, 1 + len(peers))
 
         @pl.when(self.is_mid)
         def _():
@@ -543,7 +545,7 @@
             pl.semaphore_signal(
                 barrier, inc=1, device_id={"narrow": self.other}, device_id_type=MESH
             )
-            pl.semaphore_wait(barrier, 2)
+            pl.semaphore_wait(barrier, 2 + len(peers))
 
     def send(self, first, number):
         @pl.when(self.is_end)
@@ -574,14 +576,357 @@
         def _():
             self.to_outer(k - 4).wait_recv()
 
-    def drain(self):
+    def drain(self, first):
+        @pl.loop(first, self.count)
+        def _(k):
+            self.to_inner(k).wait_send()
+
         @pl.loop(0, self.count)
         def _(k):
-            self.to_inner(k).wait_send()
-
             @pl.when(self.is_mid)
             def _():
                 self.to_outer(k).wait_send()
+
+
+def wide_peers(width):
+    spot = lax.axis_index("wide")
+    return [lax.rem(spot + step, width) for step in range(1, width)]
+
+
+def greet_wide(width):
+    barrier = pltpu.get_barrier_semaphore()
+    for peer in wide_peers(width):
+        pl.semaphore_signal(barrier, inc=1, device_id={"wide": peer}, device_id_type=MESH)
+    pl.semaphore_wait(barrier, width - 1)
+
+
+class Exchange:
+    def __init__(self, block, slot, send_sem, land_sem):
+        self.block, self.slot = block, slot
+        self.send_sem, self.land_sem = send_sem, land_sem
+        self.spot = lax.axis_index("wide")
+
+    def remote(self, target, source):
+        return pltpu.make_async_remote_copy(
+            src_ref=self.block(target),
+            dst_ref=self.slot(source),
+            send_sem=self.send_sem.at[target],
+            recv_sem=self.land_sem.at[source],
+            device_id={"wide": target},
+            device_id_type=MESH,
+        )
+
+    def here(self):
+        return pltpu.make_async_copy(
+            self.block(self.spot), self.slot(self.spot), self.land_sem.at[self.spot]
+        )
+
+    def send(self, target):
+        @pl.when(target == self.spot)
+        def _():
+            self.here().start()
+
+        @pl.when(target != self.spot)
+        def _():
+            self.remote(target, self.spot).start()
+
+    def sent(self, target, home=False):
+        @pl.when(target != self.spot)
+        def _():
+            self.remote(target, self.spot).wait_send()
+
+        if home:
+
+            @pl.when(target == self.spot)
+            def _():
+                self.here().wait()
+
+    def wait(self, source, home=True):
+        if home:
+
+            @pl.when(source == self.spot)
+            def _():
+                self.here().wait()
+
+        @pl.when(source != self.spot)
+        def _():
+            self.remote(self.spot, source).wait_recv()
+
+
+def project_kernel(
+    input_ref,
+    gain_ref,
+    weight_ref,
+    cosine_ref,
+    sine_ref,
+    head_gain_ref,
+    hidden_out,
+    raw_out,
+    packed_out,
+    rows_v,
+    weight_v,
+    hidden_v,
+    raw_v,
+    pack_v,
+    load_sem,
+    keep_sem,
+    send_sem,
+    land_sem,
+):
+    micro, tok, model = input_ref.shape
+    width = packed_out.shape[0]
+    groups = width // micro
+    heads = 2 * groups
+    spot = lax.axis_index("wide")
+    swap = Exchange(
+        lambda target: pack_v.at[target], lambda source: packed_out.at[source], send_sem, land_sem
+    )
+    loads = [
+        pltpu.make_async_copy(input_ref, rows_v, load_sem.at[0]),
+        pltpu.make_async_copy(weight_ref, weight_v, load_sem.at[1]),
+    ]
+    for copy in loads:
+        copy.start()
+    greet_wide(width)
+    for copy in loads:
+        copy.wait()
+
+    def keeps(step, m):
+        return [
+            pltpu.make_async_copy(hidden_v.at[step % 2], hidden_out.at[m], keep_sem.at[step % 2, 0]),
+            pltpu.make_async_copy(raw_v.at[step % 2], raw_out.at[m], keep_sem.at[step % 2, 1]),
+        ]
+
+    kept = []
+    for step in range(micro):
+        far = micro - 1 - step
+        own = spot // groups
+        if micro == 4:
+            m = lax.rem(own + far % 2, 2) + 2 * lax.rem(own // 2 + far // 2, 2)
+        else:
+            m = lax.rem(own + far, micro)
+        if step >= 2:
+            for copy in kept[step - 2]:
+                copy.wait()
+        rows = rows_v[m].astype(jnp.float32)
+        scale = lax.rsqrt(jnp.mean(rows * rows, axis=-1, keepdims=True) + EPSILON)
+        hidden_v[step % 2] = (rows * scale * gain_ref[...]).astype(jnp.bfloat16)
+        heads_all = dot_f32(hidden_v[step % 2], weight_v[...])
+        span = pl.ds(pl.multiple_of(m * tok, tok), tok)
+        cosine, sine = cosine_ref[span, :], sine_ref[span, :]
+        raw_v[step % 2] = heads_all[:, : (heads + groups) * HD]
+        for h in range(heads + groups):
+            raw = heads_all[:, h * HD : (h + 1) * HD]
+            gain = head_gain_ref[0:1, :] if h < heads else head_gain_ref[1:2, :]
+            unit = raw * lax.rsqrt(jnp.mean(raw * raw, axis=-1, keepdims=True) + EPSILON) * gain
+            turned = unit * cosine + pltpu.roll(unit, HD // 2, 1) * sine
+            g, place = (h // 2, h % 2) if h < heads else (h - heads, 2)
+            pack_v[m * groups + g, :, place * HD : (place + 1) * HD] = turned.astype(jnp.bfloat16)
+        for g in range(groups):
+            first = (heads + groups + g) * HD
+            pack_v[m * groups + g, :, 3 * HD :] = heads_all[:, first : first + HD].astype(
+                jnp.bfloat16
+            )
+            swap.send(m * groups + g)
+        kept.append(keeps(step, m))
+        for copy in kept[step]:
+            copy.start()
+    for copy in kept[micro - 2] + kept[micro - 1]:
+        copy.wait()
+
+    @pl.loop(0, width)
+    def _(d):
+        swap.sent(d)
+        swap.wait(d)
+
+
+def project(layer_input, gain_attn, weight, cosine, sine, head_gains, width):
+    micro, tok, model = layer_input.shape
+    groups = width // micro
+    low = jnp.bfloat16
+    anywhere = pl.BlockSpec(memory_space=pl.ANY)
+    inside = pl.BlockSpec(memory_space=pltpu.VMEM)
+    raw = 3 * groups * HD
+    return pl.pallas_call(
+        project_kernel,
+        out_shape=(
+            jax.ShapeDtypeStruct((micro, tok, model), low),
+            jax.ShapeDtypeStruct((micro, tok, raw), jnp.float32),
+            jax.ShapeDtypeStruct((width, tok, 4 * HD), low),
+        ),
+        in_specs=[anywhere, inside, anywhere, inside, inside, inside],
+        out_specs=[anywhere] * 3,
+        scratch_shapes=[
+            pltpu.VMEM((micro, tok, model), low),
+            pltpu.VMEM(weight.shape, low),
+            pltpu.VMEM((2, tok, model), low),
+            pltpu.VMEM((2, tok, raw), jnp.float32),
+            pltpu.VMEM((width, tok, 4 * HD), low),
+            pltpu.SemaphoreType.DMA((2,)),
+            pltpu.SemaphoreType.DMA((2, 2)),
+            pltpu.SemaphoreType.DMA((width,)),
+            pltpu.SemaphoreType.DMA((width,)),
+        ],
+        compiler_params=pltpu.CompilerParams(
+            collective_id=2, has_side_effects=True, vmem_limit_bytes=40 << 20
+        ),
+        cost_estimate=pl.CostEstimate(
+            flops=20_000_000_000, bytes_accessed=40_000_000, transcendentals=0
+        ),
+        name="project",
+    )(layer_input, gain_attn[None, :], weight, cosine, sine, head_gains)
+
+
+def weights_kernel(
+    back_ref,
+    raw_ref,
+    hidden_ref,
+    mixed_ref,
+    low_ref,
+    cosine_ref,
+    sine_ref,
+    head_gain_ref,
+    back_out,
+    grad_out,
+    gain_out,
+    land_v,
+    raw_v,
+    hidden_v,
+    mixed_v,
+    low_v,
+    back_v,
+    grad_v,
+    load_sem,
+    back_sem,
+    tile_sem,
+    send_sem,
+    land_sem,
+):
+    micro, tok, heads_in = mixed_ref.shape
+    width = back_ref.shape[0]
+    groups = width // micro
+    heads = 2 * groups
+    model = hidden_ref.shape[2]
+    piece = model // width
+    count = micro * tok
+    swap = Exchange(
+        lambda target: back_ref.at[target], lambda source: land_v.at[source], send_sem, land_sem
+    )
+    loads = [
+        pltpu.make_async_copy(mixed_ref, mixed_v, load_sem.at[0]),
+        pltpu.make_async_copy(low_ref, low_v, load_sem.at[1]),
+        pltpu.make_async_copy(raw_ref, raw_v, load_sem.at[2]),
+        pltpu.make_async_copy(hidden_ref, hidden_v, load_sem.at[3]),
+    ]
+    for copy in loads:
+        copy.start()
+    greet_wide(width)
+    spot = lax.axis_index("wide")
+    for step in range(width - 1, -1, -1):
+        swap.send(lax.rem(spot + step, width))
+    loads[0].wait()
+    loads[1].wait()
+    mixed_all = mixed_v[...].reshape(count, heads_in)
+    for n in range(model // LANES):
+        low = low_v[:, :, n * LANES : (n + 1) * LANES].reshape(count, LANES)
+        part = dot_f32(mixed_all, low, TN).astype(jnp.bfloat16)
+        for i in range(LANES // piece):
+            for b in range(heads_in // piece):
+                grad_v[
+                    n * (LANES // piece) + i, :, pl.ds(2 * heads_in + b * piece, piece)
+                ] = part[b * piece : (b + 1) * piece, i * piece : (i + 1) * piece]
+    loads[2].wait()
+    gain_out[...] = jnp.zeros_like(gain_out)
+
+    @pl.loop(0, width)
+    def _(d):
+        swap.wait(d)
+
+    def back_copy(m):
+        return pltpu.make_async_copy(back_v.at[m], back_out.at[m], back_sem.at[m])
+
+    @pl.loop(0, micro)
+    def _(m):
+        span = pl.ds(pl.multiple_of(m * tok, tok), tok)
+        cosine, sine = cosine_ref[span, :], sine_ref[span, :]
+        for h in range(heads + groups):
+            raw = raw_v[m, :, h * HD : (h + 1) * HD]
+            kind = 0 if h < heads else 1
+            gain = head_gain_ref[kind : kind + 1, :]
+            g, place = (h // 2, h % 2) if h < heads else (h - heads, 2)
+            grad = land_v[m * groups + g, :, place * HD : (place + 1) * HD].astype(jnp.float32)
+            straight = grad * cosine + pltpu.roll(grad * sine, HD // 2, 1)
+            scale = lax.rsqrt(jnp.mean(raw * raw, axis=-1, keepdims=True) + EPSILON)
+            gain_out[kind : kind + 1, :] += jnp.sum(straight * (raw * scale), axis=0, keepdims=True)
+            pulled = straight * gain
+            along = jnp.mean(pulled * raw, axis=-1, keepdims=True)
+            back_v[m, :, h * HD : (h + 1) * HD] = (
+                scale * (pulled - raw * (scale * scale * along))
+            ).astype(jnp.bfloat16)
+        for g in range(groups):
+            first = (heads + groups + g) * HD
+            back_v[m, :, first : first + HD] = land_v[m * groups + g, :, 3 * HD :]
+        back_copy(m).start()
+
+    loads[3].wait()
+
+    def tile_copy(i):
+        return pltpu.make_async_copy(grad_v.at[i], grad_out.at[i], tile_sem.at[i])
+
+    @pl.loop(0, width)
+    def _(i):
+        left = hidden_v[:, :, pl.ds(pl.multiple_of(i * piece, piece), piece)].reshape(count, piece)
+        right = back_v[...].reshape(count, 2 * heads_in)
+        grad_v[i, :, 0 : 2 * heads_in] = dot_f32(left, right, TN).astype(jnp.bfloat16)
+        tile_copy(i).start()
+
+    @pl.loop(0, width)
+    def _(i):
+        tile_copy(i).wait()
+        swap.sent(i)
+
+    for m in range(micro):
+        back_copy(m).wait()
+
+
+def weight_gradients(back, raw, hidden, mixed, middle_low, cosine, sine, head_gains):
+    micro, tok, heads_in = mixed.shape
+    width = back.shape[0]
+    model = hidden.shape[2]
+    low = jnp.bfloat16
+    anywhere = pl.BlockSpec(memory_space=pl.ANY)
+    inside = pl.BlockSpec(memory_space=pltpu.VMEM)
+    return pl.pallas_call(
+        weights_kernel,
+        out_shape=(
+            jax.ShapeDtypeStruct((micro, tok, 2 * heads_in), low),
+            jax.ShapeDtypeStruct((width, model // width, 3 * heads_in), low),
+            jax.ShapeDtypeStruct((2, HD), jnp.float32),
+        ),
+        in_specs=[anywhere] * 5 + [inside] * 3,
+        out_specs=[anywhere, anywhere, inside],
+        scratch_shapes=[
+            pltpu.VMEM(back.shape, low),
+            pltpu.VMEM(raw.shape, jnp.float32),
+            pltpu.VMEM(hidden.shape, low),
+            pltpu.VMEM(mixed.shape, low),
+            pltpu.VMEM(middle_low.shape, low),
+            pltpu.VMEM((micro, tok, 2 * heads_in), low),
+            pltpu.VMEM((width, model // width, 3 * heads_in), low),
+            pltpu.SemaphoreType.DMA((4,)),
+            pltpu.SemaphoreType.DMA((micro,)),
+            pltpu.SemaphoreType.DMA((width,)),
+            pltpu.SemaphoreType.DMA((width,)),
+            pltpu.SemaphoreType.DMA((width,)),
+        ],
+        compiler_params=pltpu.CompilerParams(
+            collective_id=3, has_side_effects=True, vmem_limit_bytes=48 << 20
+        ),
+        cost_estimate=pl.CostEstimate(
+            flops=1_000_000_000, bytes_accessed=1_000_000, transcendentals=0
+        ),
+        name="weight_gradients",
+    )(back, raw, hidden, mixed, middle_low, cosine, sine, head_gains)
 
 
 def relay_scratch(count, model):
@@ -601,10 +946,7 @@
     input_ref,
     grad_ref,
     gain_ref,
-    out_w,
-    gate_w,
-    up_w,
-    down_w,
+    pack_ref,
     hidden_out,
     active_out,
     gate_out,
@@ -614,6 +956,8 @@
     low_out,
     mixed_out,
     gain_out,
+    weight_out,
+    heads_out,
     own,
     landed,
     cross,
@@ -640,37 +984,65 @@
     hidden_sem,
     stage_sem,
     final_sem,
+    reload_sem,
+    tile_sem,
+    ahead_sems,
+    behind_sems,
+    heads_sem,
 ):
     micro, tok, model = input_ref.shape
-    width = out_w.shape[0]
-    piece = out_w.shape[2]
+    width, _, piece = pack_ref.shape
+    heads_in = out_v.shape[0]
     groups = width // micro
     per = tok // SUB
-    hid = gate_w.shape[1]
+    hid = gate_v.shape[1]
+    count = micro * tok
+    blocks = hid // piece
     relay = Relay(3 * micro * per, own, landed, cross, (out_sem, land_sem, back_sem, cross_sem))
     n_up = hid // LANES
     n_down = model // LANES
     slots = n_up + n_down
 
+    ahead = Exchange(
+        lambda target: mixed_ref.at[target],
+        lambda source: mixed_v.at[
+            source // groups, :, pl.ds(pl.multiple_of((source % groups) * 2 * HD, 2 * HD), 2 * HD)
+        ],
+        ahead_sems.at[0],
+        ahead_sems.at[1],
+    )
+    behind = Exchange(
+        lambda target: mixback_v.at[
+            target // groups % 2,
+            :,
+            pl.ds(pl.multiple_of((target % groups) * 2 * HD, 2 * HD), 2 * HD),
+        ],
+        lambda source: mixed_out.at[source],
+        behind_sems.at[0],
+        behind_sems.at[1],
+    )
     attn_copies = [
         pltpu.make_async_copy(
-            mixed_ref.at[i],
-            mixed_v.at[i // groups, :, pl.ds((i % groups) * 2 * HD, 2 * HD)],
+            pack_ref.at[i, pl.ds(0, heads_in)],
+            out_v.at[:, pl.ds(i * piece, piece)],
             attn_sem.at[i],
-        )
-        for i in range(width)
-    ] + [
-        pltpu.make_async_copy(
-            out_w.at[i], out_v.at[:, pl.ds(i * piece, piece)], attn_sem.at[width + i]
         )
         for i in range(width)
     ]
     weight_copies = [
-        pltpu.make_async_copy(gate_w, gate_v, weight_sem.at[0]),
-        pltpu.make_async_copy(up_w, up_v, weight_sem.at[1]),
+        pltpu.make_async_copy(
+            pack_ref.at[i, pl.ds(heads_in + (1 + q) * hid + j * piece, piece)],
+            target.at[pl.ds(i * piece, piece), pl.ds(j * piece, piece)],
+            weight_sem.at[1 + q, i, j],
+        )
+        for q, target in enumerate((gate_v, up_v))
+        for i in range(width)
+        for j in range(blocks)
     ] + [
         pltpu.make_async_copy(
-            down_w.at[i], down_v.at[:, pl.ds(i * piece, piece)], weight_sem.at[2 + i]
+            pack_ref.at[i, pl.ds(heads_in, hid)],
+            down_v.at[:, pl.ds(i * piece, piece)],
+            weight_sem.at[0, i, 0],
         )
         for i in range(width)
     ]
@@ -694,12 +1066,21 @@
 
     start_loads(0)
     gain_out[...] = jnp.zeros_like(gain_out)
-    relay.greet()
+    relay.greet(wide_peers(width))
+    spot = lax.axis_index("wide")
+    for step in range(width):
+        ahead.send(lax.rem(spot + step, width))
     for copy in attn_copies:
         copy.wait()
 
+    def heads_copy(m):
+        return pltpu.make_async_copy(mixed_v.at[m], heads_out.at[m], heads_sem.at[m])
+
     @pl.loop(0, micro)
     def _(m):
+        for g in range(groups):
+            ahead.wait(m * groups + g)
+        heads_copy(m).start()
         for n in range(n_down):
             cols = pl.ds(n * LANES, LANES)
             part = dot_f32(mixed_v[m], out_v[:, cols]).astype(jnp.bfloat16)
@@ -787,18 +1168,55 @@
     for copy in stage_copies(micro - 1):
         copy.wait()
 
+    @pl.loop(0, base)
+    def _(k):
+        relay.to_inner(k).wait_send()
+
+    def reloads(m):
+        rows = pl.ds(m * tok, tok)
+        return [
+            pltpu.make_async_copy(hidden_out.at[m], down_v.at[rows], reload_sem.at[m, 0]),
+            pltpu.make_async_copy(gate_out.at[m], gate_v.at[rows], reload_sem.at[m, 1]),
+            pltpu.make_async_copy(
+                upper_out.at[m], gate_v.at[pl.ds(count + m * tok, tok)], reload_sem.at[m, 2]
+            ),
+            pltpu.make_async_copy(active_out.at[m], up_v.at[rows], reload_sem.at[m, 3]),
+        ] + [
+            pltpu.make_async_copy(
+                grad_ref.at[m, pl.ds(r * SUB, SUB)], own.at[m * per + r], reload_sem.at[m, 4 + r]
+            )
+            for r in range(per)
+        ]
+
+    for m in range(micro):
+        for copy in reloads(m):
+            copy.start()
+
+    def tile_copy(i, q):
+        return pltpu.make_async_copy(stage_v.at[q], weight_out.at[i, q], tile_sem.at[q])
+
+    def tile(i, q):
+        cols = pl.ds(pl.multiple_of(i * piece, piece), piece)
+
+        @pl.when(i > 0)
+        def _():
+            tile_copy(i - 1, q).wait()
+
+        if q == 2:
+            right = own[0:base, :, cols].reshape(count, piece)
+            for j in range(blocks):
+                span = slice(j * piece, (j + 1) * piece)
+                stage_v[q, :, span] = dot_f32(up_v[0:count, span], right, TN).astype(jnp.bfloat16)
+        else:
+            right = (gate_v[0:count], gate_v[count : 2 * count])[q]
+            stage_v[q] = dot_f32(down_v[0:count, cols], right, TN).astype(jnp.bfloat16)
+        tile_copy(i, q).start()
+
     def final_copies(m):
         return [
             pltpu.make_async_copy(middle_v, middle_out.at[m], final_sem.at[0]),
             pltpu.make_async_copy(hidden_v, low_out.at[m], final_sem.at[1]),
             pltpu.make_async_copy(output_v, output_out.at[m], final_sem.at[2]),
-        ] + [
-            pltpu.make_async_copy(
-                mixback_v.at[:, pl.ds(g * 2 * HD, 2 * HD)],
-                mixed_out.at[m * groups + g],
-                final_sem.at[3 + g],
-            )
-            for g in range(groups)
         ]
 
     last_ticks = first_ticks + slots * micro
@@ -819,8 +1237,16 @@
             for copy in final_copies(m - 1):
                 copy.wait()
 
-        for t in range(turns // 2):
-            relay.tick(last_ticks + turns * m + t)
+        @pl.when(m == 0)
+        def _():
+            for i in range(micro):
+                for copy in reloads(i):
+                    copy.wait()
+
+        relay.tick(last_ticks + turns * m)
+        tile(2 * m, 0)
+        tile(2 * m, 1)
+        relay.tick(last_ticks + turns * m + 1)
         for r in range(per):
             span = pl.ds(r * SUB, SUB)
             middle = rows_v[slot, span, :].astype(jnp.float32) + landed[m * per + r].astype(
@@ -834,9 +1260,20 @@
             )
             middle_v[span, :] = grad_middle
             hidden_v[span, :] = grad_middle.astype(jnp.bfloat16)
-        mixback_v[...] = dot_f32(hidden_v[...], out_v[...], NT).astype(jnp.bfloat16)
-        for t in range(turns // 2, turns):
-            relay.tick(last_ticks + turns * m + t)
+        @pl.when(m >= 2)
+        def _():
+            for g in range(groups):
+                behind.sent((m - 2) * groups + g, home=True)
+
+        mixback_v[m % 2] = dot_f32(hidden_v[...], out_v[...], NT).astype(jnp.bfloat16)
+        for g in range(groups):
+            behind.send(m * groups + g)
+        tile(2 * m, 2)
+        relay.tick(last_ticks + turns * m + 2)
+        tile(2 * m + 1, 0)
+        tile(2 * m + 1, 1)
+        relay.tick(last_ticks + turns * m + 3)
+        tile(2 * m + 1, 2)
         for r in range(per):
             span = pl.ds(r * SUB, SUB)
             output_v[span, :] = (
@@ -847,15 +1284,26 @@
         for copy in final_copies(m):
             copy.start()
 
-    for copy in final_copies(micro - 1):
+    for copy in final_copies(micro - 1) + [tile_copy(width - 1, q) for q in range(3)]:
         copy.wait()
-    relay.drain()
-
-
-def feed_forward(mixed, layer_input, grad_out, gain_ffn, out_w, gate_w, up_w, down_w):
+    for m in range(micro):
+        heads_copy(m).wait()
+
+    @pl.loop(0, width)
+    def _(d):
+        ahead.sent(d)
+        behind.wait(d, home=False)
+
+    @pl.loop((micro - 2) * groups, width)
+    def _(d):
+        behind.sent(d, home=True)
+
+    relay.drain(base)
+
+
+def feed_forward(mixed, layer_input, grad_out, gain_ffn, pack, heads_in, hid):
     micro, tok, model = layer_input.shape
-    width, heads_in, piece = out_w.shape
-    hid = gate_w.shape[1]
+    width, _, piece = pack.shape
     groups = width // micro
     low = jnp.bfloat16
     count = 3 * micro * (tok // SUB)
@@ -873,9 +1321,11 @@
             jax.ShapeDtypeStruct((micro, tok, model), low),
             jax.ShapeDtypeStruct((width, tok, 2 * HD), low),
             jax.ShapeDtypeStruct((1, model), jnp.float32),
+            jax.ShapeDtypeStruct((width, 3, piece, hid), low),
+            jax.ShapeDtypeStruct((micro, tok, heads_in), low),
         ),
-        in_specs=[anywhere] * 3 + [inside] + [anywhere] * 4,
-        out_specs=[anywhere] * 8 + [inside],
+        in_specs=[anywhere] * 3 + [inside, anywhere],
+        out_specs=[anywhere] * 8 + [inside, anywhere, anywhere],
         scratch_shapes=relay_scratch(count, model)
         + [
             pltpu.VMEM((heads_in, model), low),
@@ -890,22 +1340,264 @@
             pltpu.VMEM((tok, 1), jnp.float32),
             pltpu.VMEM((tok, model), jnp.float32),
             pltpu.VMEM((tok, model), low),
-            pltpu.VMEM((tok, heads_in), low),
-            pltpu.SemaphoreType.DMA((2 + width,)),
-            pltpu.SemaphoreType.DMA((2 * width,)),
+            pltpu.VMEM((2, tok, heads_in), low),
+            pltpu.SemaphoreType.DMA((3, width, hid // piece)),
+            pltpu.SemaphoreType.DMA((width,)),
             pltpu.SemaphoreType.DMA((2, 2)),
             pltpu.SemaphoreType.DMA,
             pltpu.SemaphoreType.DMA((3,)),
-            pltpu.SemaphoreType.DMA((3 + groups,)),
+            pltpu.SemaphoreType.DMA((3,)),
+            pltpu.SemaphoreType.DMA((micro, 4 + tok // SUB)),
+            pltpu.SemaphoreType.DMA((3,)),
+            pltpu.SemaphoreType.DMA((2, width)),
+            pltpu.SemaphoreType.DMA((2, width)),
+            pltpu.SemaphoreType.DMA((micro,)),
         ],
         compiler_params=pltpu.CompilerParams(
             collective_id=0, has_side_effects=True, vmem_limit_bytes=67043328
         ),
         cost_estimate=pl.CostEstimate(
-            flops=200_000_000_000, bytes_accessed=900_000_000, transcendentals=0
+            flops=240_000_000_000, bytes_accessed=900_000_000, transcendentals=0
         ),
         name="feed_forward",
-    )(mixed, layer_input, grad_out, gain_ffn[None, :], out_w, gate_w, up_w, down_w)
+    )(mixed, layer_input, grad_out, gain_ffn[None, :], pack)
+
+
+def input_kernel(
+    back_ref,
+    input_ref,
+    middle_ref,
+    gain_ref,
+    weight_ref,
+    gain_two_ref,
+    gain_heads_ref,
+    output_out,
+    gains_out,
+    own,
+    landed,
+    cross,
+    out_sem,
+    land_sem,
+    back_sem,
+    cross_sem,
+    weight_v,
+    back_v,
+    rows_v,
+    middle_v,
+    output_v,
+    term_v,
+    other_v,
+    first_sem,
+    load_sem,
+    final_sem,
+    term_sem,
+    other_sem,
+):
+    micro, tok, model = input_ref.shape
+    per = tok // SUB
+    spot = lax.axis_index("wide")
+    flips = [spot + bit - 2 * bit * (spot // bit % 2) for bit in (1, 2, 4)]
+    relay = Relay(micro * per, own, landed, cross, (out_sem, land_sem, back_sem, cross_sem))
+    weight_copy = pltpu.make_async_copy(weight_ref, weight_v, first_sem.at[0])
+    back_copy = pltpu.make_async_copy(back_ref, back_v, first_sem.at[1])
+    weight_copy.start()
+    back_copy.start()
+
+    rows_copy = pltpu.make_async_copy(input_ref, rows_v, first_sem.at[2])
+    rows_copy.start()
+
+    def load(m):
+        return pltpu.make_async_copy(middle_ref.at[m], middle_v.at[m % 2], load_sem.at[m % 2])
+
+    def final_copy(m):
+        return pltpu.make_async_copy(output_v.at[m % 2], output_out.at[m], final_sem.at[m % 2])
+
+    def pass_on(step, where):
+        return pltpu.make_async_remote_copy(
+            src_ref=term_v.at[step],
+            dst_ref=other_v.at[step],
+            send_sem=term_sem.at[step],
+            recv_sem=other_sem.at[step],
+            device_id=where,
+            device_id_type=MESH,
+        )
+
+    targets = [{"wide": flip} for flip in flips] + [
+        {"narrow": spot} for spot in (relay.inner, relay.other, relay.outer)
+    ]
+
+    def gain_step(step):
+        if step == 0:
+            pass_on(0, targets[0]).start()
+        if 1 <= step <= 3:
+            pass_on(step - 1, targets[step - 1]).wait_recv()
+            term_v[step] = term_v[step - 1] + other_v[step - 1]
+        if step in (1, 2):
+            pass_on(step, targets[step]).start()
+        if step == 3:
+
+            @pl.when(relay.is_end)
+            def _():
+                pass_on(3, targets[3]).start()
+
+        if step in (4, 5):
+
+            @pl.when(relay.is_mid)
+            def _():
+                pass_on(step - 1, targets[step - 1]).wait_recv()
+                term_v[step] = term_v[step - 1] + other_v[step - 1]
+                pass_on(step, targets[step]).start()
+
+        if step == 6:
+
+            @pl.when(relay.is_mid)
+            def _():
+                gains_out[...] = term_v[5]
+                pass_on(4, targets[4]).wait_send()
+                pass_on(5, targets[5]).wait_send()
+
+            @pl.when(relay.is_end)
+            def _():
+                pass_on(5, targets[5]).wait_recv()
+                gains_out[...] = other_v[5]
+                pass_on(3, targets[3]).wait_send()
+
+            for early in range(3):
+                pass_on(early, targets[early]).wait_send()
+
+    load(0).start()
+    relay.greet(flips)
+    term_v[0] = jnp.zeros(term_v.shape[1:], jnp.float32)
+    weight_copy.wait()
+    back_copy.wait()
+    rows_copy.wait()
+
+    @pl.loop(0, micro)
+    def _(m):
+        rows = rows_v[m].astype(jnp.float32)
+        scale = lax.rsqrt(jnp.mean(rows * rows, axis=-1, keepdims=True) + EPSILON)
+        for n in range(model // LANES):
+            cols = pl.ds(n * LANES, LANES)
+            part = dot_f32(back_v[m], weight_v[cols, :], NT)
+            term_v[0, 0:1, cols] += jnp.sum(
+                part * (rows_v[m, :, cols].astype(jnp.float32) * scale), axis=0, keepdims=True
+            )
+            part = part.astype(jnp.bfloat16)
+            for r in range(per):
+                own[m * per + r, :, cols] = part[r * SUB : (r + 1) * SUB]
+        relay.send(m * per, per)
+
+    term_v[0, 1:2, :] = gain_two_ref[...]
+    term_v[0, 2:3, 0:HD] = gain_heads_ref[0:1, :]
+    term_v[0, 2:3, HD : 2 * HD] = gain_heads_ref[1:2, :]
+    for k in range(4):
+        if k % 3 == 0:
+            gain_step(k // 3)
+        relay.tick(k)
+
+    @pl.loop(0, micro)
+    def _(m):
+        slot = m % 2
+
+        @pl.when(m < micro - 1)
+        def _():
+            load(m + 1).start()
+
+        load(m).wait()
+
+        @pl.when(m >= 2)
+        def _():
+            final_copy(m - 2).wait()
+
+        for r in range(per):
+            for turn in range(micro):
+                if (4 + turn * per + r) % 3 == 0:
+
+                    @pl.when(m == turn)
+                    def _(step=(4 + turn * per + r) // 3):
+                        gain_step(step)
+
+            relay.tick(4 + m * per + r)
+            span = pl.ds(r * SUB, SUB)
+            rows = rows_v[m, span, :].astype(jnp.float32)
+            scale = lax.rsqrt(jnp.mean(rows * rows, axis=-1, keepdims=True) + EPSILON)
+            pulled = landed[m * per + r].astype(jnp.float32) * gain_ref[...]
+            along = jnp.mean(pulled * rows, axis=-1, keepdims=True)
+            output_v[slot, span, :] = middle_v[slot, span, :] + scale * (
+                pulled - rows * (scale * scale * along)
+            )
+        final_copy(m).start()
+
+    final_copy(micro - 2).wait()
+    final_copy(micro - 1).wait()
+    relay.drain(0)
+
+
+def input_gradient(back, layer_input, grad_middle, gain_attn, weight, gain_two, gain_heads):
+    micro, tok, model = layer_input.shape
+    low = jnp.bfloat16
+    count = micro * (tok // SUB)
+    anywhere = pl.BlockSpec(memory_space=pl.ANY)
+    inside = pl.BlockSpec(memory_space=pltpu.VMEM)
+    return pl.pallas_call(
+        input_kernel,
+        out_shape=(
+            jax.ShapeDtypeStruct((micro, tok, model), jnp.float32),
+            jax.ShapeDtypeStruct((8, model), jnp.float32),
+        ),
+        in_specs=[anywhere] * 3 + [inside, anywhere, inside, inside],
+        out_specs=[anywhere, inside],
+        scratch_shapes=relay_scratch(count, model)
+        + [
+            pltpu.VMEM(weight.shape, low),
+            pltpu.VMEM((micro, tok, weight.shape[1]), low),
+            pltpu.VMEM((micro, tok, model), low),
+            pltpu.VMEM((2, tok, model), jnp.float32),
+            pltpu.VMEM((2, tok, model), jnp.float32),
+            pltpu.VMEM((6, 8, model), jnp.float32),
+            pltpu.VMEM((6, 8, model), jnp.float32),
+            pltpu.SemaphoreType.DMA((3,)),
+            pltpu.SemaphoreType.DMA((2,)),
+            pltpu.SemaphoreType.DMA((2,)),
+            pltpu.SemaphoreType.DMA((6,)),
+            pltpu.SemaphoreType.DMA((6,)),
+        ],
+        compiler_params=pltpu.CompilerParams(
+            collective_id=1, has_side_effects=True, vmem_limit_bytes=48 << 20
+        ),
+        cost_estimate=pl.CostEstimate(
+            flops=1_000_000_000, bytes_accessed=1_000_000, transcendentals=0
+        ),
+        name="input_gradient",
+    )(back, layer_input, grad_middle, gain_attn[None, :], weight, gain_two, gain_heads)
+
+
+def widen_feed(rows_ref, gate_ref, up_ref, down_ref):
+    piece = gate_ref.shape[0]
+    gate_ref[...] = rows_ref[0:piece, :].astype(jnp.float32)
+    up_ref[...] = rows_ref[piece : 2 * piece, :].astype(jnp.float32)
+    for j in range(down_ref.shape[0] // piece):
+        span = slice(j * piece, (j + 1) * piece)
+        down_ref[span, :] = rows_ref[2 * piece :, span].astype(jnp.float32)
+
+
+def widen_attn(rows_ref, query_ref, key_ref, value_ref, out_ref):
+    piece = query_ref.shape[0]
+    first = 0
+    for target in (query_ref, key_ref, value_ref):
+        target[...] = rows_ref[:, first : first + target.shape[1]].astype(jnp.float32)
+        first += target.shape[1]
+    for j in range(out_ref.shape[0] // piece):
+        part = rows_ref[:, first + j * piece : first + (j + 1) * piece]
+        out_ref[j * piece : (j + 1) * piece, :] = part.astype(jnp.float32)
+
+
+def widen(kernel, rows, shapes):
+    return pl.pallas_call(
+        kernel,
+        out_shape=tuple(jax.ShapeDtypeStruct(shape, jnp.float32) for shape in shapes),
+        name=kernel.__name__,
+    )(rows)
 
 
 def local_batched(
@@ -933,124 +1625,95 @@
     w_qkv = lax.all_gather(
         jnp.concatenate([w_query, w_key, w_value], axis=1), "wide", axis=0, tiled=True
     )
-    w_out_all = lax.all_gather(w_out, "wide", axis=0)
-    w_gate_full = lax.all_gather(w_gate, "wide", axis=0, tiled=True)
-    w_up_full = lax.all_gather(w_up, "wide", axis=0, tiled=True)
-    w_down_all = lax.all_gather(w_down, "wide", axis=0)
+    hid = w_gate.shape[1]
+    piece = w_out.shape[1]
+
+    def stacked(weight):
+        return jnp.moveaxis(weight.reshape(piece, -1, piece), 1, 0).reshape(-1, piece)
+
+    pack = lax.all_gather(
+        jnp.concatenate([w_out, w_down, stacked(w_gate), stacked(w_up)], axis=0), "wide", axis=0
+    )
+
     starts, places = jax.vmap(lambda row: row_starts(row, total))(lengths)
     my_places = lax.dynamic_slice_in_dim(places, me * tok_rows, tok_rows, axis=1)
-    cosine, sine = jax.vmap(angles)(my_places)
-    cosine = cosine.reshape(count, 1, HD)
-    sine = sine.reshape(count, 1, HD)
+    cosine, sine = angles(my_places.reshape(count))
+    sine = jnp.where(jnp.arange(HD) < HD // 2, -sine, sine)
+    head_gains = jnp.stack([gain_query, gain_key])
     my_starts = lax.dynamic_index_in_dim(starts, me // groups, axis=0, keepdims=False)
     my_first = my_starts[::BLOCK] // BLOCK
 
-    def head_norm(rows, gain):
-        return rotate(rms_norm(rows, gain), cosine, sine)
-
-    input_float = layer_input.reshape(count, model).astype(jnp.float32)
-    grad_rows = grad_out.reshape(count, model)
-    normed_one, pull_one = jax.vjp(lambda rows: rms_norm(rows, gain_attn), input_float)
-    hidden_one = normed_one.astype(jnp.bfloat16)
-    qkv = dot_f32(hidden_one, w_qkv)
-    q_cols = w_query.shape[1]
-    k_cols = w_key.shape[1]
-    query_turned, pull_query = jax.vjp(
-        head_norm, qkv[:, :q_cols].reshape(count, -1, HD), gain_query
-    )
-    key_turned, pull_key = jax.vjp(
-        head_norm, qkv[:, q_cols : q_cols + k_cols].reshape(count, -1, HD), gain_key
-    )
-    packed = jnp.concatenate(
-        [
-            query_turned.reshape(micro, tok_rows, groups, 2 * HD),
-            key_turned.reshape(micro, tok_rows, groups, HD),
-            qkv[:, q_cols + k_cols :].reshape(micro, tok_rows, groups, HD),
-        ],
-        axis=-1,
-    ).astype(jnp.bfloat16)
-    packed = jnp.moveaxis(packed, 2, 1).reshape(width, tok_rows, 4 * HD)
-    packed = lax.all_to_all(packed, "wide", split_axis=0, concat_axis=0).reshape(total, 4 * HD)
+    hidden_one, raw, packed = project(
+        layer_input, gain_attn, w_qkv, cosine, sine, head_gains, width
+    )
+    packed = packed.reshape(total, 4 * HD)
     mixed, kept, log_total = attention_out(packed, my_starts, my_first)
-    mixed = lax.all_to_all(
-        mixed.reshape(width, tok_rows, 2 * HD), "wide", split_axis=0, concat_axis=0
-    )
     (
-        hidden_two,
-        active_low,
-        gate_back,
-        upper_back,
+        _,
+        _,
+        _,
+        _,
         output,
         grad_middle,
         middle_low,
         grad_mixed,
         gain_two,
+        feed_grads,
+        mixed_low,
     ) = feed_forward(
-        mixed, layer_input, grad_out, gain_ffn, w_out_all, w_gate_full, w_up_full, w_down_all
-    )
-    gain_two = gain_two[0]
-    hidden_two = hidden_two.reshape(count, model)
-    active_low = active_low.reshape(count, -1)
-    gate_back = gate_back.reshape(count, -1)
-    upper_back = upper_back.reshape(count, -1)
-    grad_middle = grad_middle.reshape(count, model)
-    middle_low = middle_low.reshape(count, model)
-    mixed_low = jnp.moveaxis(
-        mixed.reshape(micro, groups, tok_rows, 2 * HD), 1, 2
-    ).reshape(count, groups * 2 * HD)
-    grad_mixed = lax.all_to_all(grad_mixed, "wide", split_axis=0, concat_axis=0)
+        mixed.reshape(width, tok_rows, 2 * HD),
+        layer_input,
+        grad_out,
+        gain_ffn,
+        pack,
+        w_out.shape[0],
+        hid,
+    )
+    feed_grads = lax.psum_scatter(
+        feed_grads.reshape(width * 3 * piece, hid), "wide", scatter_dimension=0, tiled=True
+    )
     back = attention_back(
         packed, my_starts, my_first, grad_mixed.reshape(total, 2 * HD), kept, log_total
     )
-    back = lax.all_to_all(
-        back.reshape(width, tok_rows, 4 * HD), "wide", split_axis=0, concat_axis=0
-    )
-    back = jnp.moveaxis(back.reshape(micro, groups, tok_rows, 4 * HD), 1, 2)
-    back = back.reshape(count, groups, 4 * HD)
-    grad_qraw, gain_q = pull_query(
-        back[..., : 2 * HD].reshape(count, -1, HD).astype(jnp.float32)
-    )
-    grad_kraw, gain_k = pull_key(back[..., 2 * HD : 3 * HD].astype(jnp.float32))
-    qkv_back = jnp.concatenate(
-        [
-            grad_qraw.reshape(count, -1).astype(jnp.bfloat16),
-            grad_kraw.reshape(count, -1).astype(jnp.bfloat16),
-            back[..., 3 * HD :].reshape(count, -1),
-        ],
-        axis=1,
-    )
-    partial_one = dot_f32(qkv_back, w_qkv, NT)
-    gain_one = jnp.sum(partial_one * unit_rows(input_float), axis=0)
-    grad_input = (
-        grad_middle
-        + pull_one(lax.psum(partial_one.astype(jnp.bfloat16), "narrow").astype(jnp.float32))[0]
-    )
-
-    def scatter(left, right):
-        part = dot_f32(left, right, TN).astype(jnp.bfloat16)
-        return lax.psum_scatter(part, "wide", scatter_dimension=0, tiled=True).astype(jnp.float32)
-
-    def scatter_cols(left, right):
-        part = dot_f32(left, right, TN).astype(jnp.bfloat16)
-        return lax.psum_scatter(part, "wide", scatter_dimension=1, tiled=True).astype(jnp.float32)
-
-    grad_wgate = scatter(hidden_two, gate_back)
-    grad_wup = scatter(hidden_two, upper_back)
-    grad_wdown = scatter_cols(active_low, grad_rows)
-    grad_wout = scatter_cols(mixed_low, middle_low)
-    grad_wqkv = scatter(hidden_one, qkv_back)
-    gains = lax.psum((gain_one, gain_two, gain_q, gain_k), ("wide", "narrow"))
+    qkv_back, attn_grads, gain_heads = weight_gradients(
+        back.reshape(width, tok_rows, 4 * HD),
+        raw,
+        hidden_one,
+        mixed_low,
+        middle_low,
+        cosine,
+        sine,
+        head_gains,
+    )
+    attn_grads = lax.psum_scatter(
+        attn_grads.reshape(model, -1), "wide", scatter_dimension=0, tiled=True
+    )
+    grad_input, gains = input_gradient(
+        qkv_back, layer_input, grad_middle, gain_attn, w_qkv, gain_two, gain_heads
+    )
+
+    grad_gate, grad_up, grad_down = widen(
+        widen_feed, feed_grads, (w_gate.shape, w_up.shape, w_down.shape)
+    )
+    grad_gate, attn_grads = lax.optimization_barrier((grad_gate, attn_grads))
+    grad_query, grad_key, grad_value, grad_wout = widen(
+        widen_attn, attn_grads, (w_query.shape, w_key.shape, w_value.shape, w_out.shape)
+    )
     return (
         output,
-        grad_input.reshape(micro, tok_rows, model),
-        grad_wqkv[:, :q_cols],
-        grad_wqkv[:, q_cols : q_cols + k_cols],
-        grad_wqkv[:, q_cols + k_cols :],
+        grad_input,
+        grad_query,
+        grad_key,
+        grad_value,
         grad_wout,
-        grad_wgate,
-        grad_wup,
-        grad_wdown,
-    ) + tuple(gains)
+        grad_gate,
+        grad_up,
+        grad_down,
+        gains[0],
+        gains[1],
+        gains[2, :HD],
+        gains[2, HD : 2 * HD],
+    )
 
 
 def local(mesh, layer_input, grad_out, lengths, w_query, w_key, *rest):

time: 1080 us -> 724 us (0.67)
  waiting for transfers between devices: 455 us -> 85.9 us
  Pallas kernels: 345 us -> 585 us
  matrix products: 62 us -> 0 us
  blocking collectives: 59.3 us -> 0 us
  other arithmetic: 62.3 us -> 7 us
  local copies, waits for them, and re-layouts: 57.1 us -> 22.6 us
  starting transfers between devices: 11.9 us -> 0.16 us
    pallas_call x0 -> x5, Pallas kernels: none -> 233 us  [the longest x1 131 us: input_gradient(): pl.pallas_call(input_kernel, out_shape=(jax.ShapeDtypeStruct((micro, tok,...]
    reduce_scatter x5 -> x2, waiting for transfers between devices: 185 us -> 0.01 us  [the longest x1 0.01 us: local_batched(): lax.psum_scatter(feed_grads.reshape(width * 3 * piece, hid), 'wide', scat...]
    psum x1 -> x0, waiting for transfers between devices: 106 us -> none  [local_batched(): lax.psum(partial_one.astype(jnp.bfloat16), 'narrow').astype(jnp.float32)]
    all_to_all x3 -> x0, waiting for transfers between devices: 72.1 us -> none  [the longest x1 32.8 us: local_batched(): lax.all_to_all(packed, 'wide', split_axis=0, concat_axis=0)]
    dot_general x7 -> x0, matrix products: 62 us -> none  [dot_f32(): lax.dot_general(left, right, dims, preferred_element_type=jnp.float32)]
    psum x1 -> x0, blocking collectives: 39.7 us -> none  [local_batched(): gains = lax.psum((gain_one, gain_two, gain_q, gain_k), ('wide', 'narrow'))]
    all_to_all x1 -> x0, blocking collectives: 19.6 us -> none  [local_batched(): grad_mixed = lax.all_to_all(grad_mixed, 'wide', split_axis=0, concat_axis=0)]
    all_gather x4 -> x1, waiting for transfers between devices: 72.1 us -> 55.3 us  [local_batched(): lax.all_gather(jnp.concatenate([w_out, w_down, stacked(w_gate), stacked(w...]
  transfers between devices with their start and end apart: 14 -> 4, of which waited for: 10 -> 2; matrix products, arithmetic and copies ran while one was open for 15% -> 2% of each run, Pallas kernels for 2% -> 38%
where the time goes in v2:
time: 724 us; the launch traced here: 715 us
  Pallas kernels  585 us (81%)
  waiting for transfers between devices  85.9 us (12%)
  local copies, waits for them, and re-layouts  22.6 us (3%)
  between operations  14.5 us (2%)
    pallas_call x1, Pallas kernels, feed_forward(): pl.pallas_call(feed_kernel, out_shape=(jax.ShapeDtypeStruct((micro, tok,...  309 us
    pallas_call x1, Pallas kernels, input_gradient(): pl.pallas_call(input_kernel, out_shape=(jax.ShapeDtypeStruct((micro, tok,...  131 us
    all_gather x1, waiting for transfers between devices, local_batched(): lax.all_gather(jnp.concatenate([w_out, w_down, stacked(w_gate), stacked(w...  55.3 us
    pallas_call x1, Pallas kernels, weight_gradients(): pl.pallas_call(weights_kernel, out_shape=(jax.ShapeDtypeStruct((micro, to...  50.8 us
    pallas_call x1, Pallas kernels, project(): pl.pallas_call(project_kernel, out_shape=(jax.ShapeDtypeStruct((micro, to...  45 us
    all_gather x1, waiting for transfers between devices, local_batched(): lax.all_gather(jnp.concatenate([w_query, w_key, w_value], axis=1), 'wide'...  30.6 us
    pallas_call x1, Pallas kernels, attention_back(): pl.pallas_call(attend_backward, out_shape=jax.ShapeDtypeStruct((total, 4...  23.2 us
    pallas_call x1, Pallas kernels, attention_out(): pl.pallas_call(attend_forward, out_shape=(jax.ShapeDtypeStruct((total, 2...  19.6 us
  transfers between devices with their start and end apart: 4, of which 2 were waited for; matrix products, arithmetic and copies ran while one was open for 2% of the time, Pallas kernels for 38%

profile of v2, /device:TPU:0, one launch (start us, length us, event | category | flops | bytes accessed | tf_op | source)
XLA Modules:
  0.0 715.2 jit_solution(1795469136303587142)
XLA Ops:
  7.2 2.0 pad_maximum_fusion.1
  9.3 1.4 copy.40
  10.7 0.3 copy.41
  11.0 1.4 copy.42
  12.4 0.3 copy.43
  12.8 1.6 pad_maximum_fusion
  14.5 0.2 reduce_window_sum.11
  14.7 0.2 convert_reduce_fusion
  15.2 1.3 copy.39.start_ref
  16.6 0.5 and_select_fusion.first_ref
  17.1 0.2 broadcast_multiply_fusion
  17.3 2.1 negate_select_fusion
  19.4 30.6 %all-gather.4.cloned.1.call-done.weight_ref = bf16[2048,1024]{1,0:T(8,128)(2,1)} async-done(((bf16[256,1024]{1,0:T(8,128)(2,1)}), bf16[2048,1024]{1,0:T(8,128)(2,1)}) %all-gather.4.cloned.1.call-update) | async-done | bytes 4194320 | tf_op jit(solution)/shard_map/all_gather | solution.py:1625
  50.0 45.0 %project.1 = (bf16[4,256,2048]{2,1,0:T(8,128)(2,1)S(1)}, f32[4,256,768]{2,1,0:T(8,128)S(1)}, bf16[8,256,512]{2,1,0:T(8,128)(2,1)S(1)}) custom-call(bf16[4,256,2048]{2,1,0:T(8,128)(2,1)} %input_ref.5, f32[1,2048]{1,0:T(1,128)S(1)} %bitcast.32, bf16[2048,1024]{1,0:T(8,128)(2,1)} %all-gather.4.cloned.1.call-done.weight_ref, ...), custom_call_target="tpu_custom_call" | custom-call | flops 20000000000 | bytes 40000000 | tf_op jit(solution)/shard_map/project/pallas_call | solution.py:750
  95.0 1.4 copy-done
  96.4 2.0 copy-done.1
  98.4 1.7 copy-done.2
  100.1 19.6 %attend_forward.1 = (bf16[2048,256]{1,0:T(8,128)(2,1)}, f32[2048,256]{1,0:T(8,128)}, f32[2048,2]{1,0:T(8,128)}) custom-call(s32[8]{0:T(128)} %and_select_fusion.first_ref, bf16[2048,512]{1,0:T(8,128)(2,1)} %bitcast.30, s32[2048,1]{1,0:T(8,128)} %copy.39.start_ref), custom_call_target="tpu_custom_call" | custom-call | tf_op jit(solution)/shard_map/attend_forward/pallas_call | solution.py:426
  119.6 55.3 %all-gather.6.cloned.1.call-done = bf16[40960,256]{1,0:T(8,128)(2,1)} async-done(((bf16[5120,256]{1,0:T(8,128)(2,1)}), bf16[40960,256]{1,0:T(8,128)(2,1)}) %all-gather.6.cloned.1.call-update) | async-done | bytes 20971536 | tf_op jit(solution)/shard_map/all_gather | solution.py:1634
  174.9 309.1 %feed_forward.1 = (bf16[4,256,2048]{2,1,0:T(8,128)(2,1)}, bf16[4,256,1536]{2,1,0:T(8,128)(2,1)}, bf16[4,256,1536]{2,1,0:T(8,128)(2,1)}, bf16[4,256,1536]{2,1,0:T...) custom-call(bf16[8,256,256]{2,1,0:T(8,128)(2,1)} %bitcast.50, ...), custom_call_target="tpu_custom_call" | custom-call | flops 240000008192 | bytes 900000000 | tf_op jit(solution)/shard_map/feed_forward/pallas_call | solution.py:1312
  484.2 23.2 %attend_backward.1 = bf16[2048,512]{1,0:T(8,128)(2,1)} custom-call(s32[8]{0:T(128)} %and_select_fusion.first_ref, bf16[2048,512]{1,0:T(8,128)(2,1)} %bitcast.31, s32[2048,1]{1,0:T(8,128)} %copy.39.start_ref, bf16[2048,256]{1,0:T(8,128)(2,1)} %bitcast.41, f32[2048,256]{1,0:T(8,128)} %get-tuple-element.44.kept_ref, f32[2048,2]{1,0:T(8,128)} %get-tuple-element.45.log_ref), custom_call_target="tpu_custom_call" | custom-call | tf_op jit(solution)/shard_map/attend_backward/pallas_call | solution.py:454
  507.4 1.4 copy-done.7
  508.8 50.8 %weight_gradients.1 = (bf16[4,256,1024]{2,1,0:T(8,128)(2,1)S(1)}, bf16[8,256,1536]{2,1,0:T(8,128)(2,1)}, f32[2,128]{1,0:T(2,128)S(1)}) custom-call(bf16[8,256,512]{2,1,0:T(8,128)(2,1)} %bitcast.35, f32[4,256,768]{2,1,0:T(8,128)} %copy-done.2, bf16[4,256,2048]{2,1,0:T(8,128)(2,1)} %copy-done.1, bf16[4,256,512]{2,1,0:T(8,128)(2,1)S(1)} %copy-done.7, ...), custom_call_target="tpu_custom_call" | custom-call | flops 1000000000 | bytes 1000000 | tf_op jit(solution)/shard_map/weight_gradients/pallas_call | solution.py:899
  559.6 0.7 copy-done.9
  560.2 131.0 %input_gradient.1 = (f32[4,256,2048]{2,1,0:T(8,128)}, f32[8,2048]{1,0:T(8,128)S(1)}) custom-call(bf16[4,256,1024]{2,1,0:T(8,128)(2,1)S(1)} %get-tuple-element.50.back_ref, bf16[4,256,2048]{2,1,0:T(8,128)(2,1)} %input_ref.5, f32[4,256,2048]{2,1,0:T(8,128)} %get-tuple-element.51.middle_ref, f32[1,2048]{1,0:T(1,128)S(1)} %bitcast.33, ...), custom_call_target="tpu_custom_call" | custom-call | flops 1000000000 | bytes 1000000 | tf_op jit(solution)/shard_map/input_gradient/pallas_call | solution.py:1542
  691.3 0.5 slice_bitcast_fusion
  691.8 0.6 fusion.3
  692.4 3.9 widen_feed.1
  696.3 2.3 widen_attn.1
  698.6 5.1 copy.48
  703.7 1.1 copy-done.13
  704.8 3.4 copy.49
  (51 shorter events, 0.6 us)
Async XLA Ops:
  7.2 5.5 copy-start.14
  7.2 5.5 copy-start.15
  7.2 42.8 %all-gather.4.cloned.1.call-start = ((), (), s32[]{:S(2)}) async-start(), calls=%async_computation.2 | async-start | bytes 4718592 | tf_op jit(solution)/shard_map/all_gather | solution.py:1625
  9.3 165.7 %all-gather.6.cloned.1.call-start = ((), (), s32[]{:S(2)}) async-start(), calls=%async_computation.5 | async-start | bytes 23592960 | tf_op jit(solution)/shard_map/all_gather | solution.py:1634
  12.7 1.8 copy-start.16
  12.7 3.8 copy-start.17
  12.7 3.8 copy-start.18
  14.4 35.5 %copy-start.8 = (f32[2048]{0:T(1024)S(1)}, f32[2048]{0:T(1024)}, u32[]{:S(2)}) copy-start(f32[2048]{0:T(1024)} %param.24) | copy-start | bytes 24580
  14.4 678.0 %reduce-scatter.3.cloned.1.call-start = ((), (), s32[]{:S(2)}) async-start(), calls=%async_computation.3 | async-start | bytes 21233664 | tf_op jit(solution)/shard_map/reduce_scatter | solution.py:1672
  16.6 78.4 %copy-start.11 = (f32[2,128]{1,0:T(2,128)}, f32[2,128]{1,0:T(2,128)S(1)}, u32[]{:S(2)}) copy-start(f32[2,128]{1,0:T(2,128)S(1)} %pad_maximum_fusion.3.head_gain_ref) | copy-start | bytes 3076
  19.4 75.6 %copy-start.3 = (f32[1024,128]{1,0:T(8,128)}, f32[1024,128]{1,0:T(8,128)S(1)}, u32[]{:S(2)}) copy-start(f32[1024,128]{1,0:T(8,128)S(1)} %get-tuple-element.67.sine_ref) | copy-start | bytes 1572868
  19.4 75.6 %copy-start.5 = (f32[1024,128]{1,0:T(8,128)}, f32[1024,128]{1,0:T(8,128)S(1)}, u32[]{:S(2)}) copy-start(f32[1024,128]{1,0:T(8,128)S(1)} %get-tuple-element.68.cosine_ref) | copy-start | bytes 1572868
  95.0 1.4 copy-start
  96.4 2.0 copy-start.1
  98.4 1.7 copy-start.2
  484.1 212.3 %reduce-scatter.5.cloned.1.call-start = ((), (), s32[]{:S(2)}) async-start(), calls=%async_computation.4 | async-start | bytes 7077888 | tf_op jit(solution)/shard_map/reduce_scatter | solution.py:1688
  484.1 23.3 %copy-start.4 = (f32[1024,128]{1,0:T(8,128)S(1)}, f32[1024,128]{1,0:T(8,128)}, u32[]{:S(2)}) copy-start(f32[1024,128]{1,0:T(8,128)} %copy-done.3) | copy-start | bytes 1572868
  484.1 23.3 %copy-start.6 = (f32[1024,128]{1,0:T(8,128)S(1)}, f32[1024,128]{1,0:T(8,128)}, u32[]{:S(2)}) copy-start(f32[1024,128]{1,0:T(8,128)} %copy-done.5) | copy-start | bytes 1572868
  484.1 23.2 %copy-start.12 = (f32[2,128]{1,0:T(2,128)S(1)}, f32[2,128]{1,0:T(2,128)}, u32[]{:S(2)}) copy-start(f32[2,128]{1,0:T(2,128)} %copy-done.11) | copy-start | bytes 3076
  507.4 1.4 copy-start.7
  559.5 0.7 copy-start.9
  559.5 0.7 copy-start.10
  698.6 6.2 copy-start.13
Sparse Core Ops, SparseCore 0:
  10.5 39.4 all-gather.3
  51.8 123.0 all-gather.5
  484.2 142.9 reduce-scatter.2
  630.4 61.7 reduce-scatter.4

commit v3 on v2

--- a/solution.py
+++ b/solution.py
@@ -480,6 +480,8 @@
 
 SUB = 64
 RING = 8
+AHEAD = 3
+GAIN_TICKS = (0, 2, 4, 6, 11, 14, 17)
 LANES = 512
 MESH = pl.DeviceIdType.MESH
 
@@ -653,16 +655,105 @@
             self.remote(self.spot, source).wait_recv()
 
 
+class Gather:
+    def __init__(self, parts, send_sem, land_sem):
+        self.parts, self.send_sem, self.land_sem = parts, send_sem, land_sem
+        me = lax.axis_index("wide")
+        flip = lambda spot, bit: spot + bit - 2 * bit * (spot // bit % 2)
+        self.me, self.near = me, flip(me, 1)
+        self.across, self.along = flip(me, 2), flip(me, 4)
+        self.far = flip(self.across, 4)
+        self.flip = flip
+
+    def move(self, part, kind, source, target, device):
+        return pltpu.make_async_remote_copy(
+            src_ref=source,
+            dst_ref=target,
+            send_sem=self.send_sem.at[part, kind],
+            recv_sem=self.land_sem.at[part, kind],
+            device_id={"wide": device},
+            device_id_type=MESH,
+        )
+
+    def going(self, part, kind):
+        own, slot, half = self.parts[part]
+        across, along, near = self.across, self.along, self.near
+        source, target, device = (
+            lambda: (own, slot(self.me), across),
+            lambda: (own, slot(self.me), along),
+            lambda: (own, slot(self.me), near),
+            lambda: (half(along, 0), half(along, 0), across),
+            lambda: (half(across, 1), half(across, 1), along),
+            lambda: (slot(across), slot(across), near),
+            lambda: (slot(along), slot(along), near),
+            lambda: (half(self.far, 0), half(self.far, 0), near),
+            lambda: (half(self.far, 1), half(self.far, 1), near),
+        )[kind]()
+        return self.move(part, kind, source, target, device)
+
+    def coming(self, part, kind):
+        _, slot, half = self.parts[part]
+        flip = self.flip
+        place = (
+            lambda: slot(self.across),
+            lambda: slot(self.along),
+            lambda: slot(self.near),
+            lambda: half(self.far, 0),
+            lambda: half(self.far, 1),
+            lambda: slot(flip(self.across, 1)),
+            lambda: slot(flip(self.along, 1)),
+            lambda: half(flip(self.far, 1), 0),
+            lambda: half(flip(self.far, 1), 1),
+        )[kind]()
+        return self.move(part, kind, place, place, self.near)
+
+    def here(self, part):
+        own, slot, _ = self.parts[part]
+        return pltpu.make_async_copy(own, slot(self.me), self.land_sem.at[part, 9])
+
+    def first(self, part):
+        for kind in (0, 1, 2):
+            self.going(part, kind).start()
+        self.here(part).start()
+
+    def second(self, part):
+        self.coming(part, 1).wait_recv()
+        self.going(part, 3).start()
+        self.coming(part, 0).wait_recv()
+        self.going(part, 4).start()
+        self.going(part, 6).start()
+        self.going(part, 5).start()
+
+    def third(self, part):
+        self.coming(part, 3).wait_recv()
+        self.going(part, 7).start()
+        self.coming(part, 4).wait_recv()
+        self.going(part, 8).start()
+
+    def fourth(self, part):
+        self.here(part).wait()
+        for kind in (2, 5, 6, 7, 8):
+            self.coming(part, kind).wait_recv()
+
+    def drain(self):
+        for part in range(len(self.parts)):
+            for kind in range(9):
+                self.going(part, kind).wait_send()
+
+
 def project_kernel(
     input_ref,
     gain_ref,
-    weight_ref,
+    query_w,
+    key_w,
+    value_w,
     cosine_ref,
     sine_ref,
     head_gain_ref,
     hidden_out,
     raw_out,
     packed_out,
+    weight_out,
     rows_v,
     weight_v,
     hidden_v,
@@ -670,8 +761,11 @@
     pack_v,
     load_sem,
     keep_sem,
+    hidden_sem,
     send_sem,
     land_sem,
+    part_send,
+    part_land,
 ):
     micro, tok, model = input_ref.shape
     width = packed_out.shape[0]
@@ -681,21 +775,50 @@
     swap = Exchange(
         lambda target: pack_v.at[target], lambda source: packed_out.at[source], send_sem, land_sem
     )
-    loads = [
-        pltpu.make_async_copy(input_ref, rows_v, load_sem.at[0]),
-        pltpu.make_async_copy(weight_ref, weight_v, load_sem.at[1]),
-    ]
-    for copy in loads:
-        copy.start()
+    load = pltpu.make_async_copy(input_ref, rows_v, load_sem.at[0])
+    load.start()
+    piece = query_w.shape[0]
+
+    def part(own, first):
+        cols = pl.ds(first, own.shape[1])
+        return (
+            own,
+            lambda s: weight_v.at[pl.ds(pl.multiple_of(s * piece, piece), piece), cols],
+            lambda s, h: weight_v.at[
+                pl.ds(pl.multiple_of(s * piece + h * piece // 2, piece // 2), piece // 2), cols
+            ],
+        )
+
+    q_cols, k_cols = query_w.shape[1], key_w.shape[1]
+    gather = Gather(
+        [part(query_w, 0), part(key_w, q_cols), part(value_w, q_cols + k_cols)],
+        part_send,
+        part_land,
+    )
     greet_wide(width)
-    for copy in loads:
-        copy.wait()
+    for p in range(3):
+        gather.first(p)
+    load.wait()
+    hidden_copy = pltpu.make_async_copy(hidden_v, hidden_out, hidden_sem)
+
+    @pl.loop(0, micro)
+    def _(m):
+        rows = rows_v[m].astype(jnp.float32)
+        scale = lax.rsqrt(jnp.mean(rows * rows, axis=-1, keepdims=True) + EPSILON)
+        hidden_v[m] = (rows * scale * gain_ref[...]).astype(jnp.bfloat16)
+
+    hidden_copy.start()
+    for p in range(3):
+        gather.second(p)
+    for p in range(3):
+        gather.third(p)
+    for p in range(3):
+        gather.fourth(p)
+    weight_copy = pltpu.make_async_copy(weight_v, weight_out, load_sem.at[1])
+    weight_copy.start()
 
     def keeps(step, m):
-        return [
-            pltpu.make_async_copy(hidden_v.at[step % 2], hidden_out.at[m], keep_sem.at[step % 2, 0]),
-            pltpu.make_async_copy(raw_v.at[step % 2], raw_out.at[m], keep_sem.at[step % 2, 1]),
-        ]
+        return [pltpu.make_async_copy(raw_v.at[step % 2], raw_out.at[m], keep_sem.at[step % 2])]
 
     kept = []
     for step in range(micro):
@@ -708,10 +831,7 @@
         if step >= 2:
             for copy in kept[step - 2]:
                 copy.wait()
-        rows = rows_v[m].astype(jnp.float32)
-        scale = lax.rsqrt(jnp.mean(rows * rows, axis=-1, keepdims=True) + EPSILON)
-        hidden_v[step % 2] = (rows * scale * gain_ref[...]).astype(jnp.bfloat16)
-        heads_all = dot_f32(hidden_v[step % 2], weight_v[...])
+        heads_all = dot_f32(hidden_v[m], weight_v[...])
         span = pl.ds(pl.multiple_of(m * tok, tok), tok)
         cosine, sine = cosine_ref[span, :], sine_ref[span, :]
         raw_v[step % 2] = heads_all[:, : (heads + groups) * HD]
@@ -739,33 +859,42 @@
         swap.sent(d)
         swap.wait(d)
 
-
-def project(layer_input, gain_attn, weight, cosine, sine, head_gains, width):
+    gather.drain()
+    hidden_copy.wait()
+    weight_copy.wait()
+
+
+def project(layer_input, gain_attn, weights, cosine, sine, head_gains, width):
     micro, tok, model = layer_input.shape
     groups = width // micro
     low = jnp.bfloat16
     anywhere = pl.BlockSpec(memory_space=pl.ANY)
     inside = pl.BlockSpec(memory_space=pltpu.VMEM)
     raw = 3 * groups * HD
+    columns = sum(weight.shape[1] for weight in weights)
     return pl.pallas_call(
         project_kernel,
         out_shape=(
             jax.ShapeDtypeStruct((micro, tok, model), low),
             jax.ShapeDtypeStruct((micro, tok, raw), jnp.float32),
             jax.ShapeDtypeStruct((width, tok, 4 * HD), low),
+            jax.ShapeDtypeStruct((model, columns), low),
         ),
-        in_specs=[anywhere, inside, anywhere, inside, inside, inside],
-        out_specs=[anywhere] * 3,
+        in_specs=[anywhere, inside, anywhere, anywhere, anywhere, inside, inside, inside],
+        out_specs=[anywhere] * 4,
         scratch_shapes=[
             pltpu.VMEM((micro, tok, model), low),
-            pltpu.VMEM(weight.shape, low),
-            pltpu.VMEM((2, tok, model), low),
+            pltpu.VMEM((model, columns), low),
+            pltpu.VMEM((micro, tok, model), low),
             pltpu.VMEM((2, tok, raw), jnp.float32),
             pltpu.VMEM((width, tok, 4 * HD), low),
             pltpu.SemaphoreType.DMA((2,)),
-            pltpu.SemaphoreType.DMA((2, 2)),
+            pltpu.SemaphoreType.DMA((2,)),
+            pltpu.SemaphoreType.DMA,
             pltpu.SemaphoreType.DMA((width,)),
             pltpu.SemaphoreType.DMA((width,)),
+            pltpu.SemaphoreType.DMA((3, 9)),
+            pltpu.SemaphoreType.DMA((3, 10)),
         ],
         compiler_params=pltpu.CompilerParams(
             collective_id=2, has_side_effects=True, vmem_limit_bytes=40 << 20
@@ -774,7 +903,7 @@
             flops=20_000_000_000, bytes_accessed=40_000_000, transcendentals=0
         ),
         name="project",
-    )(layer_input, gain_attn[None, :], weight, cosine, sine, head_gains)
+    )(layer_input, gain_attn[None, :], *weights, cosine, sine, head_gains)
 
 
 def weights_kernel(
@@ -796,11 +925,13 @@
     low_v,
     back_v,
     grad_v,
+    pair_v,
     load_sem,
     back_sem,
     tile_sem,
     send_sem,
     land_sem,
+    pair_sems,
 ):
     micro, tok, heads_in = mixed_ref.shape
     width = back_ref.shape[0]
@@ -870,19 +1001,53 @@
 
     loads[3].wait()
 
-    def tile_copy(i):
-        return pltpu.make_async_copy(grad_v.at[i], grad_out.at[i], tile_sem.at[i])
+    core = lax.rem(spot, 2)
+    near = spot + 1 - 2 * core
+
+    def tile_copy(c):
+        return pltpu.make_async_copy(grad_v.at[2 * c + core], grad_out.at[c], tile_sem.at[c])
+
+    def pair_copy(c):
+        return pltpu.make_async_remote_copy(
+            src_ref=grad_v.at[2 * c + 1 - core],
+            dst_ref=pair_v.at[c],
+            send_sem=pair_sems.at[0, c],
+            recv_sem=pair_sems.at[1, c],
+            device_id={"wide": near},
+            device_id_type=MESH,
+        )
+
+    def tile(i):
+        left = hidden_v[:, :, pl.ds(pl.multiple_of(i * piece, piece), piece)].reshape(count, piece)
+        return dot_f32(left, back_v[...].reshape(count, 2 * heads_in), TN)
+
+    @pl.loop(0, width // 2)
+    def _(c):
+        i = 2 * c + 1 - core
+        grad_v[i, :, 0 : 2 * heads_in] = tile(i).astype(jnp.bfloat16)
+        pair_copy(c).start()
+
+    @pl.loop(0, width // 2)
+    def _(c):
+        i = 2 * c + core
+        part = tile(i)
+        pair_copy(c).wait_recv()
+        grad_v[i, :, 0 : 2 * heads_in] = (
+            part + pair_v[c, :, 0 : 2 * heads_in].astype(jnp.float32)
+        ).astype(jnp.bfloat16)
+        grad_v[i, :, 2 * heads_in :] = (
+            grad_v[i, :, 2 * heads_in :].astype(jnp.float32)
+            + pair_v[c, :, 2 * heads_in :].astype(jnp.float32)
+        ).astype(jnp.bfloat16)
+        tile_copy(c).start()
+
+    @pl.loop(0, width // 2)
+    def _(c):
+        tile_copy(c).wait()
+        pair_copy(c).wait_send()
 
     @pl.loop(0, width)
     def _(i):
-        left = hidden_v[:, :, pl.ds(pl.multiple_of(i * piece, piece), piece)].reshape(count, piece)
-        right = back_v[...].reshape(count, 2 * heads_in)
-        grad_v[i, :, 0 : 2 * heads_in] = dot_f32(left, right, TN).astype(jnp.bfloat16)
-        tile_copy(i).start()
-
-    @pl.loop(0, width)
-    def _(i):
-        tile_copy(i).wait()
         swap.sent(i)
 
     for m in range(micro):
@@ -900,7 +1065,7 @@
         weights_kernel,
         out_shape=(
             jax.ShapeDtypeStruct((micro, tok, 2 * heads_in), low),
-            jax.ShapeDtypeStruct((width, model // width, 3 * heads_in), low),
+            jax.ShapeDtypeStruct((width // 2, model // width, 3 * heads_in), low),
             jax.ShapeDtypeStruct((2, HD), jnp.float32),
         ),
         in_specs=[anywhere] * 5 + [inside] * 3,
@@ -913,11 +1078,13 @@
             pltpu.VMEM(middle_low.shape, low),
             pltpu.VMEM((micro, tok, 2 * heads_in), low),
             pltpu.VMEM((width, model // width, 3 * heads_in), low),
+            pltpu.VMEM((width // 2, model // width, 3 * heads_in), low),
             pltpu.SemaphoreType.DMA((4,)),
             pltpu.SemaphoreType.DMA((micro,)),
+            pltpu.SemaphoreType.DMA((width // 2,)),
             pltpu.SemaphoreType.DMA((width,)),
             pltpu.SemaphoreType.DMA((width,)),
-            pltpu.SemaphoreType.DMA((width,)),
+            pltpu.SemaphoreType.DMA((2, width // 2)),
         ],
         compiler_params=pltpu.CompilerParams(
             collective_id=3, has_side_effects=True, vmem_limit_bytes=48 << 20
@@ -947,6 +1114,8 @@
     grad_ref,
     gain_ref,
     pack_ref,
+    up_w,
+    down_w,
     hidden_out,
     active_out,
     gate_out,
@@ -958,6 +1127,7 @@
     gain_out,
     weight_out,
     heads_out,
+    early_out,
     own,
     landed,
     cross,
@@ -989,6 +1159,10 @@
     ahead_sems,
     behind_sems,
     heads_sem,
+    part_send,
+    part_land,
+    pair_sems,
+    credit,
 ):
     micro, tok, model = input_ref.shape
     width, _, piece = pack_ref.shape
@@ -1031,21 +1205,44 @@
     ]
     weight_copies = [
         pltpu.make_async_copy(
-            pack_ref.at[i, pl.ds(heads_in + (1 + q) * hid + j * piece, piece)],
-            target.at[pl.ds(i * piece, piece), pl.ds(j * piece, piece)],
-            weight_sem.at[1 + q, i, j],
-        )
-        for q, target in enumerate((gate_v, up_v))
+            pack_ref.at[i, pl.ds(heads_in + j * piece, piece)],
+            gate_v.at[pl.ds(i * piece, piece), pl.ds(j * piece, piece)],
+            weight_sem.at[i, j],
+        )
         for i in range(width)
         for j in range(blocks)
-    ] + [
-        pltpu.make_async_copy(
-            pack_ref.at[i, pl.ds(heads_in, hid)],
-            down_v.at[:, pl.ds(i * piece, piece)],
-            weight_sem.at[0, i, 0],
-        )
-        for i in range(width)
     ]
+
+    def up_part(j):
+        cols = pl.ds(j * LANES, LANES)
+        return (
+            up_w.at[:, cols],
+            lambda s: up_v.at[pl.ds(pl.multiple_of(s * piece, piece), piece), cols],
+            lambda s, h: up_v.at[
+                pl.ds(pl.multiple_of(s * piece + h * piece // 2, piece // 2), piece // 2), cols
+            ],
+        )
+
+    def down_part(j):
+        return (
+            down_w.at[pl.ds(j * LANES, LANES)],
+            lambda s: down_v.at[
+                pl.ds(j * LANES, LANES), pl.ds(pl.multiple_of(s * piece, piece), piece)
+            ],
+            lambda s, h: down_v.at[
+                pl.ds(j * LANES + h * LANES // 2, LANES // 2),
+                pl.ds(pl.multiple_of(s * piece, piece), piece),
+            ],
+        )
+
+    gather = Gather(
+        [make(j) for j in range(n_up) for make in (up_part, down_part)], part_send, part_land
+    )
+
+    def both(action, j):
+        action(2 * j)
+        action(2 * j + 1)
+
     for copy in attn_copies + weight_copies:
         copy.start()
 
@@ -1070,6 +1267,8 @@
     spot = lax.axis_index("wide")
     for step in range(width):
         ahead.send(lax.rem(spot + step, width))
+    both(gather.first, 0)
+    both(gather.first, 1)
     for copy in attn_copies:
         copy.wait()
 
@@ -1090,8 +1289,15 @@
 
     first_ticks = per + 4
 
-    @pl.loop(0, first_ticks)
-    def _(k):
+    for k in range(first_ticks):
+        if k == 4:
+            both(gather.second, 0)
+        if k == 5:
+            both(gather.first, 2)
+        if k == 6:
+            both(gather.second, 1)
+        if k == 7:
+            both(gather.third, 0)
         relay.tick(k)
 
     for copy in weight_copies:
@@ -1131,6 +1337,15 @@
         hidden_copy(m).start()
         for j in range(n_up):
             relay.tick(first_ticks + slots * m + j)
+
+            @pl.when(m == 0)
+            def _():
+                if j == 0:
+                    both(gather.second, 2)
+                if j + 1 < n_up:
+                    both(gather.third, j + 1)
+                both(gather.fourth, j)
+
             cols = pl.ds(j * LANES, LANES)
             gate = dot_f32(hidden_v[...], gate_v[:, cols])
             up_proj = dot_f32(hidden_v[...], up_v[:, cols])
@@ -1168,6 +1383,15 @@
     for copy in stage_copies(micro - 1):
         copy.wait()
 
+    gather.drain()
+    core = lax.rem(spot, 2)
+    near = gather.near
+
+    def offer():
+        pl.semaphore_signal(credit, inc=1, device_id={"wide": near}, device_id_type=MESH)
+
+    offer()
+
     @pl.loop(0, base)
     def _(k):
         relay.to_inner(k).wait_send()
@@ -1192,25 +1416,53 @@
         for copy in reloads(m):
             copy.start()
 
-    def tile_copy(i, q):
-        return pltpu.make_async_copy(stage_v.at[q], weight_out.at[i, q], tile_sem.at[q])
-
-    def tile(i, q):
+    def pair_slot(q):
+        return up_v.at[pl.ds(count + q * piece, piece)]
+
+    def tile_copy(m, q):
+        target = early_out.at[m] if q == 0 else weight_out.at[m, q - 1]
+        return pltpu.make_async_copy(pair_slot(q), target, tile_sem.at[q])
+
+    def pair_copy(q):
+        return pltpu.make_async_remote_copy(
+            src_ref=stage_v.at[q],
+            dst_ref=pair_slot(q),
+            send_sem=pair_sems.at[0, q],
+            recv_sem=pair_sems.at[1, q],
+            device_id={"wide": near},
+            device_id_type=MESH,
+        )
+
+    def tile(i, q, store):
         cols = pl.ds(pl.multiple_of(i * piece, piece), piece)
-
-        @pl.when(i > 0)
-        def _():
-            tile_copy(i - 1, q).wait()
-
         if q == 2:
             right = own[0:base, :, cols].reshape(count, piece)
             for j in range(blocks):
                 span = slice(j * piece, (j + 1) * piece)
-                stage_v[q, :, span] = dot_f32(up_v[0:count, span], right, TN).astype(jnp.bfloat16)
+                store(span, dot_f32(up_v[0:count, span], right, TN))
         else:
             right = (gate_v[0:count], gate_v[count : 2 * count])[q]
-            stage_v[q] = dot_f32(down_v[0:count, cols], right, TN).astype(jnp.bfloat16)
-        tile_copy(i, q).start()
+            store(slice(0, hid), dot_f32(down_v[0:count, cols], right, TN))
+
+    def give(m, q):
+        @pl.when(m > 0)
+        def _():
+            pair_copy(q).wait_send()
+
+        def store(span, part):
+            stage_v[q, :, span] = part.astype(jnp.bfloat16)
+
+        tile(2 * m + 1 - core, q, store)
+
+    def keep(m, q):
+        rows = pl.ds(count + q * piece, piece)
+        pair_copy(q).wait_recv()
+
+        def store(span, part):
+            up_v[rows, span] = (part + up_v[rows, span].astype(jnp.float32)).astype(jnp.bfloat16)
+
+        tile(2 * m + core, q, store)
+        tile_copy(m, q).start()
 
     def final_copies(m):
         return [
@@ -1244,9 +1496,13 @@
                     copy.wait()
 
         relay.tick(last_ticks + turns * m)
-        tile(2 * m, 0)
-        tile(2 * m, 1)
+        give(m, 0)
+        give(m, 1)
         relay.tick(last_ticks + turns * m + 1)
+        give(m, 2)
+        pl.semaphore_wait(credit, 1)
+        for q in range(3):
+            pair_copy(q).start()
         for r in range(per):
             span = pl.ds(r * SUB, SUB)
             middle = rows_v[slot, span, :].astype(jnp.float32) + landed[m * per + r].astype(
@@ -1268,12 +1524,11 @@
         mixback_v[m % 2] = dot_f32(hidden_v[...], out_v[...], NT).astype(jnp.bfloat16)
         for g in range(groups):
             behind.send(m * groups + g)
-        tile(2 * m, 2)
         relay.tick(last_ticks + turns * m + 2)
-        tile(2 * m + 1, 0)
-        tile(2 * m + 1, 1)
+        keep(m, 0)
+        keep(m, 1)
         relay.tick(last_ticks + turns * m + 3)
-        tile(2 * m + 1, 2)
+        keep(m, 2)
         for r in range(per):
             span = pl.ds(r * SUB, SUB)
             output_v[span, :] = (
@@ -1283,9 +1538,17 @@
             ).astype(jnp.bfloat16)
         for copy in final_copies(m):
             copy.start()
-
-    for copy in final_copies(micro - 1) + [tile_copy(width - 1, q) for q in range(3)]:
+        for q in range(3):
+            tile_copy(m, q).wait()
+
+        @pl.when(m < micro - 1)
+        def _():
+            offer()
+
+    for copy in final_copies(micro - 1):
         copy.wait()
+    for q in range(3):
+        pair_copy(q).wait_send()
     for m in range(micro):
         heads_copy(m).wait()
 
@@ -1301,8 +1564,10 @@
     relay.drain(base)
 
 
-def feed_forward(mixed, layer_input, grad_out, gain_ffn, pack, heads_in, hid):
+def feed_forward(mixed, layer_input, grad_out, gain_ffn, pack, up_w, down_w, heads_in):
     micro, tok, model = layer_input.shape
+    hid = up_w.shape[1]
+    parts = 2 * (hid // LANES)
     width, _, piece = pack.shape
     groups = width // micro
     low = jnp.bfloat16
@@ -1321,11 +1586,12 @@
             jax.ShapeDtypeStruct((micro, tok, model), low),
             jax.ShapeDtypeStruct((width, tok, 2 * HD), low),
             jax.ShapeDtypeStruct((1, model), jnp.float32),
-            jax.ShapeDtypeStruct((width, 3, piece, hid), low),
+            jax.ShapeDtypeStruct((width // 2, 2, piece, hid), low),
             jax.ShapeDtypeStruct((micro, tok, heads_in), low),
+            jax.ShapeDtypeStruct((width // 2, piece, hid), low),
         ),
-        in_specs=[anywhere] * 3 + [inside, anywhere],
-        out_specs=[anywhere] * 8 + [inside, anywhere, anywhere],
+        in_specs=[anywhere] * 3 + [inside, anywhere, anywhere, anywhere],
+        out_specs=[anywhere] * 8 + [inside] + [anywhere] * 3,
         scratch_shapes=relay_scratch(count, model)
         + [
             pltpu.VMEM((heads_in, model), low),
@@ -1341,7 +1607,7 @@
             pltpu.VMEM((tok, model), jnp.float32),
             pltpu.VMEM((tok, model), low),
             pltpu.VMEM((2, tok, heads_in), low),
-            pltpu.SemaphoreType.DMA((3, width, hid // piece)),
+            pltpu.SemaphoreType.DMA((width, hid // piece)),
             pltpu.SemaphoreType.DMA((width,)),
             pltpu.SemaphoreType.DMA((2, 2)),
             pltpu.SemaphoreType.DMA,
@@ -1352,6 +1618,10 @@
             pltpu.SemaphoreType.DMA((2, width)),
             pltpu.SemaphoreType.DMA((2, width)),
             pltpu.SemaphoreType.DMA((micro,)),
+            pltpu.SemaphoreType.DMA((parts, 9)),
+            pltpu.SemaphoreType.DMA((parts, 10)),
+            pltpu.SemaphoreType.DMA((2, 3)),
+            pltpu.SemaphoreType.REGULAR,
         ],
         compiler_params=pltpu.CompilerParams(
             collective_id=0, has_side_effects=True, vmem_limit_bytes=67043328
@@ -1360,7 +1630,7 @@
             flops=240_000_000_000, bytes_accessed=900_000_000, transcendentals=0
         ),
         name="feed_forward",
-    )(mixed, layer_input, grad_out, gain_ffn[None, :], pack)
+    )(mixed, layer_input, grad_out, gain_ffn[None, :], pack, up_w, down_w)
 
 
 def input_kernel(
@@ -1485,14 +1755,18 @@
             part = part.astype(jnp.bfloat16)
             for r in range(per):
                 own[m * per + r, :, cols] = part[r * SUB : (r + 1) * SUB]
-        relay.send(m * per, per)
+
+        @pl.when(m == 0)
+        def _():
+            relay.send(0, AHEAD)
 
     term_v[0, 1:2, :] = gain_two_ref[...]
     term_v[0, 2:3, 0:HD] = gain_heads_ref[0:1, :]
     term_v[0, 2:3, HD : 2 * HD] = gain_heads_ref[1:2, :]
     for k in range(4):
-        if k % 3 == 0:
-            gain_step(k // 3)
+        if k in GAIN_TICKS:
+            gain_step(GAIN_TICKS.index(k))
+        relay.send(AHEAD + k, 1)
         relay.tick(k)
 
     @pl.loop(0, micro)
@@ -1511,11 +1785,15 @@
 
         for r in range(per):
             for turn in range(micro):
-                if (4 + turn * per + r) % 3 == 0:
+                if 4 + turn * per + r in GAIN_TICKS:
 
                     @pl.when(m == turn)
-                    def _(step=(4 + turn * per + r) // 3):
+                    def _(step=GAIN_TICKS.index(4 + turn * per + r)):
                         gain_step(step)
+
+            @pl.when(AHEAD + 4 + m * per + r < relay.count)
+            def _():
+                relay.send(AHEAD + 4 + m * per + r, 1)
 
             relay.tick(4 + m * per + r)
             span = pl.ds(r * SUB, SUB)
@@ -1572,13 +1850,16 @@
     )(back, layer_input, grad_middle, gain_attn[None, :], weight, gain_two, gain_heads)
 
 
-def widen_feed(rows_ref, gate_ref, up_ref, down_ref):
-    piece = gate_ref.shape[0]
-    gate_ref[...] = rows_ref[0:piece, :].astype(jnp.float32)
-    up_ref[...] = rows_ref[piece : 2 * piece, :].astype(jnp.float32)
+def widen_gate(rows_ref, gate_ref):
+    gate_ref[...] = rows_ref[...].astype(jnp.float32)
+
+
+def widen_feed(rows_ref, up_ref, down_ref):
+    piece = up_ref.shape[0]
+    up_ref[...] = rows_ref[0:piece, :].astype(jnp.float32)
     for j in range(down_ref.shape[0] // piece):
         span = slice(j * piece, (j + 1) * piece)
-        down_ref[span, :] = rows_ref[2 * piece :, span].astype(jnp.float32)
+        down_ref[span, :] = rows_ref[piece:, span].astype(jnp.float32)
 
 
 def widen_attn(rows_ref, query_ref, key_ref, value_ref, out_ref):
@@ -1622,17 +1903,13 @@
     total = tok_rows * width
     count = micro * tok_rows
     me = lax.axis_index("wide")
-    w_qkv = lax.all_gather(
-        jnp.concatenate([w_query, w_key, w_value], axis=1), "wide", axis=0, tiled=True
-    )
-    hid = w_gate.shape[1]
     piece = w_out.shape[1]
 
     def stacked(weight):
         return jnp.moveaxis(weight.reshape(piece, -1, piece), 1, 0).reshape(-1, piece)
 
     pack = lax.all_gather(
-        jnp.concatenate([w_out, w_down, stacked(w_gate), stacked(w_up)], axis=0), "wide", axis=0
+        jnp.concatenate([w_out, stacked(w_gate)], axis=0), "wide", axis=0
     )
 
     starts, places = jax.vmap(lambda row: row_starts(row, total))(lengths)
@@ -1643,8 +1920,8 @@
     my_starts = lax.dynamic_index_in_dim(starts, me // groups, axis=0, keepdims=False)
     my_first = my_starts[::BLOCK] // BLOCK
 
-    hidden_one, raw, packed = project(
-        layer_input, gain_attn, w_qkv, cosine, sine, head_gains, width
+    hidden_one, raw, packed, w_qkv = project(
+        layer_input, gain_attn, (w_query, w_key, w_value), cosine, sine, head_gains, width
     )
     packed = packed.reshape(total, 4 * HD)
     mixed, kept, log_total = attention_out(packed, my_starts, my_first)
@@ -1660,18 +1937,24 @@
         gain_two,
         feed_grads,
         mixed_low,
+        gate_grads,
     ) = feed_forward(
         mixed.reshape(width, tok_rows, 2 * HD),
         layer_input,
         grad_out,
         gain_ffn,
         pack,
+        w_up,
+        w_down,
         w_out.shape[0],
-        hid,
-    )
-    feed_grads = lax.psum_scatter(
-        feed_grads.reshape(width * 3 * piece, hid), "wide", scatter_dimension=0, tiled=True
-    )
+    )
+    cores = [list(range(core, width, 2)) for core in range(2)]
+
+    def scatter(rows):
+        return lax.psum_scatter(
+            rows, "wide", scatter_dimension=0, axis_index_groups=cores, tiled=True
+        )
+
     back = attention_back(
         packed, my_starts, my_first, grad_mixed.reshape(total, 2 * HD), kept, log_total
     )
@@ -1685,17 +1968,16 @@
         sine,
         head_gains,
     )
-    attn_grads = lax.psum_scatter(
-        attn_grads.reshape(model, -1), "wide", scatter_dimension=0, tiled=True
-    )
+    gate_grads = scatter(gate_grads.reshape(-1, w_gate.shape[1]))
+    attn_grads, feed_grads = lax.optimization_barrier((attn_grads, feed_grads))
+    attn_grads = scatter(attn_grads.reshape(model // 2, -1))
+    feed_grads = scatter(feed_grads.reshape(-1, w_up.shape[1]))
     grad_input, gains = input_gradient(
         qkv_back, layer_input, grad_middle, gain_attn, w_qkv, gain_two, gain_heads
     )
 
-    grad_gate, grad_up, grad_down = widen(
-        widen_feed, feed_grads, (w_gate.shape, w_up.shape, w_down.shape)
-    )
-    grad_gate, attn_grads = lax.optimization_barrier((grad_gate, attn_grads))
+    (grad_gate,) = widen(widen_gate, gate_grads, (w_gate.shape,))
+    grad_up, grad_down = widen(widen_feed, feed_grads, (w_up.shape, w_down.shape))
     grad_query, grad_key, grad_value, grad_wout = widen(
         widen_attn, attn_grads, (w_query.shape, w_key.shape, w_value.shape, w_out.shape)
     )
@@ -1721,7 +2003,7 @@
     micro, tok_rows = layer_input.shape[:2]
     groups = w_key.shape[1] // HD
     fits = (
-        micro * groups == width
+        micro * groups == width == 8
         and w_query.shape[1] == 2 * w_key.shape[1]
         and mesh.shape["narrow"] == 4
         and tok_rows == BLOCK

time: 724 us -> 657 us (0.907)
  waiting for transfers between devices: 85.9 us -> 0.56 us
  Pallas kernels: 585 us -> 608 us
    all_gather x2 -> x1, waiting for transfers between devices: 85.8 us -> 0.01 us  [local_batched(): lax.all_gather(jnp.concatenate([w_out, stacked(w_gate)], axis=0), 'wide',...]
    pallas_call x1, Pallas kernels: 45 us -> 81.6 us  [project(): pl.pallas_call(project_kernel, out_shape=(jax.ShapeDtypeStruct((micro, to...]
    pallas_call x1, Pallas kernels: 131 us -> 121 us  [input_gradient(): pl.pallas_call(input_kernel, out_shape=(jax.ShapeDtypeStruct((micro, tok,...]
    unnamed x43 -> x46, local copies, waits for them, and re-layouts: 19.5 us -> 17.7 us
  transfers between devices with their start and end apart: 4 -> 4, of which waited for: 2 -> 0; matrix products, arithmetic and copies ran while one was open for 2% -> 1% of each run, Pallas kernels for 38% -> 46%
where the time goes in v3:
time: 657 us; the launch traced here: 648 us
  Pallas kernels  608 us (93%)
  local copies, waits for them, and re-layouts  20.5 us (3%)
  between operations  14.6 us (2%)
    pallas_call x1, Pallas kernels, feed_forward(): pl.pallas_call(feed_kernel, out_shape=(jax.ShapeDtypeStruct((micro, tok,...  308 us
    pallas_call x1, Pallas kernels, input_gradient(): pl.pallas_call(input_kernel, out_shape=(jax.ShapeDtypeStruct((micro, tok,...  121 us
    pallas_call x1, Pallas kernels, project(): pl.pallas_call(project_kernel, out_shape=(jax.ShapeDtypeStruct((micro, to...  81.6 us
    pallas_call x1, Pallas kernels, weight_gradients(): pl.pallas_call(weights_kernel, out_shape=(jax.ShapeDtypeStruct((micro, to...  48.3 us
    pallas_call x1, Pallas kernels, attention_back(): pl.pallas_call(attend_backward, out_shape=jax.ShapeDtypeStruct((total, 4...  22.5 us
    pallas_call x1, Pallas kernels, attention_out(): pl.pallas_call(attend_forward, out_shape=(jax.ShapeDtypeStruct((total, 2...  18.9 us
    unnamed x46, local copies, waits for them, and re-layouts  17.7 us
  transfers between devices with their start and end apart: 4, of which 0 were waited for; matrix products, arithmetic and copies ran while one was open for 1% of the time, Pallas kernels for 46%

profile of v3, /device:TPU:0, one launch (start us, length us, event | category | flops | bytes accessed | tf_op | source)
XLA Modules:
  0.0 648.0 jit_solution(16076684367584053406)
XLA Ops:
  7.2 1.4 copy.36
  8.7 0.3 copy.37
  9.0 1.1 pad_maximum_fusion
  10.1 0.0 reduce-scatter.6.cloned.1.call-start
  10.2 0.2 reduce_window_sum.11
  10.4 0.2 convert_reduce_fusion
  10.6 0.2 select_reduce_fusion
  10.8 0.1 slice.15
  10.9 1.3 copy.35.start_ref
  12.3 0.5 and_select_fusion.first_ref
  12.8 0.2 broadcast_multiply_fusion
  13.0 2.1 negate_select_fusion
  15.1 81.6 %project.1 = (bf16[4,256,2048]{2,1,0:T(8,128)(2,1)S(1)}, f32[4,256,768]{2,1,0:T(8,128)S(1)}, bf16[8,256,512]{2,1,0:T(8,128)(2,1)S(1)}, bf16[2048,1024]{1,0:T(8,128)(2,1)}) custom-call(bf16[4,256,2048]{2,1,0:T(8,128)(2,1)} %input_ref.5, f32[1,2048]{1,0:T(1,128)S(1)} %bitcast.29, bf16[256,512]{1,0:T(8,128)(2,1)S(1)} %copy-done.13, ...), custom_call_target="tpu_custom_call" | custom-call | flops 20000000000 | bytes 40000000 | tf_op jit(solution)/shard_map/project/pallas_call | solution.py:875
  96.8 1.4 copy-done
  98.2 2.0 copy-done.1
  100.2 1.7 copy-done.2
  101.9 18.9 %attend_forward.1 = (bf16[2048,256]{1,0:T(8,128)(2,1)}, f32[2048,256]{1,0:T(8,128)}, f32[2048,2]{1,0:T(8,128)}) custom-call(s32[8]{0:T(128)} %and_select_fusion.first_ref, bf16[2048,512]{1,0:T(8,128)(2,1)} %bitcast.27, s32[2048,1]{1,0:T(8,128)} %copy.35.start_ref), custom_call_target="tpu_custom_call" | custom-call | tf_op jit(solution)/shard_map/attend_forward/pallas_call | solution.py:426
  120.8 308.0 %feed_forward.1 = (bf16[4,256,2048]{2,1,0:T(8,128)(2,1)}, bf16[4,256,1536]{2,1,0:T(8,128)(2,1)}, bf16[4,256,1536]{2,1,0:T(8,128)(2,1)}, bf16[4,256,1536]{2,1,0:T...) custom-call(bf16[8,256,256]{2,1,0:T(8,128)(2,1)} %bitcast.46, ...), custom_call_target="tpu_custom_call" | custom-call | flops 240000008192 | bytes 900000000 | tf_op jit(solution)/shard_map/feed_forward/pallas_call | solution.py:1577
  428.9 22.5 %attend_backward.1 = bf16[2048,512]{1,0:T(8,128)(2,1)} custom-call(s32[8]{0:T(128)} %and_select_fusion.first_ref, bf16[2048,512]{1,0:T(8,128)(2,1)} %bitcast.28, s32[2048,1]{1,0:T(8,128)} %copy.35.start_ref, bf16[2048,256]{1,0:T(8,128)(2,1)} %bitcast.37, f32[2048,256]{1,0:T(8,128)} %get-tuple-element.45.kept_ref, f32[2048,2]{1,0:T(8,128)} %get-tuple-element.46.log_ref), custom_call_target="tpu_custom_call" | custom-call | tf_op jit(solution)/shard_map/attend_backward/pallas_call | solution.py:454
  451.5 1.3 copy-done.7
  452.8 48.3 %weight_gradients.1 = (bf16[4,256,1024]{2,1,0:T(8,128)(2,1)S(1)}, bf16[4,256,1536]{2,1,0:T(8,128)(2,1)}, f32[2,128]{1,0:T(2,128)S(1)}) custom-call(bf16[8,256,512]{2,1,0:T(8,128)(2,1)} %bitcast.31, f32[4,256,768]{2,1,0:T(8,128)} %copy-done.2, bf16[4,256,2048]{2,1,0:T(8,128)(2,1)} %copy-done.1, bf16[4,256,512]{2,1,0:T(8,128)(2,1)S(1)} %copy-done.7, ...), custom_call_target="tpu_custom_call" | custom-call | flops 1000000000 | bytes 1000000 | tf_op jit(solution)/shard_map/weight_gradients/pallas_call | solution.py:1064
  501.2 0.5 reduce-scatter.8.cloned.1.call-update
  501.7 0.2 copy-done.9
  501.9 120.5 %input_gradient.1 = (f32[4,256,2048]{2,1,0:T(8,128)}, f32[8,2048]{1,0:T(8,128)S(1)}) custom-call(bf16[4,256,1024]{2,1,0:T(8,128)(2,1)S(1)} %get-tuple-element.51.back_ref, bf16[4,256,2048]{2,1,0:T(8,128)(2,1)} %input_ref.5, f32[4,256,2048]{2,1,0:T(8,128)} %get-tuple-element.52.middle_ref, f32[1,2048]{1,0:T(1,128)S(1)} %bitcast.30, ...), custom_call_target="tpu_custom_call" | custom-call | flops 1000000000 | bytes 1000000 | tf_op jit(solution)/shard_map/input_gradient/pallas_call | solution.py:1820
  622.4 0.5 slice_bitcast_fusion
  623.0 0.6 fusion.3
  623.6 2.4 widen_gate.1
  626.0 2.3 widen_attn.1
  628.3 3.2 widen_feed.1
  631.4 5.1 copy.42
  636.5 1.1 copy-done.16
  637.6 3.4 copy.43
  (53 shorter events, 0.4 us)
Async XLA Ops:
  7.2 1.8 copy-start.17
  7.2 3.0 copy-start.18
  7.2 113.6 %all-gather.3.cloned.1.call-start = ((), (), s32[]{:S(2)}) async-start(), calls=%async_computation.6 | async-start | bytes 9437184 | tf_op jit(solution)/shard_map/all_gather | solution.py:1911
  8.7 3.6 copy-start.19
  8.7 3.5 copy-start.20
  9.0 6.1 copy-start.8
  9.0 6.1 copy-start.13
  9.0 6.1 copy-start.14
  9.0 6.1 copy-start.15
  10.1 613.4 %reduce-scatter.6.cloned.1.call-start = ((), (), s32[]{:S(2)}) async-start(), calls=%async_computation.4 | async-start | bytes 3932160 | tf_op jit(solution)/shard_map/reduce_scatter | solution.py:1954
  12.3 84.5 %copy-start.11 = (f32[2,128]{1,0:T(2,128)}, f32[2,128]{1,0:T(2,128)S(1)}, u32[]{:S(2)}) copy-start(f32[2,128]{1,0:T(2,128)S(1)} %pad_maximum_fusion.2.head_gain_ref) | copy-start | bytes 3076
  15.1 81.7 %copy-start.3 = (f32[1024,128]{1,0:T(8,128)}, f32[1024,128]{1,0:T(8,128)S(1)}, u32[]{:S(2)}) copy-start(f32[1024,128]{1,0:T(8,128)S(1)} %get-tuple-element.69.sine_ref) | copy-start | bytes 1572868
  15.1 81.7 %copy-start.5 = (f32[1024,128]{1,0:T(8,128)}, f32[1024,128]{1,0:T(8,128)S(1)}, u32[]{:S(2)}) copy-start(f32[1024,128]{1,0:T(8,128)S(1)} %get-tuple-element.70.cosine_ref) | copy-start | bytes 1572868
  96.8 1.4 copy-start
  98.2 2.0 copy-start.1
  100.2 1.7 copy-start.2
  428.9 197.1 %reduce-scatter.4.cloned.1.call-start = ((), (), s32[]{:S(2)}) async-start(), calls=%async_computation.3 | async-start | bytes 3932160 | tf_op jit(solution)/shard_map/reduce_scatter | solution.py:1954
  428.9 22.6 %copy-start.4 = (f32[1024,128]{1,0:T(8,128)S(1)}, f32[1024,128]{1,0:T(8,128)}, u32[]{:S(2)}) copy-start(f32[1024,128]{1,0:T(8,128)} %copy-done.3) | copy-start | bytes 1572868
  428.9 22.6 %copy-start.6 = (f32[1024,128]{1,0:T(8,128)S(1)}, f32[1024,128]{1,0:T(8,128)}, u32[]{:S(2)}) copy-start(f32[1024,128]{1,0:T(8,128)} %copy-done.5) | copy-start | bytes 1572868
  428.9 22.6 %copy-start.12 = (f32[2,128]{1,0:T(2,128)S(1)}, f32[2,128]{1,0:T(2,128)}, u32[]{:S(2)}) copy-start(f32[2,128]{1,0:T(2,128)} %copy-done.11) | copy-start | bytes 3076
  451.5 1.3 copy-start.7
  501.1 127.1 %reduce-scatter.8.cloned.1.call-start = ((), (), s32[]{:S(2)}) async-start(), calls=%async_computation.5 | async-start | bytes 7864320 | tf_op jit(solution)/shard_map/reduce_scatter | solution.py:1954
  501.2 0.7 copy-start.9
  501.2 0.7 copy-start.10
  631.4 6.2 copy-start.16
Sparse Core Ops, SparseCore 0:
  10.3 90.3 all-gather.2
  429.0 68.0 reduce-scatter.5
  501.3 46.8 reduce-scatter.3
  551.0 70.1 reduce-scatter.7

commit v4 on v3

--- a/solution.py
+++ b/solution.py
@@ -311,56 +311,70 @@
 TN = (((0,), (0,)), ((), ()))
 
 
-def attend_forward(first_ref, qkv_ref, start_ref, mixed_ref, kept_ref, log_ref):
+def piece_starts(lengths_ref, micro, spot):
+    start = jnp.zeros_like(spot)
+    finish = jnp.int32(0)
+    for piece in range(NDOC - 1):
+        finish += lengths_ref[micro, piece]
+        start = jnp.where(spot >= finish, finish if piece < NDOC - 2 else spot, start)
+    return start
+
+
+def query_rows(lengths_ref, groups, step_q):
+    micro = lax.axis_index("wide") // groups
+    spot = lax.broadcasted_iota(jnp.int32, (BLOCK, 1), 0) + step_q * BLOCK
+    start = piece_starts(lengths_ref, micro, spot)
+    first = piece_starts(lengths_ref, micro, step_q * BLOCK) // BLOCK
+    spot = jnp.concatenate([spot, spot], axis=0)
+    start = jnp.concatenate([start, start], axis=0)
+    return spot, start, first
+
+
+def attend_forward(groups, lengths_ref, qkv_ref, mixed_ref, kept_ref, log_ref):
     step_q = pl.program_id(0)
     rows = pl.ds(step_q * BLOCK, BLOCK)
     factor = 1.0 / math.sqrt(HD)
     query = jnp.concatenate([qkv_ref[rows, 0:HD], qkv_ref[rows, HD : 2 * HD]], axis=0)
-    start = start_ref[rows, :]
-    start = jnp.concatenate([start, start], axis=0)
-    spot = lax.broadcasted_iota(jnp.int32, (BLOCK, 1), 0) + step_q * BLOCK
-    spot = jnp.concatenate([spot, spot], axis=0)
+    spot, start, first = query_rows(lengths_ref, groups, step_q)
 
     def one(step_k, carry):
-        highest, total, mixed = carry
+        total, mixed = carry
         cols = pl.ds(step_k * BLOCK, BLOCK)
         scores = lax.dot_general(
             query, qkv_ref[cols, 2 * HD : 3 * HD], NT, preferred_element_type=jnp.float32
         )
         key_spot = lax.broadcasted_iota(jnp.int32, (1, BLOCK), 1) + step_k * BLOCK
         fits = (key_spot >= start) & (key_spot <= spot)
-        scores = jnp.where(fits, scores * factor, -1e30)
-        fresh = jnp.maximum(highest, jnp.max(scores, axis=-1, keepdims=True))
-        shrink = jnp.exp(highest - fresh)
-        exponent = jnp.exp(scores - fresh)
-        total = total * shrink + jnp.sum(exponent, axis=-1, keepdims=True)
-        mixed = mixed * shrink + jnp.dot(
+        exponent = jnp.where(fits, jnp.exp(scores * factor), 0.0)
+        for half in range(BLOCK // HD):
+            total += exponent[:, half * HD : (half + 1) * HD]
+        mixed += jnp.dot(
             exponent.astype(jnp.bfloat16),
             qkv_ref[cols, 3 * HD : 4 * HD],
             preferred_element_type=jnp.float32,
         )
-        return (fresh, total, mixed)
-
-    highest, total, mixed = lax.fori_loop(
-        first_ref[step_q],
+        return (total, mixed)
+
+    total, mixed = lax.fori_loop(
+        first,
         step_q + 1,
         one,
         (
-            jnp.full((2 * BLOCK, 1), -1e30, jnp.float32),
-            jnp.zeros((2 * BLOCK, 1), jnp.float32),
+            jnp.zeros((2 * BLOCK, HD), jnp.float32),
             jnp.zeros((2 * BLOCK, HD), jnp.float32),
         ),
     )
+    total = jnp.sum(total, axis=-1, keepdims=True)
     mixed = mixed / total
     mixed = jnp.concatenate([mixed[:BLOCK], mixed[BLOCK:]], axis=1)
     mixed_ref[...] = mixed.astype(jnp.bfloat16)
     kept_ref[...] = mixed
-    log_total = highest + jnp.log(total)
+    log_total = jnp.log(total)
     log_ref[...] = jnp.concatenate([log_total[:BLOCK], log_total[BLOCK:]], axis=1)
 
 
 def attend_backward(
-    first_ref, qkv_ref, start_ref, grad_ref, kept_ref, log_ref, back_ref, key_sum, value_sum
+    groups, lengths_ref, qkv_ref, grad_ref, kept_ref, log_ref, back_ref, key_sum, value_sum
 ):
     step_q = pl.program_id(0)
     rows = pl.ds(step_q * BLOCK, BLOCK)
@@ -376,10 +390,7 @@
     kept = jnp.concatenate([kept_ref[:, 0:HD], kept_ref[:, HD : 2 * HD]], axis=0)
     log_total = jnp.concatenate([log_ref[:, 0:1], log_ref[:, 1:2]], axis=0)
     weighted = jnp.sum(grad.astype(jnp.float32) * kept, axis=-1, keepdims=True)
-    start = start_ref[rows, :]
-    start = jnp.concatenate([start, start], axis=0)
-    spot = lax.broadcasted_iota(jnp.int32, (BLOCK, 1), 0) + step_q * BLOCK
-    spot = jnp.concatenate([spot, spot], axis=0)
+    spot, start, first = query_rows(lengths_ref, groups, step_q)
 
     def one(step_k, query_sum):
         cols = pl.ds(step_k * BLOCK, BLOCK)
@@ -400,9 +411,7 @@
         )
         return query_sum + jnp.dot(grad_scores, key, preferred_element_type=jnp.float32)
 
-    query_sum = lax.fori_loop(
-        first_ref[step_q], step_q + 1, one, jnp.zeros((2 * BLOCK, HD), jnp.float32)
-    )
+    query_sum = lax.fori_loop(first, step_q + 1, one, jnp.zeros((2 * BLOCK, HD), jnp.float32))
     query_sum = (query_sum * factor).astype(jnp.bfloat16)
     back_ref[rows, 0:HD] = query_sum[:BLOCK]
     back_ref[rows, HD : 2 * HD] = query_sum[BLOCK:]
@@ -413,18 +422,11 @@
         back_ref[:, 3 * HD : 4 * HD] = value_sum[...].astype(jnp.bfloat16)
 
 
-def row_starts(lengths_row, total):
-    segment, place = layout(lengths_row, total)
-    positions = jnp.arange(total, dtype=jnp.int32)
-    starts = jnp.where(segment == NDOC - 1, positions, positions - place)
-    return (starts, place)
-
-
-def attention_out(qkv, starts, first):
+def attention_out(qkv, lengths, groups):
     total = qkv.shape[0]
-    whole = lambda i, *_: (0, 0)
+    block = lambda i, *_: (i, 0)
     return pl.pallas_call(
-        attend_forward,
+        functools.partial(attend_forward, groups),
         out_shape=(
             jax.ShapeDtypeStruct((total, 2 * HD), jnp.bfloat16),
             jax.ShapeDtypeStruct((total, 2 * HD), jnp.float32),
@@ -433,33 +435,29 @@
         grid_spec=pltpu.PrefetchScalarGridSpec(
             num_scalar_prefetch=1,
             grid=(total // BLOCK,),
-            in_specs=[
-                pl.BlockSpec((total, 4 * HD), whole),
-                pl.BlockSpec((total, 1), whole),
-            ],
+            in_specs=[pl.BlockSpec((total, 4 * HD), lambda i, *_: (0, 0))],
             out_specs=[
-                pl.BlockSpec((BLOCK, 2 * HD), lambda i, *_: (i, 0)),
-                pl.BlockSpec((BLOCK, 2 * HD), lambda i, *_: (i, 0)),
-                pl.BlockSpec((BLOCK, 2), lambda i, *_: (i, 0)),
+                pl.BlockSpec((BLOCK, 2 * HD), block),
+                pl.BlockSpec((BLOCK, 2 * HD), block),
+                pl.BlockSpec((BLOCK, 2), block),
             ],
         ),
         name="attend_forward",
-    )(first, qkv, starts[:, None])
-
-
-def attention_back(qkv, starts, first, grad, kept, log_total):
+    )(lengths, qkv)
+
+
+def attention_back(qkv, lengths, groups, grad, kept, log_total):
     total = qkv.shape[0]
     whole = lambda i, *_: (0, 0)
     block = lambda i, *_: (i, 0)
     return pl.pallas_call(
-        attend_backward,
+        functools.partial(attend_backward, groups),
         out_shape=jax.ShapeDtypeStruct((total, 4 * HD), jnp.bfloat16),
         grid_spec=pltpu.PrefetchScalarGridSpec(
             num_scalar_prefetch=1,
             grid=(total // BLOCK,),
             in_specs=[
                 pl.BlockSpec((total, 4 * HD), whole),
-                pl.BlockSpec((total, 1), whole),
                 pl.BlockSpec((BLOCK, 2 * HD), block),
                 pl.BlockSpec((BLOCK, 2 * HD), block),
                 pl.BlockSpec((BLOCK, 2), block),
@@ -471,7 +469,7 @@
             ],
         ),
         name="attend_backward",
-    )(first, qkv, starts[:, None], grad, kept, log_total)
+    )(lengths, qkv, grad, kept, log_total)
 
 
 def dot_f32(left, right, dims=(((1,), (0,)), ((), ()))):
@@ -480,6 +478,7 @@
 
 SUB = 64
 RING = 8
+STRIP = 16
 AHEAD = 3
 GAIN_TICKS = (0, 2, 4, 6, 11, 14, 17)
 LANES = 512
@@ -560,18 +559,29 @@
         @pl.when(self.is_mid & (k < self.count))
         def _():
             self.to_inner(k).wait_recv()
-            self.own[k] = (
-                self.own[k].astype(jnp.float32) + self.landed[k].astype(jnp.float32)
-            ).astype(jnp.bfloat16)
+
+            @pl.loop(0, SUB // STRIP)
+            def _(i):
+                rows = pl.ds(pl.multiple_of(i * STRIP, STRIP), STRIP)
+                self.own[k, rows] = (
+                    self.own[k, rows].astype(jnp.float32) + self.landed[k, rows].astype(jnp.float32)
+                ).astype(jnp.bfloat16)
+
             self.to_other(k).start()
 
         @pl.when(self.is_mid & (k >= 2) & (k < self.count + 2))
         def _():
             j = k - 2
             self.to_other(j).wait_recv()
-            self.landed[j] = (
-                self.own[j].astype(jnp.float32) + self.cross[j % RING].astype(jnp.float32)
-            ).astype(jnp.bfloat16)
+
+            @pl.loop(0, SUB // STRIP)
+            def _(i):
+                rows = pl.ds(pl.multiple_of(i * STRIP, STRIP), STRIP)
+                self.landed[j, rows] = (
+                    self.own[j, rows].astype(jnp.float32)
+                    + self.cross[j % RING, rows].astype(jnp.float32)
+                ).astype(jnp.bfloat16)
+
             self.to_outer(j).start()
 
         @pl.when(self.is_end & (k >= 4) & (k < self.count + 4))
@@ -747,13 +757,14 @@
     query_w,
     key_w,
     value_w,
-    cosine_ref,
-    sine_ref,
+    lengths_ref,
     head_gain_ref,
     hidden_out,
     raw_out,
     packed_out,
     weight_out,
+    cosine_ref,
+    sine_ref,
     rows_v,
     weight_v,
     hidden_v,
@@ -808,6 +819,25 @@
         hidden_v[m] = (rows * scale * gain_ref[...]).astype(jnp.bfloat16)
 
     hidden_copy.start()
+    lane = lax.broadcasted_iota(jnp.int32, (1, HD), 1)
+    frequency = jnp.exp(
+        -math.log(THETA) * (2 * (lane % (HD // 2))).astype(jnp.float32) / HD
+    )
+    sign = jnp.where(lane < HD // 2, -1.0, 1.0)
+    token = lax.broadcasted_iota(jnp.int32, (tok, 1), 0) + spot * tok
+
+    @pl.loop(0, micro)
+    def _(m):
+        start = jnp.zeros_like(token)
+        finish = jnp.int32(0)
+        for piece_index in range(NDOC - 1):
+            finish += lengths_ref[m, piece_index]
+            start = jnp.where(token >= finish, finish, start)
+        turning = (token - start).astype(jnp.float32) * frequency
+        span = pl.ds(pl.multiple_of(m * tok, tok), tok)
+        cosine_ref[span, :] = jnp.cos(turning)
+        sine_ref[span, :] = jnp.sin(turning) * sign
+
     for p in range(3):
         gather.second(p)
     for p in range(3):
@@ -817,20 +847,24 @@
     weight_copy = pltpu.make_async_copy(weight_v, weight_out, load_sem.at[1])
     weight_copy.start()
 
-    def keeps(step, m):
-        return [pltpu.make_async_copy(raw_v.at[step % 2], raw_out.at[m], keep_sem.at[step % 2])]
-
-    kept = []
-    for step in range(micro):
+    def turn(step):
         far = micro - 1 - step
         own = spot // groups
-        if micro == 4:
-            m = lax.rem(own + far % 2, 2) + 2 * lax.rem(own // 2 + far // 2, 2)
-        else:
-            m = lax.rem(own + far, micro)
-        if step >= 2:
-            for copy in kept[step - 2]:
-                copy.wait()
+        return (own + far) % 2 + 2 * ((own // 2 + far // 2) % 2)
+
+    def keep(step):
+        return pltpu.make_async_copy(
+            raw_v.at[step % 2], raw_out.at[turn(step)], keep_sem.at[step % 2]
+        )
+
+    @pl.loop(0, micro)
+    def _(step):
+        m = turn(step)
+
+        @pl.when(step >= 2)
+        def _():
+            keep(step - 2).wait()
+
         heads_all = dot_f32(hidden_v[m], weight_v[...])
         span = pl.ds(pl.multiple_of(m * tok, tok), tok)
         cosine, sine = cosine_ref[span, :], sine_ref[span, :]
@@ -848,11 +882,10 @@
                 jnp.bfloat16
             )
             swap.send(m * groups + g)
-        kept.append(keeps(step, m))
-        for copy in kept[step]:
-            copy.start()
-    for copy in kept[micro - 2] + kept[micro - 1]:
-        copy.wait()
+        keep(step).start()
+
+    keep(micro - 2).wait()
+    keep(micro - 1).wait()
 
     @pl.loop(0, width)
     def _(d):
@@ -864,7 +897,7 @@
     weight_copy.wait()
 
 
-def project(layer_input, gain_attn, weights, cosine, sine, head_gains, width):
+def project(layer_input, gain_attn, weights, lengths, head_gains, width):
     micro, tok, model = layer_input.shape
     groups = width // micro
     low = jnp.bfloat16
@@ -879,9 +912,12 @@
             jax.ShapeDtypeStruct((micro, tok, raw), jnp.float32),
             jax.ShapeDtypeStruct((width, tok, 4 * HD), low),
             jax.ShapeDtypeStruct((model, columns), low),
+            jax.ShapeDtypeStruct((micro * tok, HD), jnp.float32),
+            jax.ShapeDtypeStruct((micro * tok, HD), jnp.float32),
         ),
-        in_specs=[anywhere, inside, anywhere, anywhere, anywhere, inside, inside, inside],
-        out_specs=[anywhere] * 4,
+        in_specs=[anywhere, inside, anywhere, anywhere, anywhere]
+        + [pl.BlockSpec(memory_space=pltpu.SMEM), inside],
+        out_specs=[anywhere] * 4 + [inside] * 2,
         scratch_shapes=[
             pltpu.VMEM((micro, tok, model), low),
             pltpu.VMEM((model, columns), low),
@@ -903,7 +939,7 @@
             flops=20_000_000_000, bytes_accessed=40_000_000, transcendentals=0
         ),
         name="project",
-    )(layer_input, gain_attn[None, :], *weights, cosine, sine, head_gains)
+    )(layer_input, gain_attn[None, :], *weights, lengths, head_gains)
 
 
 def weights_kernel(
@@ -912,12 +948,22 @@
     hidden_ref,
     mixed_ref,
     low_ref,
+    late_ref,
+    input_ref,
     cosine_ref,
     sine_ref,
     head_gain_ref,
     back_out,
     grad_out,
     gain_out,
+    output_out,
+    own,
+    landed,
+    cross,
+    out_sem,
+    relay_sem,
+    return_sem,
+    cross_sem,
     land_v,
     raw_v,
     hidden_v,
@@ -926,12 +972,15 @@
     back_v,
     grad_v,
     pair_v,
+    middle_v,
+    rows_v,
     load_sem,
     back_sem,
     tile_sem,
     send_sem,
     land_sem,
     pair_sems,
+    late_sem,
 ):
     micro, tok, heads_in = mixed_ref.shape
     width = back_ref.shape[0]
@@ -949,12 +998,22 @@
         pltpu.make_async_copy(raw_ref, raw_v, load_sem.at[2]),
         pltpu.make_async_copy(hidden_ref, hidden_v, load_sem.at[3]),
     ]
-    for copy in loads:
+    per = tok // SUB
+    relay = Relay(per, own, landed, cross, (out_sem, relay_sem, return_sem, cross_sem))
+    late_loads = [
+        pltpu.make_async_copy(late_ref.at[0], own, late_sem.at[0]),
+        pltpu.make_async_copy(late_ref.at[1], middle_v, late_sem.at[1]),
+        pltpu.make_async_copy(input_ref.at[micro - 1], rows_v, late_sem.at[2]),
+    ]
+    for copy in late_loads + loads:
         copy.start()
-    greet_wide(width)
+    relay.greet(wide_peers(width))
     spot = lax.axis_index("wide")
     for step in range(width - 1, -1, -1):
         swap.send(lax.rem(spot + step, width))
+    for copy in late_loads:
+        copy.wait()
+    relay.send(0, per)
     loads[0].wait()
     loads[1].wait()
     mixed_all = mixed_v[...].reshape(count, heads_in)
@@ -968,6 +1027,9 @@
                 ] = part[b * piece : (b + 1) * piece, i * piece : (i + 1) * piece]
     loads[2].wait()
     gain_out[...] = jnp.zeros_like(gain_out)
+
+    for k in range(4):
+        relay.tick(k)
 
     @pl.loop(0, width)
     def _(d):
@@ -999,6 +1061,10 @@
             back_v[m, :, first : first + HD] = land_v[m * groups + g, :, 3 * HD :]
         back_copy(m).start()
 
+        @pl.when(m % 2 == 1)
+        def _():
+            relay.tick(4 + m // 2)
+
     loads[3].wait()
 
     core = lax.rem(spot, 2)
@@ -1026,6 +1092,20 @@
         i = 2 * c + 1 - core
         grad_v[i, :, 0 : 2 * heads_in] = tile(i).astype(jnp.bfloat16)
         pair_copy(c).start()
+
+        @pl.when(c % 2 == 1)
+        def _():
+            relay.tick(6 + c // 2)
+
+    output_copy = pltpu.make_async_copy(rows_v, output_out, late_sem.at[3])
+    for r in range(per):
+        span = slice(r * SUB, (r + 1) * SUB)
+        rows_v[span, :] = (
+            rows_v[span, :].astype(jnp.float32)
+            + middle_v[r].astype(jnp.float32)
+            + landed[r].astype(jnp.float32)
+        ).astype(jnp.bfloat16)
+    output_copy.start()
 
     @pl.loop(0, width // 2)
     def _(c):
@@ -1052,9 +1132,13 @@
 
     for m in range(micro):
         back_copy(m).wait()
-
-
-def weight_gradients(back, raw, hidden, mixed, middle_low, cosine, sine, head_gains):
+    output_copy.wait()
+    relay.drain(0)
+
+
+def weight_gradients(
+    back, raw, hidden, mixed, middle_low, late, layer_input, cosine, sine, head_gains
+):
     micro, tok, heads_in = mixed.shape
     width = back.shape[0]
     model = hidden.shape[2]
@@ -1067,10 +1151,12 @@
             jax.ShapeDtypeStruct((micro, tok, 2 * heads_in), low),
             jax.ShapeDtypeStruct((width // 2, model // width, 3 * heads_in), low),
             jax.ShapeDtypeStruct((2, HD), jnp.float32),
+            jax.ShapeDtypeStruct((tok, model), low),
         ),
-        in_specs=[anywhere] * 5 + [inside] * 3,
-        out_specs=[anywhere, anywhere, inside],
-        scratch_shapes=[
+        in_specs=[anywhere] * 7 + [inside] * 3,
+        out_specs=[anywhere, anywhere, inside, anywhere],
+        scratch_shapes=relay_scratch(tok // SUB, model)
+        + [
             pltpu.VMEM(back.shape, low),
             pltpu.VMEM(raw.shape, jnp.float32),
             pltpu.VMEM(hidden.shape, low),
@@ -1079,12 +1165,15 @@
             pltpu.VMEM((micro, tok, 2 * heads_in), low),
             pltpu.VMEM((width, model // width, 3 * heads_in), low),
             pltpu.VMEM((width // 2, model // width, 3 * heads_in), low),
+            pltpu.VMEM((tok // SUB, SUB, model), low),
+            pltpu.VMEM((tok, model), low),
             pltpu.SemaphoreType.DMA((4,)),
             pltpu.SemaphoreType.DMA((micro,)),
             pltpu.SemaphoreType.DMA((width // 2,)),
             pltpu.SemaphoreType.DMA((width,)),
             pltpu.SemaphoreType.DMA((width,)),
             pltpu.SemaphoreType.DMA((2, width // 2)),
+            pltpu.SemaphoreType.DMA((4,)),
         ],
         compiler_params=pltpu.CompilerParams(
             collective_id=3, has_side_effects=True, vmem_limit_bytes=48 << 20
@@ -1093,12 +1182,12 @@
             flops=1_000_000_000, bytes_accessed=1_000_000, transcendentals=0
         ),
         name="weight_gradients",
-    )(back, raw, hidden, mixed, middle_low, cosine, sine, head_gains)
-
-
-def relay_scratch(count, model):
+    )(back, raw, hidden, mixed, middle_low, late, layer_input, cosine, sine, head_gains)
+
+
+def relay_scratch(count, model, extra=0):
     return [
-        pltpu.VMEM((count, SUB, model), jnp.bfloat16),
+        pltpu.VMEM((count + extra, SUB, model), jnp.bfloat16),
         pltpu.VMEM((count, SUB, model), jnp.bfloat16),
         pltpu.VMEM((RING, SUB, model), jnp.bfloat16),
         pltpu.SemaphoreType.DMA((count,)),
@@ -1128,6 +1217,7 @@
     weight_out,
     heads_out,
     early_out,
+    late_out,
     own,
     landed,
     cross,
@@ -1163,6 +1253,7 @@
     part_land,
     pair_sems,
     credit,
+    late_sem,
 ):
     micro, tok, model = input_ref.shape
     width, _, piece = pack_ref.shape
@@ -1172,7 +1263,8 @@
     hid = gate_v.shape[1]
     count = micro * tok
     blocks = hid // piece
-    relay = Relay(3 * micro * per, own, landed, cross, (out_sem, land_sem, back_sem, cross_sem))
+    late = 3 * micro * per - per
+    relay = Relay(late, own, landed, cross, (out_sem, land_sem, back_sem, cross_sem))
     n_up = hid // LANES
     n_down = model // LANES
     slots = n_up + n_down
@@ -1326,27 +1418,32 @@
             for copy in stage_copies(m - 1):
                 copy.wait()
 
-        for r in range(per):
-            span = pl.ds(r * SUB, SUB)
+        @pl.loop(0, per)
+        def _(r):
+            span = pl.ds(pl.multiple_of(r * SUB, SUB), SUB)
             middle = rows_v[slot, span, :].astype(jnp.float32) + landed[m * per + r].astype(
                 jnp.float32
             )
             scale = lax.rsqrt(jnp.mean(middle * middle, axis=-1, keepdims=True) + EPSILON)
             scale_v[span, :] = scale
             hidden_v[span, :] = (middle * scale * gain_ref[...]).astype(jnp.bfloat16)
+
         hidden_copy(m).start()
-        for j in range(n_up):
+
+        @pl.loop(0, n_up)
+        def _(j):
             relay.tick(first_ticks + slots * m + j)
-
-            @pl.when(m == 0)
-            def _():
-                if j == 0:
-                    both(gather.second, 2)
-                if j + 1 < n_up:
-                    both(gather.third, j + 1)
-                both(gather.fourth, j)
-
-            cols = pl.ds(j * LANES, LANES)
+            for turn in range(n_up):
+
+                @pl.when((m == 0) & (j == turn))
+                def _():
+                    if turn == 0:
+                        both(gather.second, 2)
+                    if turn + 1 < n_up:
+                        both(gather.third, turn + 1)
+                    both(gather.fourth, turn)
+
+            cols = pl.ds(pl.multiple_of(j * LANES, LANES), LANES)
             gate = dot_f32(hidden_v[...], gate_v[:, cols])
             up_proj = dot_f32(hidden_v[...], up_v[:, cols])
             grad_active = dot_f32(grads_v[slot], down_v[cols, :], NT)
@@ -1359,9 +1456,11 @@
             stage_v[2, :, cols] = (grad_active * silu).astype(jnp.bfloat16)
         for copy in stage_copies(m):
             copy.start()
-        for n in range(n_down):
+
+        @pl.loop(0, n_down)
+        def _(n):
             relay.tick(first_ticks + slots * m + n_up + n)
-            cols = pl.ds(n * LANES, LANES)
+            cols = pl.ds(pl.multiple_of(n * LANES, LANES), LANES)
             back = dot_f32(stage_v[1], gate_v[cols, :], NT) + dot_f32(
                 stage_v[2], up_v[cols, :], NT
             )
@@ -1377,11 +1476,24 @@
                 ) * scale_v[pl.ds(r * SUB, SUB), :]
                 gain_sum += jnp.sum(back[part] * unit, axis=0, keepdims=True)
             gain_out[:, cols] += gain_sum
-        relay.send(base + 2 * per * m, 2 * per)
+
+        relay.send(base + 2 * per * m, per)
+
+        @pl.when(m < micro - 1)
+        def _():
+            relay.send(base + 2 * per * m + per, per)
 
     hidden_copy(micro - 1).wait()
     for copy in stage_copies(micro - 1):
         copy.wait()
+    late_copies = [
+        pltpu.make_async_copy(own.at[pl.ds(late, per)], late_out.at[0], late_sem.at[0]),
+        pltpu.make_async_copy(
+            landed.at[pl.ds((micro - 1) * per, per)], late_out.at[1], late_sem.at[1]
+        ),
+    ]
+    for copy in late_copies:
+        copy.start()
 
     gather.drain()
     core = lax.rem(spot, 2)
@@ -1468,11 +1580,13 @@
         return [
             pltpu.make_async_copy(middle_v, middle_out.at[m], final_sem.at[0]),
             pltpu.make_async_copy(hidden_v, low_out.at[m], final_sem.at[1]),
-            pltpu.make_async_copy(output_v, output_out.at[m], final_sem.at[2]),
         ]
 
+    def output_copy(m):
+        return pltpu.make_async_copy(output_v, output_out.at[m], final_sem.at[2])
+
     last_ticks = first_ticks + slots * micro
-    rest = 3 * micro * per + 4 - last_ticks
+    rest = late + 4 - last_ticks
     turns = rest // micro
 
     @pl.loop(0, micro)
@@ -1488,6 +1602,7 @@
         def _():
             for copy in final_copies(m - 1):
                 copy.wait()
+            output_copy(m - 1).wait()
 
         @pl.when(m == 0)
         def _():
@@ -1498,13 +1613,18 @@
         relay.tick(last_ticks + turns * m)
         give(m, 0)
         give(m, 1)
-        relay.tick(last_ticks + turns * m + 1)
         give(m, 2)
         pl.semaphore_wait(credit, 1)
         for q in range(3):
             pair_copy(q).start()
-        for r in range(per):
-            span = pl.ds(r * SUB, SUB)
+        relay.tick(last_ticks + turns * m + 1)
+        keep(m, 0)
+        keep(m, 1)
+        relay.tick(last_ticks + turns * m + 2)
+
+        @pl.loop(0, per)
+        def _(r):
+            span = pl.ds(pl.multiple_of(r * SUB, SUB), SUB)
             middle = rows_v[slot, span, :].astype(jnp.float32) + landed[m * per + r].astype(
                 jnp.float32
             )
@@ -1516,6 +1636,7 @@
             )
             middle_v[span, :] = grad_middle
             hidden_v[span, :] = grad_middle.astype(jnp.bfloat16)
+
         @pl.when(m >= 2)
         def _():
             for g in range(groups):
@@ -1524,20 +1645,23 @@
         mixback_v[m % 2] = dot_f32(hidden_v[...], out_v[...], NT).astype(jnp.bfloat16)
         for g in range(groups):
             behind.send(m * groups + g)
-        relay.tick(last_ticks + turns * m + 2)
-        keep(m, 0)
-        keep(m, 1)
-        relay.tick(last_ticks + turns * m + 3)
-        keep(m, 2)
-        for r in range(per):
-            span = pl.ds(r * SUB, SUB)
-            output_v[span, :] = (
-                rows_v[slot, span, :].astype(jnp.float32)
-                + landed[m * per + r].astype(jnp.float32)
-                + landed[base + 2 * per * m + per + r].astype(jnp.float32)
-            ).astype(jnp.bfloat16)
+
+        @pl.when(m < micro - 1)
+        def _():
+            @pl.loop(0, per)
+            def _(r):
+                span = pl.ds(pl.multiple_of(r * SUB, SUB), SUB)
+                output_v[span, :] = (
+                    rows_v[slot, span, :].astype(jnp.float32)
+                    + landed[m * per + r].astype(jnp.float32)
+                    + landed[base + 2 * per * m + per + r].astype(jnp.float32)
+                ).astype(jnp.bfloat16)
+
+            output_copy(m).start()
+
         for copy in final_copies(m):
             copy.start()
+        keep(m, 2)
         for q in range(3):
             tile_copy(m, q).wait()
 
@@ -1545,6 +1669,8 @@
         def _():
             offer()
 
+    for copy in late_copies:
+        copy.wait()
     for copy in final_copies(micro - 1):
         copy.wait()
     for q in range(3):
@@ -1572,6 +1698,7 @@
     groups = width // micro
     low = jnp.bfloat16
     count = 3 * micro * (tok // SUB)
+    late = tok // SUB
     anywhere = pl.BlockSpec(memory_space=pl.ANY)
     inside = pl.BlockSpec(memory_space=pltpu.VMEM)
     return pl.pallas_call(
@@ -1581,7 +1708,7 @@
             jax.ShapeDtypeStruct((micro, tok, hid), low),
             jax.ShapeDtypeStruct((micro, tok, hid), low),
             jax.ShapeDtypeStruct((micro, tok, hid), low),
-            jax.ShapeDtypeStruct((micro, tok, model), low),
+            jax.ShapeDtypeStruct((micro - 1, tok, model), low),
             jax.ShapeDtypeStruct((micro, tok, model), jnp.float32),
             jax.ShapeDtypeStruct((micro, tok, model), low),
             jax.ShapeDtypeStruct((width, tok, 2 * HD), low),
@@ -1589,10 +1716,11 @@
             jax.ShapeDtypeStruct((width // 2, 2, piece, hid), low),
             jax.ShapeDtypeStruct((micro, tok, heads_in), low),
             jax.ShapeDtypeStruct((width // 2, piece, hid), low),
+            jax.ShapeDtypeStruct((2, late, SUB, model), low),
         ),
         in_specs=[anywhere] * 3 + [inside, anywhere, anywhere, anywhere],
-        out_specs=[anywhere] * 8 + [inside] + [anywhere] * 3,
-        scratch_shapes=relay_scratch(count, model)
+        out_specs=[anywhere] * 8 + [inside] + [anywhere] * 4,
+        scratch_shapes=relay_scratch(count - late, model, late)
         + [
             pltpu.VMEM((heads_in, model), low),
             pltpu.VMEM((model, hid), low),
@@ -1622,6 +1750,7 @@
             pltpu.SemaphoreType.DMA((parts, 10)),
             pltpu.SemaphoreType.DMA((2, 3)),
             pltpu.SemaphoreType.REGULAR,
+            pltpu.SemaphoreType.DMA((2,)),
         ],
         compiler_params=pltpu.CompilerParams(
             collective_id=0, has_side_effects=True, vmem_limit_bytes=67043328
@@ -1854,31 +1983,77 @@
     gate_ref[...] = rows_ref[...].astype(jnp.float32)
 
 
-def widen_feed(rows_ref, up_ref, down_ref):
-    piece = up_ref.shape[0]
-    up_ref[...] = rows_ref[0:piece, :].astype(jnp.float32)
-    for j in range(down_ref.shape[0] // piece):
-        span = slice(j * piece, (j + 1) * piece)
-        down_ref[span, :] = rows_ref[piece:, span].astype(jnp.float32)
-
-
-def widen_attn(rows_ref, query_ref, key_ref, value_ref, out_ref):
-    piece = query_ref.shape[0]
+def finish_kernel(
+    input_rows,
+    first_rows,
+    last_rows,
+    up_rows,
+    down_rows,
+    attn_rows,
+    out_rows,
+    grad_ref,
+    output_ref,
+    up_ref,
+    down_ref,
+    query_ref,
+    key_ref,
+    value_ref,
+    out_ref,
+):
+    grad_ref[...] = input_rows[...]
+    inside = pl.program_id(0) < pl.num_programs(0) * 3 // 4
+    output_ref[...] = jnp.where(inside, first_rows[...], last_rows[...])
+    up_ref[...] = up_rows[...].astype(jnp.float32)
+    down_ref[...] = down_rows[...].astype(jnp.float32)
     first = 0
     for target in (query_ref, key_ref, value_ref):
-        target[...] = rows_ref[:, first : first + target.shape[1]].astype(jnp.float32)
+        target[...] = attn_rows[:, first : first + target.shape[1]].astype(jnp.float32)
         first += target.shape[1]
-    for j in range(out_ref.shape[0] // piece):
-        part = rows_ref[:, first + j * piece : first + (j + 1) * piece]
-        out_ref[j * piece : (j + 1) * piece, :] = part.astype(jnp.float32)
-
-
-def widen(kernel, rows, shapes):
+    out_ref[...] = out_rows[...].astype(jnp.float32)
+
+
+def finish(grad_input, first, last, feed, attn, columns):
+    steps = 8
+    rows, model = grad_input.shape
+    piece, hid = feed.shape[0] // 2, feed.shape[1]
+    part = rows // steps
+    early = first.shape[0] // part - 1
+    strip = piece // steps
+    blocks = hid // piece
+    heads = sum(columns) // piece
+    rest = (attn.shape[1] - sum(columns)) // piece
+    f32 = jnp.float32
+    row = lambda i: (i, 0)
     return pl.pallas_call(
-        kernel,
-        out_shape=tuple(jax.ShapeDtypeStruct(shape, jnp.float32) for shape in shapes),
-        name=kernel.__name__,
-    )(rows)
+        finish_kernel,
+        grid=(steps,),
+        out_shape=(
+            jax.ShapeDtypeStruct((rows, model), f32),
+            jax.ShapeDtypeStruct((rows, model), jnp.bfloat16),
+            jax.ShapeDtypeStruct((piece, hid), f32),
+            jax.ShapeDtypeStruct((hid, piece), f32),
+        )
+        + tuple(jax.ShapeDtypeStruct((piece, column), f32) for column in columns)
+        + (jax.ShapeDtypeStruct((rest * piece, piece), f32),),
+        in_specs=[
+            pl.BlockSpec((part, model), row),
+            pl.BlockSpec((part, model), lambda i: (jnp.minimum(i, early), 0)),
+            pl.BlockSpec((part, model), lambda i: (jnp.maximum(i - early - 1, 0), 0)),
+            pl.BlockSpec((strip, hid), row),
+            pl.BlockSpec((piece, piece), lambda i: (1, jnp.minimum(i, blocks - 1))),
+            pl.BlockSpec((strip, attn.shape[1]), row),
+            pl.BlockSpec((piece, piece), lambda i: (0, heads + jnp.minimum(i, rest - 1))),
+        ],
+        out_specs=[
+            pl.BlockSpec((part, model), row),
+            pl.BlockSpec((part, model), row),
+            pl.BlockSpec((strip, hid), row),
+            pl.BlockSpec((piece, piece), lambda i: (jnp.minimum(i, blocks - 1), 0)),
+        ]
+        + [pl.BlockSpec((strip, column), row) for column in columns]
+        + [pl.BlockSpec((piece, piece), lambda i: (jnp.minimum(i, rest - 1), 0))],
+        name="finish",
+    )(grad_input, first, last, feed, feed, attn, attn)
 
 
 def local_batched(
@@ -1901,8 +2076,6 @@
     width = lax.axis_size("wide")
     groups = w_key.shape[1] // HD
     total = tok_rows * width
-    count = micro * tok_rows
-    me = lax.axis_index("wide")
     piece = w_out.shape[1]
 
     def stacked(weight):
@@ -1912,19 +2085,12 @@
         jnp.concatenate([w_out, stacked(w_gate)], axis=0), "wide", axis=0
     )
 
-    starts, places = jax.vmap(lambda row: row_starts(row, total))(lengths)
-    my_places = lax.dynamic_slice_in_dim(places, me * tok_rows, tok_rows, axis=1)
-    cosine, sine = angles(my_places.reshape(count))
-    sine = jnp.where(jnp.arange(HD) < HD // 2, -sine, sine)
     head_gains = jnp.stack([gain_query, gain_key])
-    my_starts = lax.dynamic_index_in_dim(starts, me // groups, axis=0, keepdims=False)
-    my_first = my_starts[::BLOCK] // BLOCK
-
-    hidden_one, raw, packed, w_qkv = project(
-        layer_input, gain_attn, (w_query, w_key, w_value), cosine, sine, head_gains, width
+    hidden_one, raw, packed, w_qkv, cosine, sine = project(
+        layer_input, gain_attn, (w_query, w_key, w_value), lengths, head_gains, width
     )
     packed = packed.reshape(total, 4 * HD)
-    mixed, kept, log_total = attention_out(packed, my_starts, my_first)
+    mixed, kept, log_total = attention_out(packed, lengths, groups)
     (
         _,
         _,
@@ -1938,6 +2104,7 @@
         feed_grads,
         mixed_low,
         gate_grads,
+        late,
     ) = feed_forward(
         mixed.reshape(width, tok_rows, 2 * HD),
         layer_input,
@@ -1956,14 +2123,16 @@
         )
 
     back = attention_back(
-        packed, my_starts, my_first, grad_mixed.reshape(total, 2 * HD), kept, log_total
-    )
-    qkv_back, attn_grads, gain_heads = weight_gradients(
+        packed, lengths, groups, grad_mixed.reshape(total, 2 * HD), kept, log_total
+    )
+    qkv_back, attn_grads, gain_heads, last_output = weight_gradients(
         back.reshape(width, tok_rows, 4 * HD),
         raw,
         hidden_one,
         mixed_low,
         middle_low,
+        late,
+        layer_input,
         cosine,
         sine,
         head_gains,
@@ -1976,14 +2145,31 @@
         qkv_back, layer_input, grad_middle, gain_attn, w_qkv, gain_two, gain_heads
     )
 
-    (grad_gate,) = widen(widen_gate, gate_grads, (w_gate.shape,))
-    grad_up, grad_down = widen(widen_feed, feed_grads, (w_up.shape, w_down.shape))
-    grad_query, grad_key, grad_value, grad_wout = widen(
-        widen_attn, attn_grads, (w_query.shape, w_key.shape, w_value.shape, w_out.shape)
+    grad_gate = pl.pallas_call(
+        widen_gate,
+        out_shape=jax.ShapeDtypeStruct(w_gate.shape, jnp.float32),
+        name="widen_gate",
+    )(gate_grads)
+    (
+        grad_input,
+        output,
+        grad_up,
+        grad_down,
+        grad_query,
+        grad_key,
+        grad_value,
+        grad_wout,
+    ) = finish(
+        grad_input.reshape(-1, model),
+        output.reshape(-1, model),
+        last_output,
+        feed_grads,
+        attn_grads,
+        (w_query.shape[1], w_key.shape[1], w_value.shape[1]),
     )
     return (
-        output,
-        grad_input,
+        output.reshape(layer_input.shape),
+        grad_input.reshape(layer_input.shape),
         grad_query,
         grad_key,
         grad_value,

time: 657 us -> 630 us (0.959); the launches traced: 648 us -> 630 us
  local copies, waits for them, and re-layouts: 20.5 us -> 12.9 us
  Pallas kernels: 608 us -> 601 us
    pallas_call x1, Pallas kernels: 308 us -> 294 us  [feed_forward(): pl.pallas_call(feed_kernel, out_shape=(jax.ShapeDtypeStruct((micro, tok,...]
    pallas_call x1, Pallas kernels: 48.3 us -> 59.6 us  [weight_gradients(): pl.pallas_call(weights_kernel, out_shape=(jax.ShapeDtypeStruct((micro, to...]
    unnamed x46 -> x43, local copies, waits for them, and re-layouts: 17.7 us -> 11.5 us
    pallas_call x5 -> x4, Pallas kernels: 49.3 us -> 53.2 us  [the longest x1 22.2 us: attention_back(): pl.pallas_call(functools.partial(attend_backward, groups), out_shape=jax....]
  transfers between devices with their start and end apart: 4 -> 4, of which waited for: 0 -> 0; matrix products, arithmetic and copies ran while one was open for 1% -> 0% of each run, Pallas kernels for 46% -> 47%
where the time goes in v4:
time: 630 us
  Pallas kernels  601 us (95%)
  between operations  14 us (2%)
  local copies, waits for them, and re-layouts  12.9 us (2%)
    pallas_call x1, Pallas kernels, feed_forward(): pl.pallas_call(feed_kernel, out_shape=(jax.ShapeDtypeStruct((micro, tok,...  294 us
    pallas_call x1, Pallas kernels, input_gradient(): pl.pallas_call(input_kernel, out_shape=(jax.ShapeDtypeStruct((micro, tok,...  119 us
    pallas_call x1, Pallas kernels, project(): pl.pallas_call(project_kernel, out_shape=(jax.ShapeDtypeStruct((micro, to...  75.4 us
    pallas_call x1, Pallas kernels, weight_gradients(): pl.pallas_call(weights_kernel, out_shape=(jax.ShapeDtypeStruct((micro, to...  59.6 us
    pallas_call x1, Pallas kernels, attention_back(): pl.pallas_call(functools.partial(attend_backward, groups), out_shape=jax....  22.2 us
    pallas_call x1, Pallas kernels, attention_out(): pl.pallas_call(functools.partial(attend_forward, groups), out_shape=(jax....  15.5 us
    pallas_call x1, Pallas kernels, finish(): pl.pallas_call(finish_kernel, grid=(steps,), out_shape=(jax.ShapeDtypeStr...  13.1 us
  transfers between devices with their start and end apart: 4, of which 0 were waited for; matrix products, arithmetic and copies ran while one was open for 0% of the time, Pallas kernels for 47%

profile of v4, /device:TPU:0, one launch (start us, length us, event | category | flops | bytes accessed | tf_op | source)
XLA Modules:
  0.0 630.0 jit_solution(6362989330186658585)
XLA Ops:
  7.3 0.0 all-gather.3.cloned.1.call-start
  7.3 1.6 copy.29
  8.9 0.3 copy.30
  9.2 1.0 pad_maximum_fusion
  10.2 0.0 all-gather.3.cloned.1.call-update
  10.2 0.0 reduce-scatter.8.cloned.1.call-start
  10.3 0.0 copy-start.13
  10.4 75.4 %project.1 = (bf16[4,256,2048]{2,1,0:T(8,128)(2,1)S(1)}, f32[4,256,768]{2,1,0:T(8,128)S(1)}, bf16[8,256,512]{2,1,0:T(8,128)(2,1)S(1)}, bf16[2048,1024]{1,0:T(8,1...) custom-call(bf16[4,256,2048]{2,1,0:T(8,128)(2,1)} %input_ref.7, f32[1,2048]{1,0:T(1,128)S(1)} %bitcast.28, ...), custom_call_target="tpu_custom_call" | custom-call | flops 20000000000 | bytes 40000000 | tf_op jit(solution)/shard_map/project/pallas_call | solution.py:908
  85.8 1.3 copy-done
  87.1 2.0 copy-done.1
  89.1 1.7 copy-done.2
  90.8 0.8 copy-done.5
  91.6 0.8 copy-done.7
  92.3 15.5 %attend_forward.1 = (bf16[2048,256]{1,0:T(8,128)(2,1)}, f32[2048,256]{1,0:T(8,128)}, f32[2048,2]{1,0:T(8,128)}) custom-call(s32[4,8]{1,0:T(4,128)} %lengths_ref.5, bf16[2048,512]{1,0:T(8,128)(2,1)} %bitcast.26), custom_call_target="tpu_custom_call" | custom-call | tf_op jit(solution)/shard_map/attend_forward/pallas_call | solution.py:428
  107.9 293.7 %feed_forward.1 = (bf16[4,256,2048]{2,1,0:T(8,128)(2,1)}, bf16[4,256,1536]{2,1,0:T(8,128)(2,1)}, bf16[4,256,1536]{2,1,0:T(8,128)(2,1)}, bf16[4,256,1536]{2,1,0:T...) custom-call(bf16[8,256,256]{2,1,0:T(8,128)(2,1)} %bitcast.46, ...), custom_call_target="tpu_custom_call" | custom-call | flops 240000008192 | bytes 900000000 | tf_op jit(solution)/shard_map/feed_forward/pallas_call | solution.py:1704
  401.6 0.0 reduce-scatter.8.cloned.1.call-update
  401.7 0.0 reduce-scatter.6.cloned.1.call-start
  401.7 22.2 %attend_backward.1 = bf16[2048,512]{1,0:T(8,128)(2,1)} custom-call(s32[4,8]{1,0:T(4,128)} %lengths_ref.5, bf16[2048,512]{1,0:T(8,128)(2,1)} %bitcast.27, bf16[2048,256]{1,0:T(8,128)(2,1)} %bitcast.38, f32[2048,256]{1,0:T(8,128)} %get-tuple-element.50.kept_ref, f32[2048,2]{1,0:T(8,128)} %get-tuple-element.51.log_ref), custom_call_target="tpu_custom_call" | custom-call | tf_op jit(solution)/shard_map/attend_backward/pallas_call | solution.py:453
  423.9 1.0 copy-done.6
  425.0 1.1 copy-done.8
  426.0 59.6 %weight_gradients.1 = (bf16[4,256,1024]{2,1,0:T(8,128)(2,1)S(1)}, bf16[4,256,1536]{2,1,0:T(8,128)(2,1)}, f32[2,128]{1,0:T(2,128)S(1)}, bf16[256,2048]{1,0:T(8,128)(2,1)S(1)}) custom-call(bf16[8,256,512]{2,1,0:T(8,128)(2,1)} %bitcast.31, f32[4,256,768]{2,1,0:T(8,128)} %copy-done.2, bf16[4,256,2048]{2,1,0:T(8,128)(2,1)} %copy-done.1, ...), custom_call_target="tpu_custom_call" | custom-call | flops 1000000000 | bytes 1000000 | tf_op jit(solution)/shard_map/weight_gradients/pallas_call | solution.py:1148
  485.7 1.0 copy-done.3
  486.6 0.0 reduce-scatter.6.cloned.1.call-update
  486.7 0.0 reduce-scatter.4.cloned.1.call-start
  486.7 0.5 reduce-scatter.4.cloned.1.call-update
  487.2 0.2 copy-done.10
  487.4 0.0 copy-done.11
  487.4 119.4 %input_gradient.1 = (f32[4,256,2048]{2,1,0:T(8,128)}, f32[8,2048]{1,0:T(8,128)S(1)}) custom-call(bf16[4,256,1024]{2,1,0:T(8,128)(2,1)S(1)} %get-tuple-element.59.back_ref, bf16[4,256,2048]{2,1,0:T(8,128)(2,1)} %input_ref.7, f32[4,256,2048]{2,1,0:T(8,128)} %get-tuple-element.60.middle_ref, f32[1,2048]{1,0:T(1,128)S(1)} %bitcast.29, ...), custom_call_target="tpu_custom_call" | custom-call | flops 1000000000 | bytes 1000000 | tf_op jit(solution)/shard_map/input_gradient/pallas_call | solution.py:1949
  606.8 0.5 slice_bitcast_fusion
  607.3 0.6 fusion
  607.9 2.4 widen_gate.1
  610.3 13.1 %finish.1 = (f32[1024,2048]{1,0:T(8,128)}, bf16[1024,2048]{1,0:T(8,128)(2,1)}, f32[256,1536]{1,0:T(8,128)}, f32[1536,256]{1,0:T(8,128)}, f32[256,512]{1,0:T(8,12...) custom-call(f32[1024,2048]{1,0:T(8,128)} %bitcast.30, bf16[768,2048]{1,0:T(8,128)(2,1)} %bitcast.37, ...), custom_call_target="tpu_custom_call" | custom-call | tf_op jit(solution)/shard_map/finish/pallas_call | solution.py:2027
  (36 shorter events, 0.1 us)
Async XLA Ops:
  7.2 2.0 copy-start.18
  7.2 3.1 copy-start.19
  7.2 3.1 copy-start.20
  7.2 3.1 copy-start.12
  7.2 3.1 copy-start.9
  7.2 3.1 copy-start.17
  7.2 3.1 copy-start.16
  7.3 3.1 copy-start.15
  7.3 100.6 %all-gather.3.cloned.1.call-start = ((), (), s32[]{:S(2)}) async-start(), calls=%async_computation.6 | async-start | bytes 9437184 | tf_op jit(solution)/shard_map/all_gather | solution.py:2084
  10.2 597.7 %reduce-scatter.8.cloned.1.call-start = ((), (), s32[]{:S(2)}) async-start(), calls=%async_computation.5 | async-start | bytes 3932160 | tf_op jit(solution)/shard_map/reduce_scatter | solution.py:2121
  10.3 75.5 %copy-start.13 = (f32[2,128]{1,0:T(2,128)}, f32[2,128]{1,0:T(2,128)S(1)}, u32[]{:S(2)}) copy-start(f32[2,128]{1,0:T(2,128)S(1)} %pad_maximum_fusion.1.head_gain_ref) | copy-start | bytes 3076
  85.8 1.3 copy-start
  87.1 2.0 copy-start.1
  89.1 1.7 copy-start.2
  90.8 0.8 copy-start.5
  91.6 0.8 copy-start.7
  401.7 208.7 %reduce-scatter.6.cloned.1.call-start = ((), (), s32[]{:S(2)}) async-start(), calls=%async_computation.4 | async-start | bytes 3932160 | tf_op jit(solution)/shard_map/reduce_scatter | solution.py:2121
  401.7 22.2 %copy-start.4 = (bf16[4,256,512]{2,1,0:T(8,128)(2,1)S(1)}, bf16[4,256,512]{2,1,0:T(8,128)(2,1)}, u32[]{:S(2)}) copy-start(bf16[4,256,512]{2,1,0:T(8,128)(2,1)} %get-tuple-element.54.mixed_ref) | copy-start | bytes 3145732
  401.7 22.2 %copy-start.14 = (f32[2,128]{1,0:T(2,128)S(1)}, f32[2,128]{1,0:T(2,128)}, u32[]{:S(2)}) copy-start(f32[2,128]{1,0:T(2,128)} %copy-done.13) | copy-start | bytes 3076
  423.9 1.0 copy-start.6
  425.0 1.1 copy-start.8
  485.6 1.0 copy-start.3
  486.7 123.7 %reduce-scatter.4.cloned.1.call-start = ((), (), s32[]{:S(2)}) async-start(), calls=%async_computation.3 | async-start | bytes 7864320 | tf_op jit(solution)/shard_map/reduce_scatter | solution.py:2121
  486.7 0.7 copy-start.10
  486.7 0.7 copy-start.11
Sparse Core Ops, SparseCore 0:
  10.6 84.8 all-gather.2
  401.8 68.8 reduce-scatter.7
  486.8 45.2 reduce-scatter.5
  534.9 70.1 reduce-scatter.3

commit v5 on v4

--- a/solution.py
+++ b/solution.py
@@ -307,6 +307,7 @@
 
 
 BLOCK = 256
+HEAD_GROUPS = 2
 NT = (((1,), (1,)), ((), ()))
 TN = (((0,), (0,)), ((), ()))
 
@@ -320,117 +321,59 @@
     return start
 
 
-def query_rows(lengths_ref, groups, step_q):
-    micro = lax.axis_index("wide") // groups
-    spot = lax.broadcasted_iota(jnp.int32, (BLOCK, 1), 0) + step_q * BLOCK
-    start = piece_starts(lengths_ref, micro, spot)
-    first = piece_starts(lengths_ref, micro, step_q * BLOCK) // BLOCK
-    spot = jnp.concatenate([spot, spot], axis=0)
-    start = jnp.concatenate([start, start], axis=0)
-    return spot, start, first
-
-
-def attend_forward(groups, lengths_ref, qkv_ref, mixed_ref, kept_ref, log_ref):
+def query_lanes(lengths_ref, step_q):
+    micro = lax.axis_index("wide") // HEAD_GROUPS
+    lane = lax.broadcasted_iota(jnp.int32, (1, 2 * BLOCK), 1)
+    spot = lane % BLOCK + step_q * BLOCK
+    return spot, piece_starts(lengths_ref, micro, spot)
+
+
+def key_fits(step_k, spot, start):
+    key_spot = lax.broadcasted_iota(jnp.int32, (BLOCK, 1), 0) + step_k * BLOCK
+    return (key_spot >= start) & (key_spot <= spot)
+
+
+def attend_forward(lengths_ref, qkv_ref, mixed_ref, kept_ref, log_ref):
     step_q = pl.program_id(0)
     rows = pl.ds(step_q * BLOCK, BLOCK)
     factor = 1.0 / math.sqrt(HD)
     query = jnp.concatenate([qkv_ref[rows, 0:HD], qkv_ref[rows, HD : 2 * HD]], axis=0)
-    spot, start, first = query_rows(lengths_ref, groups, step_q)
+    spot, start = query_lanes(lengths_ref, step_q)
+    micro = lax.axis_index("wide") // HEAD_GROUPS
+    first = piece_starts(lengths_ref, micro, step_q * BLOCK) // BLOCK
 
     def one(step_k, carry):
-        total, mixed = carry
+        total, total_low, mixed = carry
         cols = pl.ds(step_k * BLOCK, BLOCK)
-        scores = lax.dot_general(
-            query, qkv_ref[cols, 2 * HD : 3 * HD], NT, preferred_element_type=jnp.float32
-        )
-        key_spot = lax.broadcasted_iota(jnp.int32, (1, BLOCK), 1) + step_k * BLOCK
-        fits = (key_spot >= start) & (key_spot <= spot)
-        exponent = jnp.where(fits, jnp.exp(scores * factor), 0.0)
-        for half in range(BLOCK // HD):
-            total += exponent[:, half * HD : (half + 1) * HD]
-        mixed += jnp.dot(
-            exponent.astype(jnp.bfloat16),
-            qkv_ref[cols, 3 * HD : 4 * HD],
-            preferred_element_type=jnp.float32,
-        )
-        return (total, mixed)
-
-    total, mixed = lax.fori_loop(
-        first,
-        step_q + 1,
-        one,
-        (
-            jnp.zeros((2 * BLOCK, HD), jnp.float32),
-            jnp.zeros((2 * BLOCK, HD), jnp.float32),
-        ),
-    )
-    total = jnp.sum(total, axis=-1, keepdims=True)
-    mixed = mixed / total
+        scores = dot_f32(qkv_ref[cols, 2 * HD : 3 * HD], query, NT)
+        exponent = jnp.where(key_fits(step_k, spot, start), jnp.exp(scores * factor), 0.0)
+        low = exponent.astype(jnp.bfloat16)
+        total += jnp.sum(exponent.reshape(-1, 8, 2 * BLOCK), axis=0)
+        total_low += jnp.sum(low.astype(jnp.float32).reshape(-1, 8, 2 * BLOCK), axis=0)
+        mixed += dot_f32(qkv_ref[cols, 3 * HD : 4 * HD], low, TN)
+        return (total, total_low, mixed)
+
+    zeros = jnp.zeros((8, 2 * BLOCK), jnp.float32)
+    total, total_low, mixed = lax.fori_loop(
+        first, step_q + 1, one, (zeros, zeros, jnp.zeros((HD, 2 * BLOCK), jnp.float32))
+    )
+    mixed = (mixed / jnp.sum(total_low, axis=0, keepdims=True)).T
     mixed = jnp.concatenate([mixed[:BLOCK], mixed[BLOCK:]], axis=1)
     mixed_ref[...] = mixed.astype(jnp.bfloat16)
     kept_ref[...] = mixed
-    log_total = jnp.log(total)
-    log_ref[...] = jnp.concatenate([log_total[:BLOCK], log_total[BLOCK:]], axis=1)
-
-
-def attend_backward(
-    groups, lengths_ref, qkv_ref, grad_ref, kept_ref, log_ref, back_ref, key_sum, value_sum
-):
-    step_q = pl.program_id(0)
-    rows = pl.ds(step_q * BLOCK, BLOCK)
-    factor = 1.0 / math.sqrt(HD)
-
-    @pl.when(step_q == 0)
-    def _():
-        key_sum[...] = jnp.zeros_like(key_sum)
-        value_sum[...] = jnp.zeros_like(value_sum)
-
-    query = jnp.concatenate([qkv_ref[rows, 0:HD], qkv_ref[rows, HD : 2 * HD]], axis=0)
-    grad = jnp.concatenate([grad_ref[:, 0:HD], grad_ref[:, HD : 2 * HD]], axis=0)
-    kept = jnp.concatenate([kept_ref[:, 0:HD], kept_ref[:, HD : 2 * HD]], axis=0)
-    log_total = jnp.concatenate([log_ref[:, 0:1], log_ref[:, 1:2]], axis=0)
-    weighted = jnp.sum(grad.astype(jnp.float32) * kept, axis=-1, keepdims=True)
-    spot, start, first = query_rows(lengths_ref, groups, step_q)
-
-    def one(step_k, query_sum):
-        cols = pl.ds(step_k * BLOCK, BLOCK)
-        key = qkv_ref[cols, 2 * HD : 3 * HD]
-        scores = lax.dot_general(query, key, NT, preferred_element_type=jnp.float32) * factor
-        key_spot = lax.broadcasted_iota(jnp.int32, (1, BLOCK), 1) + step_k * BLOCK
-        fits = (key_spot >= start) & (key_spot <= spot)
-        probs = jnp.where(fits, jnp.exp(scores - log_total), 0.0)
-        grad_probs = lax.dot_general(
-            grad, qkv_ref[cols, 3 * HD : 4 * HD], NT, preferred_element_type=jnp.float32
-        )
-        grad_scores = (probs * (grad_probs - weighted)).astype(jnp.bfloat16)
-        value_sum[cols, :] += lax.dot_general(
-            probs.astype(jnp.bfloat16), grad, TN, preferred_element_type=jnp.float32
-        )
-        key_sum[cols, :] += lax.dot_general(
-            grad_scores, query, TN, preferred_element_type=jnp.float32
-        )
-        return query_sum + jnp.dot(grad_scores, key, preferred_element_type=jnp.float32)
-
-    query_sum = lax.fori_loop(first, step_q + 1, one, jnp.zeros((2 * BLOCK, HD), jnp.float32))
-    query_sum = (query_sum * factor).astype(jnp.bfloat16)
-    back_ref[rows, 0:HD] = query_sum[:BLOCK]
-    back_ref[rows, HD : 2 * HD] = query_sum[BLOCK:]
-
-    @pl.when(step_q == pl.num_programs(0) - 1)
-    def _():
-        back_ref[:, 2 * HD : 3 * HD] = (key_sum[...] * factor).astype(jnp.bfloat16)
-        back_ref[:, 3 * HD : 4 * HD] = value_sum[...].astype(jnp.bfloat16)
-
-
-def attention_out(qkv, lengths, groups):
+    log_total = jnp.log(jnp.sum(total, axis=0, keepdims=True))
+    log_ref[...] = jnp.broadcast_to(log_total, zeros.shape)[None]
+
+
+def attention_out(qkv, lengths):
     total = qkv.shape[0]
     block = lambda i, *_: (i, 0)
     return pl.pallas_call(
-        functools.partial(attend_forward, groups),
+        attend_forward,
         out_shape=(
             jax.ShapeDtypeStruct((total, 2 * HD), jnp.bfloat16),
             jax.ShapeDtypeStruct((total, 2 * HD), jnp.float32),
-            jax.ShapeDtypeStruct((total, 2), jnp.float32),
+            jax.ShapeDtypeStruct((total // BLOCK, 8, 2 * BLOCK), jnp.float32),
         ),
         grid_spec=pltpu.PrefetchScalarGridSpec(
             num_scalar_prefetch=1,
@@ -439,37 +382,11 @@
             out_specs=[
                 pl.BlockSpec((BLOCK, 2 * HD), block),
                 pl.BlockSpec((BLOCK, 2 * HD), block),
-                pl.BlockSpec((BLOCK, 2), block),
+                pl.BlockSpec((1, 8, 2 * BLOCK), lambda i, *_: (i, 0, 0)),
             ],
         ),
         name="attend_forward",
     )(lengths, qkv)
-
-
-def attention_back(qkv, lengths, groups, grad, kept, log_total):
-    total = qkv.shape[0]
-    whole = lambda i, *_: (0, 0)
-    block = lambda i, *_: (i, 0)
-    return pl.pallas_call(
-        functools.partial(attend_backward, groups),
-        out_shape=jax.ShapeDtypeStruct((total, 4 * HD), jnp.bfloat16),
-        grid_spec=pltpu.PrefetchScalarGridSpec(
-            num_scalar_prefetch=1,
-            grid=(total // BLOCK,),
-            in_specs=[
-                pl.BlockSpec((total, 4 * HD), whole),
-                pl.BlockSpec((BLOCK, 2 * HD), block),
-                pl.BlockSpec((BLOCK, 2 * HD), block),
-                pl.BlockSpec((BLOCK, 2), block),
-            ],
-            out_specs=pl.BlockSpec((total, 4 * HD), whole),
-            scratch_shapes=[
-                pltpu.VMEM((total, HD), jnp.float32),
-                pltpu.VMEM((total, HD), jnp.float32),
-            ],
-        ),
-        name="attend_backward",
-    )(lengths, qkv, grad, kept, log_total)
 
 
 def dot_f32(left, right, dims=(((1,), (0,)), ((), ()))):
@@ -943,7 +860,11 @@
 
 
 def weights_kernel(
-    back_ref,
+    lengths_ref,
+    qkv_ref,
+    upper_ref,
+    kept_ref,
+    log_ref,
     raw_ref,
     hidden_ref,
     mixed_ref,
@@ -974,24 +895,47 @@
     pair_v,
     middle_v,
     rows_v,
+    qkv_v,
+    upper_v,
+    kept_v,
+    log_v,
+    sent_v,
+    query_sum,
+    key_sum,
+    value_sum,
     load_sem,
     back_sem,
     tile_sem,
-    send_sem,
-    land_sem,
+    send_sems,
+    land_sems,
     pair_sems,
     late_sem,
+    attn_sem,
 ):
     micro, tok, heads_in = mixed_ref.shape
-    width = back_ref.shape[0]
+    width = upper_ref.shape[0]
     groups = width // micro
     heads = 2 * groups
     model = hidden_ref.shape[2]
     piece = model // width
     count = micro * tok
-    swap = Exchange(
-        lambda target: back_ref.at[target], lambda source: land_v.at[source], send_sem, land_sem
-    )
+    factor = 1.0 / math.sqrt(HD)
+    halves = (pl.ds(0, 2 * HD), pl.ds(2 * HD, 2 * HD))
+    swaps = [
+        Exchange(
+            lambda target, cols=cols: sent_v.at[target, :, cols],
+            lambda source, cols=cols: land_v.at[source, :, cols],
+            send_sems.at[i],
+            land_sems.at[i],
+        )
+        for i, cols in enumerate(halves)
+    ]
+    attn_loads = [
+        pltpu.make_async_copy(source, target, attn_sem.at[i])
+        for i, (source, target) in enumerate(
+            ((qkv_ref, qkv_v), (upper_ref, upper_v), (kept_ref, kept_v), (log_ref, log_v))
+        )
+    ]
     loads = [
         pltpu.make_async_copy(mixed_ref, mixed_v, load_sem.at[0]),
         pltpu.make_async_copy(low_ref, low_v, load_sem.at[1]),
@@ -1005,15 +949,75 @@
         pltpu.make_async_copy(late_ref.at[1], middle_v, late_sem.at[1]),
         pltpu.make_async_copy(input_ref.at[micro - 1], rows_v, late_sem.at[2]),
     ]
-    for copy in late_loads + loads:
+    for copy in attn_loads + late_loads + loads:
         copy.start()
+    key_sum[...] = jnp.zeros_like(key_sum)
+    value_sum[...] = jnp.zeros_like(value_sum)
     relay.greet(wide_peers(width))
     spot = lax.axis_index("wide")
-    for step in range(width - 1, -1, -1):
-        swap.send(lax.rem(spot + step, width))
     for copy in late_loads:
         copy.wait()
     relay.send(0, per)
+    for copy in attn_loads:
+        copy.wait()
+    band = width * tok // 2 // BLOCK
+
+    @pl.loop(0, width)
+    def _(step):
+        far = micro - 1 - step // 2
+        chip = spot // 2
+        turn = (chip + far) % 2 + 2 * ((chip // 2 + far // 2) % 2)
+        step_q = 2 * turn + step % 2
+        rows = pl.ds(pl.multiple_of(step_q * BLOCK, BLOCK), BLOCK)
+        query = jnp.concatenate([qkv_v[rows, 0:HD], qkv_v[rows, HD : 2 * HD]], axis=0)
+        grad = jnp.concatenate([upper_v[step_q, :, 0:HD], upper_v[step_q, :, HD : 2 * HD]], axis=0)
+        kept = jnp.concatenate([kept_v[rows, 0:HD], kept_v[rows, HD : 2 * HD]], axis=0)
+        weighted = lax.dot_general(
+            jnp.ones((8, HD), jnp.float32),
+            grad.astype(jnp.float32) * kept,
+            NT,
+            precision=lax.Precision.HIGHEST,
+            preferred_element_type=jnp.float32,
+        )[0:1]
+        log_total = log_v[step_q, 0:1, :]
+        spots, start = query_lanes(lengths_ref, step_q)
+        query_sum[...] = jnp.zeros_like(query_sum)
+
+        @pl.loop(0, band + 1)
+        def _(t):
+            step_k = step_q - band + t
+
+            @pl.when(step_k >= 0)
+            def _():
+                cols = pl.ds(pl.multiple_of(step_k * BLOCK, BLOCK), BLOCK)
+                key = qkv_v[cols, 2 * HD : 3 * HD]
+                scores = dot_f32(key, query, NT) * factor
+                probs = jnp.where(
+                    key_fits(step_k, spots, start), jnp.exp(scores - log_total), 0.0
+                )
+                grad_probs = dot_f32(qkv_v[cols, 3 * HD : 4 * HD], grad, NT)
+                grad_scores = (probs * (grad_probs - weighted)).astype(jnp.bfloat16)
+                value_sum[cols, :] += dot_f32(probs.astype(jnp.bfloat16), grad)
+                key_sum[cols, :] += dot_f32(grad_scores, query)
+                query_sum[...] += dot_f32(grad_scores, key, TN)
+
+        part = (query_sum[...] * factor).astype(jnp.bfloat16)
+        sent_v[step_q, :, 0:HD] = part[:BLOCK]
+        sent_v[step_q, :, HD : 2 * HD] = part[BLOCK:]
+        swaps[0].send(step_q)
+
+        @pl.when(step % 2 == 1)
+        def _():
+            relay.tick(step // 2)
+
+    @pl.loop(0, width)
+    def _(i):
+        rows = pl.ds(pl.multiple_of(i * BLOCK, BLOCK), BLOCK)
+        sent_v[i, :, 2 * HD : 3 * HD] = (key_sum[rows, :] * factor).astype(jnp.bfloat16)
+        sent_v[i, :, 3 * HD : 4 * HD] = value_sum[rows, :].astype(jnp.bfloat16)
+
+    for step in range(width - 1, -1, -1):
+        swaps[1].send(lax.rem(spot + step, width))
     loads[0].wait()
     loads[1].wait()
     mixed_all = mixed_v[...].reshape(count, heads_in)
@@ -1028,42 +1032,52 @@
     loads[2].wait()
     gain_out[...] = jnp.zeros_like(gain_out)
 
-    for k in range(4):
-        relay.tick(k)
+    def back_copy(m):
+        return pltpu.make_async_copy(back_v.at[m], back_out.at[m], back_sem.at[m])
+
+    def turn_back(m, h):
+        span = pl.ds(pl.multiple_of(m * tok, tok), tok)
+        raw = raw_v[m, :, h * HD : (h + 1) * HD]
+        kind = 0 if h < heads else 1
+        gain = head_gain_ref[kind : kind + 1, :]
+        g, place = (h // 2, h % 2) if h < heads else (h - heads, 2)
+        grad = land_v[m * groups + g, :, place * HD : (place + 1) * HD].astype(jnp.float32)
+        straight = grad * cosine_ref[span, :] + pltpu.roll(grad * sine_ref[span, :], HD // 2, 1)
+        scale = lax.rsqrt(jnp.mean(raw * raw, axis=-1, keepdims=True) + EPSILON)
+        gain_out[kind : kind + 1, :] += jnp.sum(straight * (raw * scale), axis=0, keepdims=True)
+        pulled = straight * gain
+        along = jnp.mean(pulled * raw, axis=-1, keepdims=True)
+        back_v[m, :, h * HD : (h + 1) * HD] = (
+            scale * (pulled - raw * (scale * scale * along))
+        ).astype(jnp.bfloat16)
 
     @pl.loop(0, width)
     def _(d):
-        swap.wait(d)
-
-    def back_copy(m):
-        return pltpu.make_async_copy(back_v.at[m], back_out.at[m], back_sem.at[m])
+        swaps[0].wait(d)
 
     @pl.loop(0, micro)
     def _(m):
-        span = pl.ds(pl.multiple_of(m * tok, tok), tok)
-        cosine, sine = cosine_ref[span, :], sine_ref[span, :]
-        for h in range(heads + groups):
-            raw = raw_v[m, :, h * HD : (h + 1) * HD]
-            kind = 0 if h < heads else 1
-            gain = head_gain_ref[kind : kind + 1, :]
-            g, place = (h // 2, h % 2) if h < heads else (h - heads, 2)
-            grad = land_v[m * groups + g, :, place * HD : (place + 1) * HD].astype(jnp.float32)
-            straight = grad * cosine + pltpu.roll(grad * sine, HD // 2, 1)
-            scale = lax.rsqrt(jnp.mean(raw * raw, axis=-1, keepdims=True) + EPSILON)
-            gain_out[kind : kind + 1, :] += jnp.sum(straight * (raw * scale), axis=0, keepdims=True)
-            pulled = straight * gain
-            along = jnp.mean(pulled * raw, axis=-1, keepdims=True)
-            back_v[m, :, h * HD : (h + 1) * HD] = (
-                scale * (pulled - raw * (scale * scale * along))
-            ).astype(jnp.bfloat16)
+        for h in range(heads):
+            turn_back(m, h)
+
+        @pl.when(m == 1)
+        def _():
+            relay.tick(4)
+
+    relay.tick(5)
+
+    @pl.loop(0, width)
+    def _(d):
+        swaps[1].wait(d)
+
+    @pl.loop(0, micro)
+    def _(m):
+        for h in range(heads, heads + groups):
+            turn_back(m, h)
         for g in range(groups):
             first = (heads + groups + g) * HD
             back_v[m, :, first : first + HD] = land_v[m * groups + g, :, 3 * HD :]
         back_copy(m).start()
-
-        @pl.when(m % 2 == 1)
-        def _():
-            relay.tick(4 + m // 2)
 
     loads[3].wait()
 
@@ -1128,7 +1142,8 @@
 
     @pl.loop(0, width)
     def _(i):
-        swap.sent(i)
+        for swap in swaps:
+            swap.sent(i)
 
     for m in range(micro):
         back_copy(m).wait()
@@ -1136,11 +1151,12 @@
     relay.drain(0)
 
 
-def weight_gradients(
-    back, raw, hidden, mixed, middle_low, late, layer_input, cosine, sine, head_gains
+def attention_gradients(
+    lengths, qkv, upper, kept, log_total, raw, hidden, mixed, middle_low, late, layer_input, *rest
 ):
     micro, tok, heads_in = mixed.shape
-    width = back.shape[0]
+    width = upper.shape[0]
+    total = qkv.shape[0]
     model = hidden.shape[2]
     low = jnp.bfloat16
     anywhere = pl.BlockSpec(memory_space=pl.ANY)
@@ -1153,11 +1169,11 @@
             jax.ShapeDtypeStruct((2, HD), jnp.float32),
             jax.ShapeDtypeStruct((tok, model), low),
         ),
-        in_specs=[anywhere] * 7 + [inside] * 3,
+        in_specs=[pl.BlockSpec(memory_space=pltpu.SMEM)] + [anywhere] * 10 + [inside] * 3,
         out_specs=[anywhere, anywhere, inside, anywhere],
         scratch_shapes=relay_scratch(tok // SUB, model)
         + [
-            pltpu.VMEM(back.shape, low),
+            pltpu.VMEM((width, tok, 4 * HD), low),
             pltpu.VMEM(raw.shape, jnp.float32),
             pltpu.VMEM(hidden.shape, low),
             pltpu.VMEM(mixed.shape, low),
@@ -1167,22 +1183,31 @@
             pltpu.VMEM((width // 2, model // width, 3 * heads_in), low),
             pltpu.VMEM((tok // SUB, SUB, model), low),
             pltpu.VMEM((tok, model), low),
+            pltpu.VMEM(qkv.shape, low),
+            pltpu.VMEM(upper.shape, low),
+            pltpu.VMEM(kept.shape, jnp.float32),
+            pltpu.VMEM(log_total.shape, jnp.float32),
+            pltpu.VMEM((width, tok, 4 * HD), low),
+            pltpu.VMEM((2 * BLOCK, HD), jnp.float32),
+            pltpu.VMEM((total, HD), jnp.float32),
+            pltpu.VMEM((total, HD), jnp.float32),
             pltpu.SemaphoreType.DMA((4,)),
             pltpu.SemaphoreType.DMA((micro,)),
             pltpu.SemaphoreType.DMA((width // 2,)),
-            pltpu.SemaphoreType.DMA((width,)),
-            pltpu.SemaphoreType.DMA((width,)),
+            pltpu.SemaphoreType.DMA((2, width)),
+            pltpu.SemaphoreType.DMA((2, width)),
             pltpu.SemaphoreType.DMA((2, width // 2)),
+            pltpu.SemaphoreType.DMA((4,)),
             pltpu.SemaphoreType.DMA((4,)),
         ],
         compiler_params=pltpu.CompilerParams(
-            collective_id=3, has_side_effects=True, vmem_limit_bytes=48 << 20
+            collective_id=3, has_side_effects=True, vmem_limit_bytes=56 << 20
         ),
         cost_estimate=pl.CostEstimate(
             flops=1_000_000_000, bytes_accessed=1_000_000, transcendentals=0
         ),
-        name="weight_gradients",
-    )(back, raw, hidden, mixed, middle_low, late, layer_input, cosine, sine, head_gains)
+        name="attention_gradients",
+    )(lengths, qkv, upper, kept, log_total, raw, hidden, mixed, middle_low, late, layer_input, *rest)
 
 
 def relay_scratch(count, model, extra=0):
@@ -2090,7 +2115,7 @@
         layer_input, gain_attn, (w_query, w_key, w_value), lengths, head_gains, width
     )
     packed = packed.reshape(total, 4 * HD)
-    mixed, kept, log_total = attention_out(packed, lengths, groups)
+    mixed, kept, log_total = attention_out(packed, lengths)
     (
         _,
         _,
@@ -2122,11 +2147,12 @@
             rows, "wide", scatter_dimension=0, axis_index_groups=cores, tiled=True
         )
 
-    back = attention_back(
-        packed, lengths, groups, grad_mixed.reshape(total, 2 * HD), kept, log_total
-    )
-    qkv_back, attn_grads, gain_heads, last_output = weight_gradients(
-        back.reshape(width, tok_rows, 4 * HD),
+    qkv_back, attn_grads, gain_heads, last_output = attention_gradients(
+        lengths,
+        packed,
+        grad_mixed,
+        kept,
+        log_total,
         raw,
         hidden_one,
         mixed_low,
@@ -2189,7 +2215,8 @@
     micro, tok_rows = layer_input.shape[:2]
     groups = w_key.shape[1] // HD
     fits = (
-        micro * groups == width == 8
+        groups == HEAD_GROUPS
+        and micro * groups == width == 8
         and w_query.shape[1] == 2 * w_key.shape[1]
         and mesh.shape["narrow"] == 4
         and tok_rows == BLOCK

time: 630 us -> 618 us (0.981)
  Pallas kernels: 601 us -> 589 us
    pallas_call x3 -> x2, Pallas kernels: 97.3 us -> 84.6 us  [the longest x1 68.6 us: attention_gradients(): pl.pallas_call(weights_kernel, out_shape=(jax.ShapeDtypeStruct((micro, to...]
  transfers between devices with their start and end apart: 4 -> 4, of which waited for: 0 -> 1; matrix products, arithmetic and copies ran while one was open for 0% -> 0% of each run, Pallas kernels for 47% -> 46%
where the time goes in v5:
time: 618 us
  Pallas kernels  589 us (95%)
  between operations  14 us (2%)
  local copies, waits for them, and re-layouts  10.7 us (2%)
    pallas_call x1, Pallas kernels, feed_forward(): pl.pallas_call(feed_kernel, out_shape=(jax.ShapeDtypeStruct((micro, tok,...  294 us
    pallas_call x1, Pallas kernels, input_gradient(): pl.pallas_call(input_kernel, out_shape=(jax.ShapeDtypeStruct((micro, tok,...  120 us
    pallas_call x1, Pallas kernels, project(): pl.pallas_call(project_kernel, out_shape=(jax.ShapeDtypeStruct((micro, to...  75.4 us
    pallas_call x1, Pallas kernels, attention_gradients(): pl.pallas_call(weights_kernel, out_shape=(jax.ShapeDtypeStruct((micro, to...  68.6 us
    pallas_call x1, Pallas kernels, attention_out(): pl.pallas_call(attend_forward, out_shape=(jax.ShapeDtypeStruct((total, 2...  16 us
    pallas_call x1, Pallas kernels, finish(): pl.pallas_call(finish_kernel, grid=(steps,), out_shape=(jax.ShapeDtypeStr...  13.1 us
  transfers between devices with their start and end apart: 4, of which 1 were waited for; matrix products, arithmetic and copies ran while one was open for 0% of the time, Pallas kernels for 46%

profile of v5, /device:TPU:0, one launch (start us, length us, event | category | flops | bytes accessed | tf_op | source)
XLA Modules:
  0.0 618.3 jit_solution(9326581225110181430)
XLA Ops:
  7.2 0.0 copy-start.9
  7.2 0.0 copy-start.6
  7.3 0.0 all-gather.3.cloned.1.call-start
  7.3 1.6 copy.29
  8.9 0.3 copy.30
  9.2 0.0 copy-done.15
  9.2 1.0 pad_maximum_fusion
  10.2 0.0 all-gather.3.cloned.1.call-update
  10.2 0.0 reduce-scatter.8.cloned.1.call-start
  10.3 0.0 copy-start.10
  10.4 75.4 %project.1 = (bf16[4,256,2048]{2,1,0:T(8,128)(2,1)S(1)}, f32[4,256,768]{2,1,0:T(8,128)S(1)}, bf16[8,256,512]{2,1,0:T(8,128)(2,1)S(1)}, bf16[2048,1024]{1,0:T(8,1...) custom-call(bf16[4,256,2048]{2,1,0:T(8,128)(2,1)} %input_ref.7, f32[1,2048]{1,0:T(1,128)S(1)} %bitcast.26, ...), custom_call_target="tpu_custom_call" | custom-call | flops 20000000000 | bytes 40000000 | tf_op jit(solution)/shard_map/project/pallas_call | solution.py:825
  85.8 1.3 copy-done
  87.1 2.0 copy-done.1
  89.1 1.7 copy-done.2
  90.8 0.8 copy-done.4
  91.6 0.8 copy-done.5
  92.4 16.0 %attend_forward.1 = (bf16[2048,256]{1,0:T(8,128)(2,1)}, f32[2048,256]{1,0:T(8,128)}, f32[8,8,512]{2,1,0:T(8,128)}) custom-call(s32[4,8]{1,0:T(4,128)} %lengths_ref.5, bf16[2048,512]{1,0:T(8,128)(2,1)} %bitcast.24), custom_call_target="tpu_custom_call" | custom-call | tf_op jit(solution)/shard_map/attend_forward/pallas_call | solution.py:371
  108.4 293.8 %feed_forward.1 = (bf16[4,256,2048]{2,1,0:T(8,128)(2,1)}, bf16[4,256,1536]{2,1,0:T(8,128)(2,1)}, bf16[4,256,1536]{2,1,0:T(8,128)(2,1)}, bf16[4,256,1536]{2,1,0:T...) custom-call(bf16[8,256,256]{2,1,0:T(8,128)(2,1)} %bitcast.42, ...), custom_call_target="tpu_custom_call" | custom-call | flops 240000008192 | bytes 900000000 | tf_op jit(solution)/shard_map/feed_forward/pallas_call | solution.py:1729
  402.2 0.0 reduce-scatter.8.cloned.1.call-update
  402.2 0.0 reduce-scatter.6.cloned.1.call-start
  402.2 68.6 %attention_gradients.1 = (bf16[4,256,1024]{2,1,0:T(8,128)(2,1)}, bf16[4,256,1536]{2,1,0:T(8,128)(2,1)}, f32[2,128]{1,0:T(2,128)}, bf16[256,2048]{1,0:T(8,128)(2,1)}) custom-call(s32[4,8]{1,0:T(4,128)} %lengths_ref.5, bf16[2048,512]{1,0:T(8,128)(2,1)} %bitcast.25, bf16[8,256,256]{2,1,0:T(8,128)(2,1)} %get-tuple-element.49.upper_ref, ...), custom_call_target="tpu_custom_call" | custom-call | flops 1000000000 | bytes 1000000 | tf_op jit(solution)/shard_map/attention_gradients/pallas_call | solution.py:1164
  470.9 0.0 reduce-scatter.6.cloned.1.call-update
  470.9 0.0 reduce-scatter.4.cloned.1.call-start
  470.9 0.0 copy-start.7
  471.0 0.5 reduce-scatter.4.cloned.1.call-update
  471.5 1.1 copy-done.3
  472.6 119.8 %input_gradient.1 = (f32[4,256,2048]{2,1,0:T(8,128)}, f32[8,2048]{1,0:T(8,128)S(1)}) custom-call(bf16[4,256,1024]{2,1,0:T(8,128)(2,1)S(1)} %copy-done.3, bf16[4,256,2048]{2,1,0:T(8,128)(2,1)} %input_ref.7, f32[4,256,2048]{2,1,0:T(8,128)} %get-tuple-element.60.middle_ref, f32[1,2048]{1,0:T(1,128)S(1)} %bitcast.27, ...), custom_call_target="tpu_custom_call" | custom-call | flops 1000000000 | bytes 1000000 | tf_op jit(solution)/shard_map/input_gradient/pallas_call | solution.py:1974
  592.4 0.5 slice_bitcast_fusion
  592.9 0.6 fusion
  593.5 2.4 widen_gate.1
  595.9 2.8 reduce-scatter.4.cloned.1.call-done.up_rows.down_rows
  598.7 13.1 %finish.1 = (f32[1024,2048]{1,0:T(8,128)}, bf16[1024,2048]{1,0:T(8,128)(2,1)}, f32[256,1536]{1,0:T(8,128)}, f32[1536,256]{1,0:T(8,128)}, f32[256,512]{1,0:T(8,12...) custom-call(f32[1024,2048]{1,0:T(8,128)} %bitcast.28, bf16[768,2048]{1,0:T(8,128)(2,1)} %bitcast.34, ...), custom_call_target="tpu_custom_call" | custom-call | tf_op jit(solution)/shard_map/finish/pallas_call | solution.py:2052
  (29 shorter events, 0.1 us)
Async XLA Ops:
  7.2 2.0 copy-start.15
  7.2 3.1 copy-start.16
  7.2 3.1 copy-start.17
  7.2 3.1 copy-start.9
  7.2 3.1 copy-start.6
  7.2 3.1 copy-start.14
  7.2 3.1 copy-start.13
  7.3 3.1 copy-start.12
  7.3 101.1 %all-gather.3.cloned.1.call-start = ((), (), s32[]{:S(2)}) async-start(), calls=%async_computation.6 | async-start | bytes 9437184 | tf_op jit(solution)/shard_map/all_gather | solution.py:2109
  10.2 583.3 %reduce-scatter.8.cloned.1.call-start = ((), (), s32[]{:S(2)}) async-start(), calls=%async_computation.5 | async-start | bytes 3932160 | tf_op jit(solution)/shard_map/reduce_scatter | solution.py:2146
  10.3 75.5 %copy-start.10 = (f32[2,128]{1,0:T(2,128)}, f32[2,128]{1,0:T(2,128)S(1)}, u32[]{:S(2)}) copy-start(f32[2,128]{1,0:T(2,128)S(1)} %pad_maximum_fusion.1.head_gain_ref) | copy-start | bytes 3076
  85.8 1.3 copy-start
  87.1 2.0 copy-start.1
  89.1 1.7 copy-start.2
  90.8 0.8 copy-start.4
  91.6 0.8 copy-start.5
  402.2 193.7 %reduce-scatter.6.cloned.1.call-start = ((), (), s32[]{:S(2)}) async-start(), calls=%async_computation.4 | async-start | bytes 3932160 | tf_op jit(solution)/shard_map/reduce_scatter | solution.py:2146
  470.9 127.8 %reduce-scatter.4.cloned.1.call-start = ((), (), s32[]{:S(2)}) async-start(), calls=%async_computation.3 | async-start | bytes 7864320 | tf_op jit(solution)/shard_map/reduce_scatter | solution.py:2146
  470.9 1.6 copy-start.3
  470.9 1.6 copy-start.7
  470.9 1.6 copy-start.8
  471.0 1.6 copy-start.11
Sparse Core Ops, SparseCore 0:
  10.6 84.8 all-gather.2
  402.3 75.8 reduce-scatter.7
  481.2 44.4 reduce-scatter.5
  528.5 70.1 reduce-scatter.3

commit v6 on v5

--- a/solution.py
+++ b/solution.py
@@ -396,8 +396,9 @@
 SUB = 64
 RING = 8
 STRIP = 16
-AHEAD = 3
-GAIN_TICKS = (0, 2, 4, 6, 11, 14, 17)
+FINE = 32
+AHEAD = 6
+GAIN_PLACES = (0, 2, 4, 6, 10, 13, 16)
 LANES = 512
 MESH = pl.DeviceIdType.MESH
 
@@ -477,7 +478,7 @@
         def _():
             self.to_inner(k).wait_recv()
 
-            @pl.loop(0, SUB // STRIP)
+            @pl.loop(0, self.own.shape[1] // STRIP)
             def _(i):
                 rows = pl.ds(pl.multiple_of(i * STRIP, STRIP), STRIP)
                 self.own[k, rows] = (
@@ -491,7 +492,7 @@
             j = k - 2
             self.to_other(j).wait_recv()
 
-            @pl.loop(0, SUB // STRIP)
+            @pl.loop(0, self.own.shape[1] // STRIP)
             def _(i):
                 rows = pl.ds(pl.multiple_of(i * STRIP, STRIP), STRIP)
                 self.landed[j, rows] = (
@@ -504,6 +505,10 @@
         @pl.when(self.is_end & (k >= 4) & (k < self.count + 4))
         def _():
             self.to_outer(k - 4).wait_recv()
+
+    def place(self, p):
+        self.tick(2 * p)
+        self.tick(2 * p + 1)
 
     def drain(self, first):
         @pl.loop(first, self.count)
@@ -874,6 +879,7 @@
     cosine_ref,
     sine_ref,
     head_gain_ref,
+    _,
     back_out,
     grad_out,
     gain_out,
@@ -1085,7 +1091,7 @@
     near = spot + 1 - 2 * core
 
     def tile_copy(c):
-        return pltpu.make_async_copy(grad_v.at[2 * c + core], grad_out.at[c], tile_sem.at[c])
+        return pltpu.make_async_copy(grad_v.at[2 * c + core], grad_out.at[c, 2], tile_sem.at[c])
 
     def pair_copy(c):
         return pltpu.make_async_remote_copy(
@@ -1165,11 +1171,15 @@
         weights_kernel,
         out_shape=(
             jax.ShapeDtypeStruct((micro, tok, 2 * heads_in), low),
-            jax.ShapeDtypeStruct((width // 2, model // width, 3 * heads_in), low),
+            jax.ShapeDtypeStruct((width // 2, 3, model // width, 3 * heads_in), low),
             jax.ShapeDtypeStruct((2, HD), jnp.float32),
             jax.ShapeDtypeStruct((tok, model), low),
         ),
-        in_specs=[pl.BlockSpec(memory_space=pltpu.SMEM)] + [anywhere] * 10 + [inside] * 3,
+        in_specs=[pl.BlockSpec(memory_space=pltpu.SMEM)]
+        + [anywhere] * 10
+        + [inside] * 3
+        + [anywhere],
+        input_output_aliases={14: 1},
         out_specs=[anywhere, anywhere, inside, anywhere],
         scratch_shapes=relay_scratch(tok // SUB, model)
         + [
@@ -1210,11 +1220,11 @@
     )(lengths, qkv, upper, kept, log_total, raw, hidden, mixed, middle_low, late, layer_input, *rest)
 
 
-def relay_scratch(count, model, extra=0):
+def relay_scratch(count, model, extra=0, rows=SUB):
     return [
-        pltpu.VMEM((count + extra, SUB, model), jnp.bfloat16),
-        pltpu.VMEM((count, SUB, model), jnp.bfloat16),
-        pltpu.VMEM((RING, SUB, model), jnp.bfloat16),
+        pltpu.VMEM((count + extra, rows, model), jnp.bfloat16),
+        pltpu.VMEM((count, rows, model), jnp.bfloat16),
+        pltpu.VMEM((RING, rows, model), jnp.bfloat16),
         pltpu.SemaphoreType.DMA((count,)),
         pltpu.SemaphoreType.DMA((count,)),
         pltpu.SemaphoreType.DMA((count,)),
@@ -1738,7 +1748,7 @@
             jax.ShapeDtypeStruct((micro, tok, model), low),
             jax.ShapeDtypeStruct((width, tok, 2 * HD), low),
             jax.ShapeDtypeStruct((1, model), jnp.float32),
-            jax.ShapeDtypeStruct((width // 2, 2, piece, hid), low),
+            jax.ShapeDtypeStruct((width // 2, 3, piece, hid), low),
             jax.ShapeDtypeStruct((micro, tok, heads_in), low),
             jax.ShapeDtypeStruct((width // 2, piece, hid), low),
             jax.ShapeDtypeStruct((2, late, SUB, model), low),
@@ -1818,7 +1828,7 @@
     other_sem,
 ):
     micro, tok, model = input_ref.shape
-    per = tok // SUB
+    per = tok // FINE
     spot = lax.axis_index("wide")
     flips = [spot + bit - 2 * bit * (spot // bit % 2) for bit in (1, 2, 4)]
     relay = Relay(micro * per, own, landed, cross, (out_sem, land_sem, back_sem, cross_sem))
@@ -1908,7 +1918,7 @@
             )
             part = part.astype(jnp.bfloat16)
             for r in range(per):
-                own[m * per + r, :, cols] = part[r * SUB : (r + 1) * SUB]
+                own[m * per + r, :, cols] = part[r * FINE : (r + 1) * FINE]
 
         @pl.when(m == 0)
         def _():
@@ -1917,11 +1927,11 @@
     term_v[0, 1:2, :] = gain_two_ref[...]
     term_v[0, 2:3, 0:HD] = gain_heads_ref[0:1, :]
     term_v[0, 2:3, HD : 2 * HD] = gain_heads_ref[1:2, :]
-    for k in range(4):
-        if k in GAIN_TICKS:
-            gain_step(GAIN_TICKS.index(k))
-        relay.send(AHEAD + k, 1)
-        relay.tick(k)
+    for k in range(2):
+        if k in GAIN_PLACES:
+            gain_step(GAIN_PLACES.index(k))
+        relay.send(AHEAD + 2 * k, 2)
+        relay.place(k)
 
     @pl.loop(0, micro)
     def _(m):
@@ -1937,27 +1947,28 @@
         def _():
             final_copy(m - 2).wait()
 
-        for r in range(per):
+        for r in range(per // 2):
             for turn in range(micro):
-                if 4 + turn * per + r in GAIN_TICKS:
+                if 2 + turn * per // 2 + r in GAIN_PLACES:
 
                     @pl.when(m == turn)
-                    def _(step=GAIN_TICKS.index(4 + turn * per + r)):
+                    def _(step=GAIN_PLACES.index(2 + turn * per // 2 + r)):
                         gain_step(step)
 
-            @pl.when(AHEAD + 4 + m * per + r < relay.count)
+            @pl.when(AHEAD + 4 + m * per + 2 * r < relay.count)
             def _():
-                relay.send(AHEAD + 4 + m * per + r, 1)
-
-            relay.tick(4 + m * per + r)
-            span = pl.ds(r * SUB, SUB)
-            rows = rows_v[m, span, :].astype(jnp.float32)
-            scale = lax.rsqrt(jnp.mean(rows * rows, axis=-1, keepdims=True) + EPSILON)
-            pulled = landed[m * per + r].astype(jnp.float32) * gain_ref[...]
-            along = jnp.mean(pulled * rows, axis=-1, keepdims=True)
-            output_v[slot, span, :] = middle_v[slot, span, :] + scale * (
-                pulled - rows * (scale * scale * along)
-            )
+                relay.send(AHEAD + 4 + m * per + 2 * r, 2)
+
+            relay.place(2 + m * per // 2 + r)
+            for half in range(2):
+                span = pl.ds((2 * r + half) * FINE, FINE)
+                rows = rows_v[m, span, :].astype(jnp.float32)
+                scale = lax.rsqrt(jnp.mean(rows * rows, axis=-1, keepdims=True) + EPSILON)
+                pulled = landed[m * per + 2 * r + half].astype(jnp.float32) * gain_ref[...]
+                along = jnp.mean(pulled * rows, axis=-1, keepdims=True)
+                output_v[slot, span, :] = middle_v[slot, span, :] + scale * (
+                    pulled - rows * (scale * scale * along)
+                )
         final_copy(m).start()
 
     final_copy(micro - 2).wait()
@@ -1968,7 +1979,7 @@
 def input_gradient(back, layer_input, grad_middle, gain_attn, weight, gain_two, gain_heads):
     micro, tok, model = layer_input.shape
     low = jnp.bfloat16
-    count = micro * (tok // SUB)
+    count = micro * (tok // FINE)
     anywhere = pl.BlockSpec(memory_space=pl.ANY)
     inside = pl.BlockSpec(memory_space=pltpu.VMEM)
     return pl.pallas_call(
@@ -1979,7 +1990,7 @@
         ),
         in_specs=[anywhere] * 3 + [inside, anywhere, inside, inside],
         out_specs=[anywhere, inside],
-        scratch_shapes=relay_scratch(count, model)
+        scratch_shapes=relay_scratch(count, model, rows=FINE)
         + [
             pltpu.VMEM(weight.shape, low),
             pltpu.VMEM((micro, tok, weight.shape[1]), low),
@@ -2037,16 +2048,16 @@
     out_ref[...] = out_rows[...].astype(jnp.float32)
 
 
-def finish(grad_input, first, last, feed, attn, columns):
+def finish(grad_input, first, last, grads, columns):
     steps = 8
     rows, model = grad_input.shape
-    piece, hid = feed.shape[0] // 2, feed.shape[1]
+    piece, hid = grads.shape[0] // 3, grads.shape[1]
     part = rows // steps
     early = first.shape[0] // part - 1
     strip = piece // steps
     blocks = hid // piece
     heads = sum(columns) // piece
-    rest = (attn.shape[1] - sum(columns)) // piece
+    rest = (hid - sum(columns)) // piece
     f32 = jnp.float32
     row = lambda i: (i, 0)
     return pl.pallas_call(
@@ -2066,8 +2077,8 @@
             pl.BlockSpec((part, model), lambda i: (jnp.maximum(i - early - 1, 0), 0)),
             pl.BlockSpec((strip, hid), row),
             pl.BlockSpec((piece, piece), lambda i: (1, jnp.minimum(i, blocks - 1))),
-            pl.BlockSpec((strip, attn.shape[1]), row),
-            pl.BlockSpec((piece, piece), lambda i: (0, heads + jnp.minimum(i, rest - 1))),
+            pl.BlockSpec((strip, hid), lambda i: (2 * steps + i, 0)),
+            pl.BlockSpec((piece, piece), lambda i: (2, heads + jnp.minimum(i, rest - 1))),
         ],
         out_specs=[
             pl.BlockSpec((part, model), row),
@@ -2078,7 +2089,7 @@
         + [pl.BlockSpec((strip, column), row) for column in columns]
         + [pl.BlockSpec((piece, piece), lambda i: (jnp.minimum(i, rest - 1), 0))],
         name="finish",
-    )(grad_input, first, last, feed, feed, attn, attn)
+    )(grad_input, first, last, grads, grads, grads, grads)
 
 
 def local_batched(
@@ -2147,7 +2158,7 @@
             rows, "wide", scatter_dimension=0, axis_index_groups=cores, tiled=True
         )
 
-    qkv_back, attn_grads, gain_heads, last_output = attention_gradients(
+    qkv_back, other_grads, gain_heads, last_output = attention_gradients(
         lengths,
         packed,
         grad_mixed,
@@ -2162,11 +2173,10 @@
         cosine,
         sine,
         head_gains,
+        feed_grads,
     )
     gate_grads = scatter(gate_grads.reshape(-1, w_gate.shape[1]))
-    attn_grads, feed_grads = lax.optimization_barrier((attn_grads, feed_grads))
-    attn_grads = scatter(attn_grads.reshape(model // 2, -1))
-    feed_grads = scatter(feed_grads.reshape(-1, w_up.shape[1]))
+    other_grads = scatter(other_grads.reshape(-1, w_up.shape[1]))
     grad_input, gains = input_gradient(
         qkv_back, layer_input, grad_middle, gain_attn, w_qkv, gain_two, gain_heads
     )
@@ -2189,8 +2199,7 @@
         grad_input.reshape(-1, model),
         output.reshape(-1, model),
         last_output,
-        feed_grads,
-        attn_grads,
+        other_grads,
         (w_query.shape[1], w_key.shape[1], w_value.shape[1]),
     )
     return (

time: 618 us -> 612 us (level)
  transfers between devices with their start and end apart: 4 -> 3, of which waited for: 1 -> 0; matrix products, arithmetic and copies ran while one was open for 0% -> 0% of each run, Pallas kernels for 46% -> 45%
where the time goes in v6:
time: 612 us; the launch traced here: 611 us
  Pallas kernels  585 us (96%)
  between operations  14 us (2%)
  local copies, waits for them, and re-layouts  11.1 us (2%)
    pallas_call x1, Pallas kernels, feed_forward(): pl.pallas_call(feed_kernel, out_shape=(jax.ShapeDtypeStruct((micro, tok,...  294 us
    pallas_call x1, Pallas kernels, input_gradient(): pl.pallas_call(input_kernel, out_shape=(jax.ShapeDtypeStruct((micro, tok,...  116 us
    pallas_call x1, Pallas kernels, project(): pl.pallas_call(project_kernel, out_shape=(jax.ShapeDtypeStruct((micro, to...  75.4 us
    pallas_call x1, Pallas kernels, attention_gradients(): pl.pallas_call(weights_kernel, out_shape=(jax.ShapeDtypeStruct((micro, to...  68.6 us
    pallas_call x1, Pallas kernels, attention_out(): pl.pallas_call(attend_forward, out_shape=(jax.ShapeDtypeStruct((total, 2...  16 us
    pallas_call x1, Pallas kernels, finish(): pl.pallas_call(finish_kernel, grid=(steps,), out_shape=(jax.ShapeDtypeStr...  13.1 us
  transfers between devices with their start and end apart: 3, of which 0 were waited for; matrix products, arithmetic and copies ran while one was open for 0% of the time, Pallas kernels for 45%

profile of v6, /device:TPU:0, one launch (start us, length us, event | category | flops | bytes accessed | tf_op | source)
XLA Modules:
  0.0 611.2 jit_solution(17407255712742224590)
XLA Ops:
  7.2 0.0 copy-start.15
  7.2 0.0 copy-start.16
  7.2 0.0 copy-start.17
  7.2 0.0 copy-start.9
  7.2 0.0 copy-start.6
  7.3 0.0 all-gather.3.cloned.1.call-start
  7.3 1.6 copy.30
  8.9 0.3 copy.31
  9.2 1.0 pad_maximum_fusion
  10.2 0.0 all-gather.3.cloned.1.call-update
  10.2 0.0 reduce-scatter.5.cloned.1.call-start
  10.3 0.0 copy-start.10
  10.4 75.4 %project.1 = (bf16[4,256,2048]{2,1,0:T(8,128)(2,1)S(1)}, f32[4,256,768]{2,1,0:T(8,128)S(1)}, bf16[8,256,512]{2,1,0:T(8,128)(2,1)S(1)}, bf16[2048,1024]{1,0:T(8,1...) custom-call(bf16[4,256,2048]{2,1,0:T(8,128)(2,1)} %input_ref.7, f32[1,2048]{1,0:T(1,128)S(1)} %bitcast.25, ...), custom_call_target="tpu_custom_call" | custom-call | flops 20000000000 | bytes 40000000 | tf_op jit(solution)/shard_map/project/pallas_call | solution.py:830
  85.8 1.3 copy-done
  87.1 2.0 copy-done.1
  89.1 1.7 copy-done.2
  90.8 0.8 copy-done.4
  91.6 0.8 copy-done.5
  92.4 16.0 %attend_forward.1 = (bf16[2048,256]{1,0:T(8,128)(2,1)}, f32[2048,256]{1,0:T(8,128)}, f32[8,8,512]{2,1,0:T(8,128)}) custom-call(s32[4,8]{1,0:T(4,128)} %lengths_ref.5, bf16[2048,512]{1,0:T(8,128)(2,1)} %bitcast.23), custom_call_target="tpu_custom_call" | custom-call | tf_op jit(solution)/shard_map/attend_forward/pallas_call | solution.py:371
  108.4 293.8 %feed_forward.1 = (bf16[4,256,2048]{2,1,0:T(8,128)(2,1)}, bf16[4,256,1536]{2,1,0:T(8,128)(2,1)}, bf16[4,256,1536]{2,1,0:T(8,128)(2,1)}, bf16[4,256,1536]{2,1,0:T...) custom-call(bf16[8,256,256]{2,1,0:T(8,128)(2,1)} %bitcast.40, ...), custom_call_target="tpu_custom_call" | custom-call | flops 240000008192 | bytes 900000000 | tf_op jit(solution)/shard_map/feed_forward/pallas_call | solution.py:1739
  402.2 0.0 reduce-scatter.5.cloned.1.call-update
  402.2 0.0 reduce-scatter.3.cloned.1.call-start
  402.2 68.6 %attention_gradients.1 = (bf16[4,256,1024]{2,1,0:T(8,128)(2,1)}, bf16[4,3,256,1536]{3,2,1,0:T(8,128)(2,1)}, f32[2,128]{1,0:T(2,128)}, bf16[256,2048]{1,0:T(8,128)(2,1)}) custom-call(s32[4,8]{1,0:T(4,128)} %lengths_ref.5, bf16[2048,512]{1,0:T(8,128)(2,1)} %bitcast.24, ...), custom_call_target="tpu_custom_call", output_to_operand_aliasing={{1}: (14, {})} | custom-call | flops 1000000000 | bytes 1000000 | tf_op jit(solution)/shard_map/attention_gradients/pallas_call | solution.py:1170
  470.8 0.0 copy-start.7
  470.8 0.0 copy-start.8
  470.8 0.0 reduce-scatter.3.cloned.1.call-update
  470.9 1.6 copy-done.3
  472.4 115.6 %input_gradient.1 = (f32[4,256,2048]{2,1,0:T(8,128)}, f32[8,2048]{1,0:T(8,128)S(1)}) custom-call(bf16[4,256,1024]{2,1,0:T(8,128)(2,1)S(1)} %copy-done.3, bf16[4,256,2048]{2,1,0:T(8,128)(2,1)} %input_ref.7, f32[4,256,2048]{2,1,0:T(8,128)} %get-tuple-element.59.middle_ref, f32[1,2048]{1,0:T(1,128)S(1)} %bitcast.26, ...), custom_call_target="tpu_custom_call" | custom-call | flops 1000000000 | bytes 1000000 | tf_op jit(solution)/shard_map/input_gradient/pallas_call | solution.py:1985
  588.0 0.5 slice_bitcast_fusion
  588.6 0.6 fusion
  589.2 2.4 widen_gate.1
  591.6 13.1 %finish.1 = (f32[1024,2048]{1,0:T(8,128)}, bf16[1024,2048]{1,0:T(8,128)(2,1)}, f32[256,1536]{1,0:T(8,128)}, f32[1536,256]{1,0:T(8,128)}, f32[256,512]{1,0:T(8,12...) custom-call(f32[1024,2048]{1,0:T(8,128)} %bitcast.28, bf16[768,2048]{1,0:T(8,128)(2,1)} %bitcast.32, ...), custom_call_target="tpu_custom_call" | custom-call | tf_op jit(solution)/shard_map/finish/pallas_call | solution.py:2063
  (26 shorter events, 0.1 us)
Async XLA Ops:
  7.2 2.0 copy-start.15
  7.2 3.1 copy-start.16
  7.2 3.1 copy-start.17
  7.2 3.1 copy-start.9
  7.2 3.1 copy-start.6
  7.2 3.1 copy-start.14
  7.2 3.1 copy-start.13
  7.3 3.1 copy-start.12
  7.3 101.1 %all-gather.3.cloned.1.call-start = ((), (), s32[]{:S(2)}) async-start(), calls=%async_computation.4 | async-start | bytes 9437184 | tf_op jit(solution)/shard_map/all_gather | solution.py:2120
  10.2 578.9 %reduce-scatter.5.cloned.1.call-start = ((), (), s32[]{:S(2)}) async-start(), calls=%async_computation.3 | async-start | bytes 3932160 | tf_op jit(solution)/shard_map/reduce_scatter | solution.py:2157
  10.3 75.5 %copy-start.10 = (f32[2,128]{1,0:T(2,128)}, f32[2,128]{1,0:T(2,128)S(1)}, u32[]{:S(2)}) copy-start(f32[2,128]{1,0:T(2,128)S(1)} %pad_maximum_fusion.1.head_gain_ref) | copy-start | bytes 3076
  85.8 1.3 copy-start
  87.1 2.0 copy-start.1
  89.1 1.7 copy-start.2
  90.8 0.8 copy-start.4
  91.6 0.8 copy-start.5
  402.2 189.4 %reduce-scatter.3.cloned.1.call-start = ((), (), s32[]{:S(2)}) async-start(), calls=%async_computation.2 | async-start | bytes 11796480 | tf_op jit(solution)/shard_map/reduce_scatter | solution.py:2157
  470.8 1.6 copy-start.3
  470.8 1.6 copy-start.7
  470.8 1.6 copy-start.8
  470.8 1.6 copy-start.11
Sparse Core Ops, SparseCore 0:
  10.6 84.8 all-gather.2
  402.3 75.7 reduce-scatter.4
  481.3 96.3 reduce-scatter.2

commit v7 on v6

--- a/solution.py
+++ b/solution.py
@@ -1091,7 +1091,7 @@
     near = spot + 1 - 2 * core
 
     def tile_copy(c):
-        return pltpu.make_async_copy(grad_v.at[2 * c + core], grad_out.at[c, 2], tile_sem.at[c])
+        return pltpu.make_async_copy(grad_v.at[2 * c + core], grad_out.at[c, 3], tile_sem.at[c])
 
     def pair_copy(c):
         return pltpu.make_async_remote_copy(
@@ -1171,7 +1171,7 @@
         weights_kernel,
         out_shape=(
             jax.ShapeDtypeStruct((micro, tok, 2 * heads_in), low),
-            jax.ShapeDtypeStruct((width // 2, 3, model // width, 3 * heads_in), low),
+            jax.ShapeDtypeStruct((width // 2, 4, model // width, 3 * heads_in), low),
             jax.ShapeDtypeStruct((2, HD), jnp.float32),
             jax.ShapeDtypeStruct((tok, model), low),
         ),
@@ -1251,7 +1251,6 @@
     gain_out,
     weight_out,
     heads_out,
-    early_out,
     late_out,
     own,
     landed,
@@ -1567,8 +1566,7 @@
         return up_v.at[pl.ds(count + q * piece, piece)]
 
     def tile_copy(m, q):
-        target = early_out.at[m] if q == 0 else weight_out.at[m, q - 1]
-        return pltpu.make_async_copy(pair_slot(q), target, tile_sem.at[q])
+        return pltpu.make_async_copy(pair_slot(q), weight_out.at[m, q], tile_sem.at[q])
 
     def pair_copy(q):
         return pltpu.make_async_remote_copy(
@@ -1748,13 +1746,12 @@
             jax.ShapeDtypeStruct((micro, tok, model), low),
             jax.ShapeDtypeStruct((width, tok, 2 * HD), low),
             jax.ShapeDtypeStruct((1, model), jnp.float32),
-            jax.ShapeDtypeStruct((width // 2, 3, piece, hid), low),
+            jax.ShapeDtypeStruct((width // 2, 4, piece, hid), low),
             jax.ShapeDtypeStruct((micro, tok, heads_in), low),
-            jax.ShapeDtypeStruct((width // 2, piece, hid), low),
             jax.ShapeDtypeStruct((2, late, SUB, model), low),
         ),
         in_specs=[anywhere] * 3 + [inside, anywhere, anywhere, anywhere],
-        out_specs=[anywhere] * 8 + [inside] + [anywhere] * 4,
+        out_specs=[anywhere] * 8 + [inside] + [anywhere] * 3,
         scratch_shapes=relay_scratch(count - late, model, late)
         + [
             pltpu.VMEM((heads_in, model), low),
@@ -2015,20 +2012,18 @@
     )(back, layer_input, grad_middle, gain_attn[None, :], weight, gain_two, gain_heads)
 
 
-def widen_gate(rows_ref, gate_ref):
-    gate_ref[...] = rows_ref[...].astype(jnp.float32)
-
-
 def finish_kernel(
     input_rows,
     first_rows,
     last_rows,
+    gate_rows,
     up_rows,
     down_rows,
     attn_rows,
     out_rows,
     grad_ref,
     output_ref,
+    gate_ref,
     up_ref,
     down_ref,
     query_ref,
@@ -2039,6 +2034,7 @@
     grad_ref[...] = input_rows[...]
     inside = pl.program_id(0) < pl.num_programs(0) * 3 // 4
     output_ref[...] = jnp.where(inside, first_rows[...], last_rows[...])
+    gate_ref[...] = gate_rows[...].astype(jnp.float32)
     up_ref[...] = up_rows[...].astype(jnp.float32)
     down_ref[...] = down_rows[...].astype(jnp.float32)
     first = 0
@@ -2051,7 +2047,7 @@
 def finish(grad_input, first, last, grads, columns):
     steps = 8
     rows, model = grad_input.shape
-    piece, hid = grads.shape[0] // 3, grads.shape[1]
+    piece, hid = grads.shape[0] // 4, grads.shape[1]
     part = rows // steps
     early = first.shape[0] // part - 1
     strip = piece // steps
@@ -2067,6 +2063,7 @@
             jax.ShapeDtypeStruct((rows, model), f32),
             jax.ShapeDtypeStruct((rows, model), jnp.bfloat16),
             jax.ShapeDtypeStruct((piece, hid), f32),
+            jax.ShapeDtypeStruct((piece, hid), f32),
             jax.ShapeDtypeStruct((hid, piece), f32),
         )
         + tuple(jax.ShapeDtypeStruct((piece, column), f32) for column in columns)
@@ -2076,20 +2073,22 @@
             pl.BlockSpec((part, model), lambda i: (jnp.minimum(i, early), 0)),
             pl.BlockSpec((part, model), lambda i: (jnp.maximum(i - early - 1, 0), 0)),
             pl.BlockSpec((strip, hid), row),
-            pl.BlockSpec((piece, piece), lambda i: (1, jnp.minimum(i, blocks - 1))),
-            pl.BlockSpec((strip, hid), lambda i: (2 * steps + i, 0)),
-            pl.BlockSpec((piece, piece), lambda i: (2, heads + jnp.minimum(i, rest - 1))),
+            pl.BlockSpec((strip, hid), lambda i: (steps + i, 0)),
+            pl.BlockSpec((piece, piece), lambda i: (2, jnp.minimum(i, blocks - 1))),
+            pl.BlockSpec((strip, hid), lambda i: (3 * steps + i, 0)),
+            pl.BlockSpec((piece, piece), lambda i: (3, heads + jnp.minimum(i, rest - 1))),
         ],
         out_specs=[
             pl.BlockSpec((part, model), row),
             pl.BlockSpec((part, model), row),
+            pl.BlockSpec((strip, hid), row),
             pl.BlockSpec((strip, hid), row),
             pl.BlockSpec((piece, piece), lambda i: (jnp.minimum(i, blocks - 1), 0)),
         ]
         + [pl.BlockSpec((strip, column), row) for column in columns]
         + [pl.BlockSpec((piece, piece), lambda i: (jnp.minimum(i, rest - 1), 0))],
         name="finish",
-    )(grad_input, first, last, grads, grads, grads, grads)
+    )(grad_input, first, last, grads, grads, grads, grads, grads)
 
 
 def local_batched(
@@ -2139,7 +2138,6 @@
         gain_two,
         feed_grads,
         mixed_low,
-        gate_grads,
         late,
     ) = feed_forward(
         mixed.reshape(width, tok_rows, 2 * HD),
@@ -2175,20 +2173,15 @@
         head_gains,
         feed_grads,
     )
-    gate_grads = scatter(gate_grads.reshape(-1, w_gate.shape[1]))
     other_grads = scatter(other_grads.reshape(-1, w_up.shape[1]))
     grad_input, gains = input_gradient(
         qkv_back, layer_input, grad_middle, gain_attn, w_qkv, gain_two, gain_heads
     )
 
-    grad_gate = pl.pallas_call(
-        widen_gate,
-        out_shape=jax.ShapeDtypeStruct(w_gate.shape, jnp.float32),
-        name="widen_gate",
-    )(gate_grads)
     (
         grad_input,
         output,
+        grad_gate,
         grad_up,
         grad_down,
         grad_query,

time: 612 us -> 611 us (level)
  Pallas kernels: 585 us -> 576 us
  waiting for transfers between devices: 0.05 us -> 7.17 us
    reduce_scatter x2 -> x1, waiting for transfers between devices: 0.01 us -> 7.14 us  [scatter(): lax.psum_scatter(rows, 'wide', scatter_dimension=0, axis_index_groups=cor...]
    pallas_call x1, Pallas kernels: 68.6 us -> 61.9 us  [attention_gradients(): pl.pallas_call(weights_kernel, out_shape=(jax.ShapeDtypeStruct((micro, to...]
  transfers between devices with their start and end apart: 3 -> 2, of which waited for: 0 -> 1; matrix products, arithmetic and copies ran while one was open for 0% -> 0% of each run, Pallas kernels for 45% -> 33%
where the time goes in v7:
time: 611 us; the launch traced here: 610 us
  Pallas kernels  576 us (94%)
  between operations  14.3 us (2%)
  local copies, waits for them, and re-layouts  11.1 us (2%)
  waiting for transfers between devices  7.17 us (1%)
    pallas_call x1, Pallas kernels, feed_forward(): pl.pallas_call(feed_kernel, out_shape=(jax.ShapeDtypeStruct((micro, tok,...  297 us
    pallas_call x1, Pallas kernels, input_gradient(): pl.pallas_call(input_kernel, out_shape=(jax.ShapeDtypeStruct((micro, tok,...  117 us
    pallas_call x1, Pallas kernels, project(): pl.pallas_call(project_kernel, out_shape=(jax.ShapeDtypeStruct((micro, to...  75.4 us
    pallas_call x1, Pallas kernels, attention_gradients(): pl.pallas_call(weights_kernel, out_shape=(jax.ShapeDtypeStruct((micro, to...  61.9 us
    pallas_call x1, Pallas kernels, finish(): pl.pallas_call(finish_kernel, grid=(steps,), out_shape=(jax.ShapeDtypeStr...  13.7 us
  transfers between devices with their start and end apart: 2, of which 1 were waited for; matrix products, arithmetic and copies ran while one was open for 0% of the time, Pallas kernels for 33%

profile of v7, /device:TPU:0, one launch (start us, length us, event | category | flops | bytes accessed | tf_op | source)
XLA Modules:
  0.0 610.1 jit_solution(218692187319638761)
XLA Ops:
  7.2 0.0 copy-start.15
  7.2 0.0 copy-start.16
  7.2 0.0 copy-start.17
  7.2 0.0 copy-start.9
  7.2 0.0 copy-start.6
  7.3 0.0 all-gather.3.cloned.1.call-start
  7.3 1.6 copy.30
  8.9 0.3 copy.31
  9.2 1.0 pad_maximum_fusion
  10.2 0.0 all-gather.3.cloned.1.call-update
  10.2 0.0 reduce-scatter.2.cloned.1.call-start
  10.3 0.0 copy-start.10
  10.3 0.0 copy-done.9
  10.3 0.0 copy-done.6
  10.4 0.0 copy-done.14
  10.4 75.4 %project.1 = (bf16[4,256,2048]{2,1,0:T(8,128)(2,1)S(1)}, f32[4,256,768]{2,1,0:T(8,128)S(1)}, bf16[8,256,512]{2,1,0:T(8,128)(2,1)S(1)}, bf16[2048,1024]{1,0:T(8,1...) custom-call(bf16[4,256,2048]{2,1,0:T(8,128)(2,1)} %input_ref.7, f32[1,2048]{1,0:T(1,128)S(1)} %bitcast.24, ...), custom_call_target="tpu_custom_call" | custom-call | flops 20000000000 | bytes 40000000 | tf_op jit(solution)/shard_map/project/pallas_call | solution.py:830
  85.8 1.3 copy-done
  87.1 2.0 copy-done.1
  89.1 1.7 copy-done.2
  90.8 0.8 copy-done.4
  91.6 0.8 copy-done.5
  92.4 11.3 %attend_forward.1 = (bf16[2048,256]{1,0:T(8,128)(2,1)}, f32[2048,256]{1,0:T(8,128)}, f32[8,8,512]{2,1,0:T(8,128)}) custom-call(s32[4,8]{1,0:T(4,128)} %lengths_ref.5, bf16[2048,512]{1,0:T(8,128)(2,1)} %bitcast.22), custom_call_target="tpu_custom_call" | custom-call | tf_op jit(solution)/shard_map/attend_forward/pallas_call | solution.py:371
  103.6 297.0 %feed_forward.1 = (bf16[4,256,2048]{2,1,0:T(8,128)(2,1)}, bf16[4,256,1536]{2,1,0:T(8,128)(2,1)}, bf16[4,256,1536]{2,1,0:T(8,128)(2,1)}, bf16[4,256,1536]{2,1,0:T...) custom-call(bf16[8,256,256]{2,1,0:T(8,128)(2,1)} %bitcast.38, ...), custom_call_target="tpu_custom_call" | custom-call | flops 240000008192 | bytes 900000000 | tf_op jit(solution)/shard_map/feed_forward/pallas_call | solution.py:1737
  400.6 61.9 %attention_gradients.1 = (bf16[4,256,1024]{2,1,0:T(8,128)(2,1)}, bf16[4,4,256,1536]{3,2,1,0:T(8,128)(2,1)}, f32[2,128]{1,0:T(2,128)}, bf16[256,2048]{1,0:T(8,128)(2,1)}) custom-call(s32[4,8]{1,0:T(4,128)} %lengths_ref.5, bf16[2048,512]{1,0:T(8,128)(2,1)} %bitcast.23, ...), custom_call_target="tpu_custom_call", output_to_operand_aliasing={{1}: (14, {})} | custom-call | flops 1000000000 | bytes 1000000 | tf_op jit(solution)/shard_map/attention_gradients/pallas_call | solution.py:1170
  462.5 0.0 copy-start.7
  462.6 0.0 reduce-scatter.2.cloned.1.call-update
  462.6 1.5 copy-done.3
  464.1 117.2 %input_gradient.1 = (f32[4,256,2048]{2,1,0:T(8,128)}, f32[8,2048]{1,0:T(8,128)S(1)}) custom-call(bf16[4,256,1024]{2,1,0:T(8,128)(2,1)S(1)} %copy-done.3, bf16[4,256,2048]{2,1,0:T(8,128)(2,1)} %input_ref.7, f32[4,256,2048]{2,1,0:T(8,128)} %get-tuple-element.59.middle_ref, f32[1,2048]{1,0:T(1,128)S(1)} %bitcast.25, ...), custom_call_target="tpu_custom_call" | custom-call | flops 1000000000 | bytes 1000000 | tf_op jit(solution)/shard_map/input_gradient/pallas_call | solution.py:1982
  581.3 0.5 slice_bitcast_fusion
  581.8 0.6 fusion
  582.4 7.1 %reduce-scatter.2.cloned.1.call-done.gate_rows.up_rows.down_rows.attn_rows.out_rows = bf16[1024,1536]{1,0:T(8,128)(2,1)} async-done(((bf16[4096,1536]{1,0:T(8,128)(2,1)}), bf16[1024,1536]{1,0:T(8,128)(2,1)}) %reduce-scatter.2.cloned.1.call-update) | async-done | bytes 3145744 | tf_op jit(solution)/shard_map/reduce_scatter | solution.py:2155
  589.6 13.7 %finish.1 = (f32[1024,2048]{1,0:T(8,128)}, bf16[1024,2048]{1,0:T(8,128)(2,1)}, f32[256,1536]{1,0:T(8,128)}, f32[256,1536]{1,0:T(8,128)}, f32[1536,256]{1,0:T(8,1...) custom-call(f32[1024,2048]{1,0:T(8,128)} %bitcast.27, ...), custom_call_target="tpu_custom_call" | custom-call | tf_op jit(solution)/shard_map/finish/pallas_call | solution.py:2059
  (22 shorter events, 0.1 us)
Async XLA Ops:
  7.2 2.0 copy-start.15
  7.2 3.1 copy-start.16
  7.2 3.1 copy-start.17
  7.2 3.1 copy-start.9
  7.2 3.1 copy-start.6
  7.2 3.1 copy-start.14
  7.2 3.1 copy-start.13
  7.3 3.1 copy-start.12
  7.3 96.4 %all-gather.3.cloned.1.call-start = ((), (), s32[]{:S(2)}) async-start(), calls=%async_computation.2 | async-start | bytes 9437184 | tf_op jit(solution)/shard_map/all_gather | solution.py:2119
  10.2 579.3 %reduce-scatter.2.cloned.1.call-start = ((), (), s32[]{:S(2)}) async-start(), calls=%async_computation.1 | async-start | bytes 15728640 | tf_op jit(solution)/shard_map/reduce_scatter | solution.py:2155
  10.3 75.5 %copy-start.10 = (f32[2,128]{1,0:T(2,128)}, f32[2,128]{1,0:T(2,128)S(1)}, u32[]{:S(2)}) copy-start(f32[2,128]{1,0:T(2,128)S(1)} %pad_maximum_fusion.1.head_gain_ref) | copy-start | bytes 3076
  85.8 1.3 copy-start
  87.1 2.0 copy-start.1
  89.1 1.7 copy-start.2
  90.8 0.8 copy-start.4
  91.6 0.8 copy-start.5
  462.5 1.6 copy-start.3
  462.5 1.6 copy-start.7
  462.5 1.6 copy-start.8
  462.5 1.6 copy-start.11
Sparse Core Ops, SparseCore 0:
  10.6 84.8 all-gather.2
  462.7 126.8 reduce-scatter.1
